TPU v7x, 256 devices: a whole 4x4x8 slice. The times are simulated.
256 devices in a mesh: space: 32 (over y, x, z_hi), coil: 8 (over z_lo, core).
Axes of the slice: x: 4, y: 4, z: 8 (z_hi: 2, z_lo: 4; z = z_hi * 4 + z_lo), core: 2. Of those that a mesh axis runs over, the one named last changes fastest.
Arguments:
- state: bfloat16 [32, 2, 1024, 768], P(None, None, 'space', 'coil'), may hold values from -6 to 6
- sens: float32 [2, 16, 2, 1024, 768], P(None, 'coil', None, 'space'), may hold values from -2 to 2
- kdata: float32 [2, 16, 2, 768, 1024], P(None, 'coil', None, 'space'), may hold values from -3 to 3
- mask: int32 [768, 1024], P('space'), may hold values 0 or 1
- inject: float32 [32, 2], replicated, may hold values from -4 to 4
- kernels: bfloat16 [4, 27, 16, 16], replicated, may hold values from -0.3125 to 0.3125
- biases: float32 [4, 16], replicated, may hold values from -3 to 3
- mixers: bfloat16 [4, 16, 16], replicated, may hold values from -1.5 to 1.5
Outputs:
- new_state: bfloat16 [32, 2, 1024, 768], P(None, None, 'space', 'coil')
- gradient: float32 [2, 2, 1024, 768], P(None, None, 'space', 'coil')
All inputs are finite; a program needn't handle non-finite values. No bound on the sum of `mask` on one device may be relied on, other than what follows from the above.
Results may differ from a plain program's by a relative error of at most 0.015.
Values may be sent and summed in bfloat16 or wider, within the bound.
No kernel may reach another device: no remote copies, remote signals or barrier semaphores. Data moves between devices by JAX's collectives and lax.ppermute only.
A program may use at most 64 MiB of HBM per device.

v0:
```python
import numpy as np

import jax
import jax.numpy as jnp
from jax import lax
from jax.experimental import pallas as pl
from jax.experimental.pallas import tpu as pltpu
from jax.sharding import PartitionSpec as P

F32 = jnp.float32
BF16 = jnp.bfloat16
REACH = 4
VMEM = pl.BlockSpec(memory_space=pltpu.VMEM)
SMEM = pl.BlockSpec(memory_space=pltpu.SMEM)


def call(body, outs, scratch, name, in_specs):
    single = not isinstance(outs, (list, tuple))
    return pl.pallas_call(
        body,
        out_shape=outs,
        in_specs=in_specs,
        out_specs=VMEM if single else [VMEM] * len(outs),
        scratch_shapes=scratch,
        name=name,
    )


def dft_factors(length, columns, step):
    columns = np.asarray(columns)[None, :]
    coarse = (step * np.arange(length // step))[:, None] * columns % length
    fine = np.arange(step)[:, None] * columns % length
    angle_coarse = coarse * (2.0 * np.pi / length)
    angle_fine = fine * (2.0 * np.pi / length)
    scale = 1.0 / np.sqrt(length)
    return [
        np.asarray(part, np.float32)
        for part in (
            np.cos(angle_coarse) * scale,
            np.sin(angle_coarse) * scale,
            np.cos(angle_fine),
            np.sin(angle_fine),
        )
    ]


def dft_tables(length, columns, step):
    cos_a, sin_a, cos_b, sin_b = [jnp.asarray(part) for part in dft_factors(length, columns, step)]
    cos_a, sin_a = cos_a[:, None, :], sin_a[:, None, :]
    cos_b, sin_b = cos_b[None], sin_b[None]
    cos = (cos_a * cos_b - sin_a * sin_b).astype(BF16)
    sin = (sin_a * cos_b + cos_a * sin_b).astype(BF16)
    return cos.reshape(length, -1), sin.reshape(length, -1)


def swap_groups(tiles, group):
    tiles = list(tiles)
    count = len(tiles)
    lane = lax.broadcasted_iota(jnp.int32, tiles[0].shape, 1)
    bit = count // 2
    while bit:
        shift = bit * group
        high = (lane // shift) % 2 == 1
        for low in range(count):
            if low & bit:
                continue
            a, b = tiles[low], tiles[low | bit]
            tiles[low] = jnp.where(high, pltpu.roll(b, shift, 1), a)
            tiles[low | bit] = jnp.where(high, b, pltpu.roll(a, 128 - shift, 1))
        bit //= 2
    return tiles


def nn(a, b):
    return lax.dot_general(a, b, (((1,), (0,)), ((), ())), preferred_element_type=F32)


def nt(a, b):
    return lax.dot_general(a, b, (((1,), (1,)), ((), ())), preferred_element_type=F32)


def forward_columns(est_ref, sens_ref, cos_ref, sin_ref, out_ref, img_ref):
    owners = est_ref.shape[0]
    rows = sens_ref.shape[3]
    npar = sens_ref.shape[4]
    width = npar // owners
    lane = lax.broadcasted_iota(jnp.int32, (rows, 128), 1)
    coils, spots = sens_ref.shape[1:3]
    for spot in range(spots):
        for tile in range(npar // 128):
            full = []
            for part in range(2):
                value = None
                for owner in range(128 * tile // width, (128 * tile + 127) // width + 1):
                    at = width * owner - 128 * tile
                    piece = est_ref[owner, part, spot].astype(F32)
                    if at % 128:
                        piece = pltpu.roll(piece, at % 128, 1)
                    value = piece if value is None else jnp.where(lane >= at, piece, value)
                full.append(value)
            est_re, est_im = full
            cols = pl.ds(128 * tile, 128)
            for coil in range(coils):
                sens_re = sens_ref[0, coil, spot, :, cols]
                sens_im = sens_ref[1, coil, spot, :, cols]
                row = (coil * spots + spot) * rows
                img_ref[pl.ds(row, rows), cols] = (sens_re * est_re - sens_im * est_im).astype(BF16)
                img_ref[pl.ds(128 + row, rows), cols] = (sens_re * est_im + sens_im * est_re).astype(BF16)
    img = img_ref[...]
    step = 256
    for start in range(0, npar, step):
        here = pl.ds(start, step)
        by_cos = nt(cos_ref[here, :], img)
        by_sin = nt(sin_ref[here, :], img)
        out_ref[here, 0:128] = (by_cos[:, :128] + by_sin[:, 128:]).astype(BF16)
        out_ref[here, 128:256] = (by_cos[:, 128:] - by_sin[:, :128]).astype(BF16)


def consistency(recv_ref, kdata_ref, mask_ref, cos_ref, sin_ref, out_ref, x_ref, res_ref):
    lines = mask_ref.shape[0]
    npe = mask_ref.shape[1]
    sources = recv_ref.shape[0] // lines
    half = 4 * lines
    for quad in range(sources // 4):
        stacked = []
        for part in range(2):
            tiles = [
                recv_ref[pl.ds((4 * quad + s) * lines, lines), pl.ds(128 * part, 128)].astype(F32) for s in range(4)
            ]
            stacked += swap_groups(tiles, 32)
        x_ref[:, pl.ds(128 * quad, 128)] = jnp.concatenate(stacked, axis=0).astype(BF16)
    x = x_ref[...]
    step = 256
    for start in range(0, npe, step):
        here = pl.ds(start, step)
        by_cos = nn(x, cos_ref[:, here])
        by_sin = nn(x, sin_ref[:, here])
        sampled = mask_ref[:, here].astype(F32)
        sampled = jnp.concatenate([sampled] * 4, axis=0)
        data = [
            jnp.concatenate([kdata_ref[part, c, p, :, here] for c in range(2) for p in range(2)], axis=0)
            for part in range(2)
        ]
        real = sampled * (by_cos[:half] + by_sin[half:] - data[0])
        imag = sampled * (by_cos[half:] - by_sin[:half] - data[1])
        res_ref[0:half, here] = real.astype(BF16)
        res_ref[half : 2 * half, here] = imag.astype(BF16)
    res = res_ref[...]
    for start in range(0, cos_ref.shape[1], step):
        here = pl.ds(start, step)
        by_cos = nn(res, cos_ref[:, here])
        by_sin = nn(res, sin_ref[:, here])
        parts = (by_cos[:half] - by_sin[half:], by_cos[half:] + by_sin[:half])
        for tile in range(step // 128):
            at = slice(128 * tile, 128 * tile + 128)
            tiles = [part[lines * g : lines * (g + 1), at] for part in parts for g in range(4)]
            if start < npe:
                quad = start // 128 + tile
                for part in range(2):
                    for s, value in enumerate(swap_groups(tiles[4 * part : 4 * part + 4], 32)):
                        out_ref[pl.ds((4 * quad + s) * lines, lines), pl.ds(128 * part, 128)] = value.astype(BF16)
            else:
                group = (start - npe) // 128 + tile
                for s, value in enumerate(swap_groups(tiles, 8)):
                    value = value.astype(BF16)
                    for half_id in range(2):
                        owner = 16 * group + 8 * half_id + s
                        out_ref[pl.ds(owner * lines, lines), 256:384] = value


def backward_columns(recv_ref, sens_ref, edge_ref, place_ref, cos_ref, sin_ref, out_ref, part_ref):
    npar = sens_ref.shape[4]
    coils, spots, rows = sens_ref.shape[1:4]
    cells = coils * spots * rows
    edges = coils * spots * 2 * REACH
    turned = recv_ref[...].astype(F32).T
    low = place_ref[0] // 8 % 2 == 0
    border = jnp.where(low, turned[2 * cells : 2 * cells + 2 * edges], turned[2 * cells + 2 * edges :])
    x = jnp.concatenate([turned[: 2 * cells], border], axis=0).astype(BF16)
    step = 256
    for start in range(0, npar, step):
        here = pl.ds(start, step)
        by_cos = nn(x, cos_ref[:, here])
        by_sin = nn(x, sin_ref[:, here])
        for first, count, profile_ref, offset in ((0, cells, sens_ref, 0), (2 * cells, edges, edge_ref, rows)):
            second = first + count
            last = second + count
            real = by_cos[first:second] - by_sin[second:last]
            imag = by_cos[second:last] + by_sin[first:second]
            per_coil = count // coils
            height = per_coil // spots
            sums = [0.0, 0.0]
            for coil in range(coils):
                profile = [
                    jnp.concatenate([profile_ref[part, coil, spot, :, here] for spot in range(spots)], axis=0).astype(F32)
                    for part in range(2)
                ]
                re = real[coil * per_coil : (coil + 1) * per_coil]
                im = imag[coil * per_coil : (coil + 1) * per_coil]
                sums[0] = sums[0] + (profile[0] * re + profile[1] * im)
                sums[1] = sums[1] + (profile[0] * im - profile[1] * re)
            for part in range(2):
                for spot in range(spots):
                    row = (part * spots + spot) * (rows + 2 * REACH) + offset
                    part_ref[pl.ds(row, height), here] = sums[part][spot * height : (spot + 1) * height]
    total = part_ref.shape[0]
    owners = out_ref.shape[0] // total
    width = npar // owners
    lane = lax.broadcasted_iota(jnp.int32, (total, 128), 1)
    count = npar // 128
    for owner in range(owners):
        tile, off = divmod(width * owner, 128)
        value = part_ref[:, pl.ds(128 * tile, 128)]
        if off:
            value = pltpu.roll(value, 128 - off, 1)
            if tile + 1 < count:
                following = pltpu.roll(part_ref[:, pl.ds(128 * (tile + 1), 128)], 128 - off, 1)
                value = jnp.where((lane >= 128 - off) & (lane < 112), following, value)
        elif tile:
            value = jnp.where(lane >= 112, part_ref[:, pl.ds(128 * (tile - 1), 128)], value)
        out_ref[pl.ds(owner * total, total), :] = value.astype(BF16)


def couple(
    recv_ref, state_ref, place_ref, inject_ref, weight_ref, bias_ref, mixer_ref, new_ref, grad_ref, wide_ref, a_ref, b_ref
):
    channels, spots, tall = state_ref.shape[:3]
    rows = tall - 2 * REACH
    half = channels // 2
    block = spots * half
    total = 2 * spots * tall
    owners = recv_ref.shape[0] // total
    cols = grad_ref.shape[3]
    grad = recv_ref[0:total, :].astype(F32)
    for owner in range(1, owners):
        grad = grad + recv_ref[pl.ds(owner * total, total), :].astype(F32)
    for part in range(2):
        for spot in range(spots):
            row = (part * spots + spot) * tall
            grad_ref[part, spot] = grad[row : row + rows, :cols]
    lane = lax.broadcasted_iota(jnp.int32, (tall, 128), 1)
    row = lax.broadcasted_iota(jnp.int32, (tall, 128), 0)
    col_id = place_ref[1] * cols + jnp.where(lane < 112, lane, lane - 128)
    row_id = place_ref[0] * rows + jnp.where(row < rows + REACH, row, row - tall)
    inside = (col_id >= 0) & (col_id < cols * owners) & (row_id >= 0) & (row_id < place_ref[2])
    for channel in range(channels):
        for spot in range(spots):
            real = grad[spot * tall : (spot + 1) * tall]
            imag = grad[(spots + spot) * tall : (spots + spot + 1) * tall]
            added = inject_ref[channel, 0] * real + inject_ref[channel, 1] * imag
            merged = (state_ref[channel, spot].astype(F32) + added).astype(BF16).astype(F32)
            at = (channel // half * block + spot * half + channel % half) * tall
            wide_ref[pl.ds(at, tall), :] = jnp.where(inside, merged, 0.0)
    for i in range(tall):
        source = (i - REACH) % tall
        a_ref[pl.ds(i * block, block), :] = wide_ref[pl.ds(source, block, stride=tall), :].astype(BF16)
        b_ref[pl.ds(i * block, block), :] = wide_ref[pl.ds(block * tall + source, block, stride=tall), :].astype(BF16)
    keep = inside.astype(F32)
    for layer in range(weight_ref.shape[0]):
        source_ref, target_ref = (a_ref, b_ref) if layer % 2 == 0 else (b_ref, a_ref)
        weight = weight_ref[layer]
        mixer = mixer_ref[layer]
        bias = bias_ref[layer]
        for i in range(1 + layer, tall - 1 - layer, 2):
            cells = jnp.concatenate(
                [source_ref[pl.ds((j - 1) * block, 3 * block), :] for j in (i, i + 1)], axis=1
            )
            taps = nn(weight, cells)
            raw = []
            for j in range(2):
                at = slice(128 * j, 128 * j + 128)
                value = pltpu.roll(taps[0:block, at], 1, 1) + taps[block : 2 * block, at]
                value = value + pltpu.roll(taps[2 * block :, at], 127, 1)
                raw.append(jnp.maximum(value + bias, 0.0).astype(BF16))
            mixed = nn(mixer, jnp.concatenate(raw, axis=1))
            for j in range(2):
                here = pl.ds((i + j) * block, block)
                value = target_ref[here, :].astype(F32) + mixed[:, 128 * j : 128 * j + 128]
                source = (i + j - REACH) % tall
                value = value * keep[source : source + 1, :]
                target_ref[here, :] = value.astype(BF16)
    for i in range(REACH, REACH + rows):
        source = i - REACH
        wide_ref[pl.ds(source, block, stride=tall), :] = a_ref[pl.ds(i * block, block), :].astype(F32)
        wide_ref[pl.ds(block * tall + source, block, stride=tall), :] = b_ref[pl.ds(i * block, block), :].astype(F32)
    for channel in range(channels):
        for spot in range(spots):
            at = (channel // half * block + spot * half + channel % half) * tall
            new_ref[channel, spot] = wide_ref[pl.ds(at, rows), :][:, :cols].astype(BF16)


def coupling_weights(kernels, mixers):
    layers = kernels.shape[0]
    half = kernels.shape[2]
    taps = kernels.reshape(layers, 3, 3, 3, half, half)
    rows = []
    for out_spot in range(2):
        rows.append(jnp.stack([taps[:, in_spot - out_spot + 1] for in_spot in range(2)], axis=1))
    both = jnp.stack(rows, axis=1)
    weight = jnp.transpose(both, (0, 4, 1, 5, 3, 2, 6)).reshape(layers, 6 * half, 6 * half)
    zero = jnp.zeros_like(mixers)
    mixer = jnp.concatenate(
        [jnp.concatenate([mixers, zero], axis=2), jnp.concatenate([zero, mixers], axis=2)], axis=1
    )
    return weight, mixer


def swapped_edges(array, axis, dim):
    count = lax.axis_size(axis)
    ends = count - 1
    size = array.shape[dim]
    head = lax.slice_in_dim(array, 0, REACH, axis=dim)
    tail = lax.slice_in_dim(array, size - REACH, size, axis=dim)
    before = lax.ppermute(tail, axis, [(i, i + 1) for i in range(ends)])
    after = lax.ppermute(head, axis, [(i + 1, i) for i in range(ends)])
    return before, after


def per_device(state, sens, kdata, mask, inject, kernels, biases, mixers):
    channels, spots, rows, cols = state.shape
    coils = sens.shape[1]
    npar = sens.shape[4]
    npe = kdata.shape[4]
    lines = kdata.shape[3]
    groups = lax.axis_size("space")
    owners = lax.axis_size("coil")
    tall = rows + 2 * REACH
    place = jnp.stack([lax.axis_index("space"), lax.axis_index("coil"), jnp.int32(npe)]).astype(jnp.int32)

    estimate = jnp.pad(state[0:2], ((0, 0), (0, 0), (0, 0), (0, 128 - cols)))
    estimate = jnp.broadcast_to(estimate[None], (owners, *estimate.shape))
    estimate = lax.all_to_all(estimate, "coil", 0, 0, tiled=True)

    par_cos, par_sin = dft_tables(npar, np.arange(npar), 32)
    edge_columns = [
        (rows * d + r) % npe for d in range(groups) for r in (*range(rows, rows + REACH), *range(-REACH, 0))
    ]
    pe_cos, pe_sin = dft_tables(npe, [*range(npe), *edge_columns], 32)

    cells = coils * spots * rows
    sent = call(
        forward_columns,
        jax.ShapeDtypeStruct((npar, 2 * cells), BF16),
        [pltpu.VMEM((2 * cells, npar), BF16)],
        "forward_columns",
        [VMEM] * 4,
    )(estimate, sens, par_cos, par_sin)
    spectra = lax.all_to_all(sent, "space", 0, 0, tiled=True)

    sent = call(
        consistency,
        jax.ShapeDtypeStruct((npar, 384), BF16),
        [pltpu.VMEM((8 * lines, npe), BF16), pltpu.VMEM((8 * lines, npe), BF16)],
        "consistency",
        [VMEM] * 5,
    )(spectra, kdata, mask, pe_cos, pe_sin)
    returned = lax.all_to_all(sent, "space", 0, 0, tiled=True)

    above, below = swapped_edges(sens.astype(BF16), "space", 3)
    edge = jnp.concatenate([below, above], axis=3).astype(F32)

    sent = call(
        backward_columns,
        jax.ShapeDtypeStruct((owners * 2 * spots * tall, 128), BF16),
        [pltpu.VMEM((2 * spots * tall, npar), F32)],
        "backward_columns",
        [VMEM, VMEM, VMEM, SMEM, VMEM, VMEM],
    )(returned, sens, edge, place, par_cos, par_sin)
    shares = lax.all_to_all(sent, "coil", 0, 0, tiled=True)

    above, below = swapped_edges(state, "space", 2)
    wide = jnp.concatenate([state, below, above], axis=2)
    left, right = swapped_edges(wide, "coil", 3)
    gap = jnp.zeros((channels, spots, tall, 128 - cols - 2 * REACH), state.dtype)
    wide = jnp.concatenate([wide, right, gap, left], axis=3)

    weight, mixer = coupling_weights(kernels, mixers)
    block = channels // 2 * spots
    bias = jnp.broadcast_to(jnp.tile(biases, (1, spots))[:, :, None], (*biases.shape[:1], block, 128))
    new_state, gradient = call(
        couple,
        [
            jax.ShapeDtypeStruct(state.shape, BF16),
            jax.ShapeDtypeStruct((2, spots, rows, cols), F32),
        ],
        [
            pltpu.VMEM((2 * block * tall, 128), F32),
            pltpu.VMEM((block * tall, 128), BF16),
            pltpu.VMEM((block * tall, 128), BF16),
        ],
        "couple",
        [VMEM, VMEM, SMEM, SMEM, VMEM, VMEM, VMEM],
    )(shares, wide, place, inject, weight, bias, mixer)
    return (new_state, gradient)


def solution(mesh):
    return jax.shard_map(
        per_device,
        mesh=mesh,
        in_specs=(
            P(None, None, "space", "coil"),
            P(None, "coil", None, "space", None),
            P(None, "coil", None, "space", None),
            P("space", None),
            P(),
            P(),
            P(),
            P(),
        ),
        out_specs=(P(None, None, "space", "coil"), P(None, None, "space", "coil")),
        check_vma=False,
    )
```

profile of v0, /device:TPU:25, one launch (start us, length us, event | category | flops | bytes accessed | tf_op | source)
XLA Modules:
  0.0 140.8 jit_solution(3294502079819547835)
XLA Ops:
  0.6 0.8 slice.27
  1.4 0.8 broadcast_in_dim.6
  2.2 6.6 %all-to-all-start = ((bf16[8,2,2,32,128]{4,3,2,1,0:T(8,128)(2,1)}), bf16[8,2,2,32,128]{4,3,2,1,0:T(8,128)(2,1)S(1)}, u32[]{:S(2)}, u32[]{:S(2)}) async-start(bf16[8,2,2,32,128]{4,3,2,1,0:T(8,128)(2,1)} %broadcast_in_dim.6), calls=%async_computation | async-start | bytes 524288 | tf_op jit(solution)/shard_map/all_to_all | solution.py:332
  8.7 3.1 %add_convert_fusion.1 = (bf16[24,32,768]{2,1,0:T(8,128)(2,1)}, bf16[24,32,768]{2,1,0:T(8,128)(2,1)}) fusion(f32[32,768]{1,0:T(8,128)} %constant.35.clone, f32[24,768]{1,0:T(8,128)} %constant.33.clone, f32[32,768]{1,0:T(8,128)} %constant.34.clone, f32[24,768]{1,0:T(8,128)} %constant.32.clone), kind=kLoop, calls=%fused_computation.2 | loop fusion | flops 4718592 | bytes 2703360 | tf_op jit(solution)/shard_map/convert_element_type | solution.py:52
  11.9 5.5 %all-to-all-done.est_ref = bf16[8,2,2,32,128]{4,3,2,1,0:T(8,128)(2,1)S(1)} async-done(((bf16[8,2,2,32,128]{4,3,2,1,0:T(8,128)(2,1)}), bf16[8,2,2,32,128]{4,3,2,1,0:T(8,128)(2,1)S(1)}, u32[]{:S(2)}, u32[]{:S(2)}) %all-to-all-start) | async-done | bytes 262176 | tf_op jit(solution)/shard_map/all_to_all | solution.py:332
  17.4 0.7 copy-done.6
  18.1 3.7 %forward_columns.1 = bf16[768,256]{1,0:T(8,128)(2,1)} custom-call(bf16[8,2,2,32,128]{4,3,2,1,0:T(8,128)(2,1)} %copy-done.6, f32[2,2,2,32,768]{4,3,2,1,0:T(8,128)} %sens_ref.3, bf16[768,768]{1,0:T(8,128)(2,1)} %bitcast.21, bf16[768,768]{1,0:T(8,128)(2,1)} %bitcast.19), custom_call_target="tpu_custom_call" | custom-call | tf_op jit(solution)/shard_map/forward_columns/pallas_call | solution.py:341
  21.8 10.9 %all-to-all-start.1 = ((bf16[32,24,256]{2,1,0:T(8,128)(2,1)}), bf16[32,24,256]{2,1,0:T(8,128)(2,1)S(1)}, u32[]{:S(2)}, u32[]{:S(2)}) async-start(bf16[32,24,256]{2,1,0:T(8,128)(2,1)} %bitcast.29), calls=%async_computation.1 | async-start | bytes 786432 | tf_op jit(solution)/shard_map/all_to_all | solution.py:348
  32.8 3.9 %add_convert_fusion = (bf16[32,32,1280]{2,1,0:T(8,128)(2,1)}, bf16[32,32,1280]{2,1,0:T(8,128)(2,1)}) fusion(f32[32,1280]{1,0:T(8,128)S(1)} %copy-done.11, f32[32,1280]{1,0:T(8,128)S(1)} %copy-done.9, f32[32,1280]{1,0:T(8,128)S(1)} %copy-done.10, f32[32,1280]{1,0:T(8,128)S(1)} %copy-done.8), kind=kLoop, calls=%fused_computation | loop fusion | flops 10485760 | bytes 5898240 | tf_op jit(solution)/shard_map/convert_element_type | solution.py:52
  36.7 8.8 %all-to-all-done.1 = bf16[32,24,256]{2,1,0:T(8,128)(2,1)S(1)} async-done(((bf16[32,24,256]{2,1,0:T(8,128)(2,1)}), bf16[32,24,256]{2,1,0:T(8,128)(2,1)S(1)}, u32[]{:S(2)}, u32[]{:S(2)}) %all-to-all-start.1) | async-done | bytes 393248 | tf_op jit(solution)/shard_map/all_to_all | solution.py:348
  45.5 0.7 copy-done.4
  46.3 6.8 %consistency.1 = bf16[768,384]{1,0:T(8,128)(2,1)} custom-call(bf16[768,256]{1,0:T(8,128)(2,1)} %bitcast.28, f32[2,2,2,24,1024]{4,3,2,1,0:T(8,128)} %kdata_ref.1, s32[24,1024]{1,0:T(8,128)} %mask_ref.1, bf16[1024,1280]{1,0:T(8,128)(2,1)} %bitcast.24, bf16[1024,1280]{1,0:T(8,128)(2,1)} %bitcast.23), custom_call_target="tpu_custom_call" | custom-call | tf_op jit(solution)/shard_map/consistency/pallas_call | solution.py:350
  53.1 6.8 %all-to-all-start.2 = ((bf16[32,24,384]{2,1,0:T(8,128)(2,1)}), bf16[32,24,384]{2,1,0:T(8,128)(2,1)S(1)}, u32[]{:S(2)}, u32[]{:S(2)}) async-start(bf16[32,24,384]{2,1,0:T(8,128)(2,1)} %bitcast.27), calls=%async_computation.2 | async-start | bytes 1179648 | tf_op jit(solution)/shard_map/all_to_all | solution.py:357
  60.0 9.4 %collective-permute-start = (bf16[2,2,2,4,768]{4,3,2,1,0:T(4,128)(2,1)S(1)}, bf16[2,2,2,4,768]{4,3,2,1,0:T(4,128)(2,1)S(1)}, u32[]{:S(2)}, u32[]{:S(2)}) collective-permute-start(bf16[2,2,2,4,768]{4,3,2,1,0:T(4,128)(2,1)S(1)} %get-tuple-element.10), channel_id=1, source_target_pairs={{8,0},{16,8},{24,16},{32,24},{40,32},{48,40},{56,48},{64,56},{72,6... | collective-permute-start | bytes 147464 | tf_op jit(solution)/shard_map/ppermute | solution.py:315
  69.4 1.9 %collective-permute-start.1 = (bf16[2,2,2,4,768]{4,3,2,1,0:T(4,128)(2,1)S(1)}, bf16[2,2,2,4,768]{4,3,2,1,0:T(4,128)(2,1)S(1)}, u32[]{:S(2)}, u32[]{:S(2)}) collective-permute-start(bf16[2,2,2,4,768]{4,3,2,1,0:T(4,128)(2,1)S(1)} %get-tuple-element.11), channel_id=1, source_target_pairs={{0,8},{8,16},{16,24},{24,32},{32,40},{40,48},{48,56},{56,64},{64,7... | collective-permute-start | bytes 147464 | tf_op jit(solution)/shard_map/ppermute | solution.py:314
  71.3 0.1 fusion.4
  71.4 10.3 %collective-permute-start.2 = (bf16[32,2,4,96]{3,2,1,0:T(4,128)(2,1)S(1)}, bf16[32,2,4,96]{3,2,1,0:T(4,128)(2,1)S(1)}, u32[]{:S(2)}, u32[]{:S(2)}) collective-permute-start(bf16[32,2,4,96]{3,2,1,0:T(4,128)(2,1)S(1)} %get-tuple-element.6), channel_id=1, source_target_pairs={{8,0},{16,8},{24,16},{32,24},{40,32},{48,40},{56,48},{64,56},{72,6... | collective-permute-start | bytes 147464 | tf_op jit(solution)/shard_map/ppermute | solution.py:315
  81.7 1.9 %collective-permute-start.3 = (bf16[32,2,4,96]{3,2,1,0:T(4,128)(2,1)S(1)}, bf16[32,2,4,96]{3,2,1,0:T(4,128)(2,1)S(1)}, u32[]{:S(2)}, u32[]{:S(2)}) collective-permute-start(bf16[32,2,4,96]{3,2,1,0:T(4,128)(2,1)S(1)} %get-tuple-element.7), channel_id=1, source_target_pairs={{0,8},{8,16},{16,24},{24,32},{32,40},{40,48},{48,56},{56,64},{64,7... | collective-permute-start | bytes 147464 | tf_op jit(solution)/shard_map/ppermute | solution.py:314
  83.6 0.5 copy.28
  84.1 0.1 slice_bitcast_fusion.1
  84.2 1.0 maximum_bitcast_fusion
  85.2 0.6 pad_add_fusion.place_ref
  85.7 0.0 collective-permute-done
  85.7 0.7 maximum_convert_fusion.edge_ref
  86.5 0.0 collective-permute-done.2
  86.5 7.1 %collective-permute-done.3 = bf16[32,2,4,96]{3,2,1,0:T(4,128)(2,1)S(1)} collective-permute-done((bf16[32,2,4,96]{3,2,1,0:T(4,128)(2,1)S(1)}, bf16[32,2,4,96]{3,2,1,0:T(4,128)(2,1)S(1)}, u32[]{:S(2)}, u32[]{:S(2)}) %collective-permute-start.3) | collective-permute-done | bytes 49184 | tf_op jit(solution)/shard_map/ppermute | solution.py:314
  93.6 0.2 pad_maximum_fusion
  93.8 0.8 copy-done.2
  94.7 4.0 %backward_columns.1 = bf16[1280,128]{1,0:T(8,128)(2,1)} custom-call(bf16[768,384]{1,0:T(8,128)(2,1)} %bitcast.26, f32[2,2,2,32,768]{4,3,2,1,0:T(8,128)} %sens_ref.3, f32[2,2,2,8,768]{4,3,2,1,0:T(8,128)} %maximum_convert_fusion.edge_ref, s32[3]{0:T(128)} %pad_add_fusion.place_ref, bf16[768,768]{1,0:T(8,128)(2,1)} %bitcast.22, bf16[768,768]{1,0:T(8,128)(2,1)} %bitcast.20), custom_call_target="tpu_custom_call" | custom-call | tf_op jit(solution)/shard_map/backward_columns/pallas_call | solution.py:362
  98.7 9.5 %all-to-all-start.3 = ((bf16[8,160,128]{2,1,0:T(8,128)(2,1)}), bf16[8,160,128]{2,1,0:T(8,128)(2,1)S(1)}, u32[]{:S(2)}, u32[]{:S(2)}) async-start(bf16[8,160,128]{2,1,0:T(8,128)(2,1)} %bitcast.30), calls=%async_computation.3 | async-start | bytes 655360 | tf_op jit(solution)/shard_map/all_to_all | solution.py:369
  108.2 0.3 fusion.3
  108.4 0.5 copy.24
  109.0 2.0 %collective-permute-start.4 = (bf16[32,2,40,4]{2,0,3,1:T(8,128)(2,1)S(1)}, bf16[32,2,40,4]{2,0,3,1:T(8,128)(2,1)S(1)}, u32[]{:S(2)}, u32[]{:S(2)}) collective-permute-start(bf16[32,2,40,4]{2,0,3,1:T(8,128)(2,1)S(1)} %copy.24), channel_id=1, source_target_pairs={{1,0},{2,1},{3,2},{4,3},{5,4},{6,5},{7,6},{9,8},{10,9},{11,10},{12... | collective-permute-start | bytes 61448 | tf_op jit(solution)/shard_map/ppermute | solution.py:315
  111.0 0.5 copy.25
  111.5 3.7 %collective-permute-start.5 = (bf16[32,2,40,4]{2,0,3,1:T(8,128)(2,1)S(1)}, bf16[32,2,40,4]{2,0,3,1:T(8,128)(2,1)S(1)}, u32[]{:S(2)}, u32[]{:S(2)}) collective-permute-start(bf16[32,2,40,4]{2,0,3,1:T(8,128)(2,1)S(1)} %copy.25), channel_id=1, source_target_pairs={{0,1},{1,2},{2,3},{3,4},{4,5},{5,6},{6,7},{8,9},{9,10},{10,11},{11... | collective-permute-start | bytes 61448 | tf_op jit(solution)/shard_map/ppermute | solution.py:314
  115.3 0.7 fusion.2.mixer_ref
  116.0 0.6 copy.29
  116.6 0.9 reshape.68.weight_ref
  117.5 0.7 tile.8
  118.2 0.1 tile.9
  118.3 1.4 copy.30.inject_ref
  119.6 0.1 pad.15.clone
  119.7 0.0 collective-permute-done.4
  119.7 0.5 copy.26
  120.2 0.5 copy.27
  120.7 1.5 %pad_maximum_fusion.1.state_ref = bf16[32,2,40,128]{3,2,1,0:T(8,128)(2,1)} fusion(bf16[32,2,40,4]{3,2,1,0:T(8,128)(2,1)S(1)} %copy.27, bf16[32,2,40,4]{3,2,1,0:T(8,128)(2,1)S(1)} %copy.26, bf16[32,2,4,96]{3,2,1,0:T(4,128)(2,1)S(1)} %collective-permute-done.3, bf16[32,2,4,96]{3,2,1,0:T(4,128)(2,1)S(1)} %collective-permute-done.2, ...), kind=kLoop, calls=%fused_computation.5 | loop fusion | flops 3932160 | bytes 1188096 | tf_op jit(solution)/shard_map/concatenate | solution.py:375
  122.3 0.8 broadcast_in_dim.8.bias_ref
  123.1 17.7 %couple.1 = (bf16[32,2,32,96]{3,2,1,0:T(8,128)(2,1)}, f32[2,2,32,96]{3,2,1,0:T(8,128)}) custom-call(bf16[1280,128]{1,0:T(8,128)(2,1)} %bitcast.31, bf16[32,2,40,128]{3,2,1,0:T(8,128)(2,1)} %pad_maximum_fusion.1.state_ref, s32[3]{0:T(128)} %pad_add_fusion.place_ref, f32[32,2]{1,0:T(8,128)} %copy.30.inject_ref, bf16[4,96,96]{2,1,0:T(8,128)(2,1)} %reshape.68.weight_ref, ...), custom_call_target="tpu_custom_call" | custom-call | tf_op jit(solution)/shard_map/couple/pallas_call | solution.py:380
  (31 shorter events, 0.2 us)
Async XLA Ops:
  2.2 15.2 %all-to-all-start = ((bf16[8,2,2,32,128]{4,3,2,1,0:T(8,128)(2,1)}), bf16[8,2,2,32,128]{4,3,2,1,0:T(8,128)(2,1)S(1)}, u32[]{:S(2)}, u32[]{:S(2)}) async-start(bf16[8,2,2,32,128]{4,3,2,1,0:T(8,128)(2,1)} %broadcast_in_dim.6), calls=%async_computation | async-start | bytes 524288 | tf_op jit(solution)/shard_map/all_to_all | solution.py:332
  11.9 20.8 %copy-start = (f32[2,2,2,32,768]{4,3,2,1,0:T(8,128)S(1)}, f32[2,2,2,32,768]{4,3,2,1,0:T(8,128)}, u32[]{:S(2)}) copy-start(f32[2,2,2,32,768]{4,3,2,1,0:T(8,128)} %sens_ref.3) | copy-start | bytes 2359300
  17.4 0.7 copy-start.6
  18.1 14.6 %copy-start.8 = (f32[32,1280]{1,0:T(8,128)S(1)}, f32[32,1280]{1,0:T(8,128)}, u32[]{:S(2)}) copy-start(f32[32,1280]{1,0:T(8,128)} %constant.36.clone) | copy-start | bytes 491524
  18.1 14.6 %copy-start.9 = (f32[32,1280]{1,0:T(8,128)S(1)}, f32[32,1280]{1,0:T(8,128)}, u32[]{:S(2)}) copy-start(f32[32,1280]{1,0:T(8,128)} %constant.37.clone) | copy-start | bytes 491524
  18.1 14.7 %copy-start.10 = (f32[32,1280]{1,0:T(8,128)S(1)}, f32[32,1280]{1,0:T(8,128)}, u32[]{:S(2)}) copy-start(f32[32,1280]{1,0:T(8,128)} %constant.38.clone) | copy-start | bytes 491524
  18.1 14.7 %copy-start.11 = (f32[32,1280]{1,0:T(8,128)S(1)}, f32[32,1280]{1,0:T(8,128)}, u32[]{:S(2)}) copy-start(f32[32,1280]{1,0:T(8,128)} %constant.39.clone) | copy-start | bytes 491524
  21.8 23.7 %all-to-all-start.1 = ((bf16[32,24,256]{2,1,0:T(8,128)(2,1)}), bf16[32,24,256]{2,1,0:T(8,128)(2,1)S(1)}, u32[]{:S(2)}, u32[]{:S(2)}) async-start(bf16[32,24,256]{2,1,0:T(8,128)(2,1)} %bitcast.29), calls=%async_computation.1 | async-start | bytes 786432 | tf_op jit(solution)/shard_map/all_to_all | solution.py:348
  45.5 0.7 copy-start.4
  46.3 25.0 %copy-start.1 = (bf16[32,2,32,96]{3,2,1,0:T(8,128)(2,1)S(1)}, bf16[32,2,32,96]{3,2,1,0:T(8,128)(2,1)}, u32[]{:S(2)}) copy-start(bf16[32,2,32,96]{3,2,1,0:T(8,128)(2,1)} %param.16) | copy-start | bytes 1179652
  46.3 37.3 %copy-start.7 = (bf16[4,27,16,16]{1,3,2,0:T(8,128)(2,1)S(1)}, bf16[4,27,16,16]{1,3,2,0:T(8,128)(2,1)}, u32[]{:S(2)}) copy-start(bf16[4,27,16,16]{1,3,2,0:T(8,128)(2,1)} %param.21) | copy-start | bytes 165892
  53.1 40.7 %all-to-all-start.2 = ((bf16[32,24,384]{2,1,0:T(8,128)(2,1)}), bf16[32,24,384]{2,1,0:T(8,128)(2,1)S(1)}, u32[]{:S(2)}, u32[]{:S(2)}) async-start(bf16[32,24,384]{2,1,0:T(8,128)(2,1)} %bitcast.27), calls=%async_computation.2 | async-start | bytes 1179648 | tf_op jit(solution)/shard_map/all_to_all | solution.py:357
  60.0 25.8 %collective-permute-start = (bf16[2,2,2,4,768]{4,3,2,1,0:T(4,128)(2,1)S(1)}, bf16[2,2,2,4,768]{4,3,2,1,0:T(4,128)(2,1)S(1)}, u32[]{:S(2)}, u32[]{:S(2)}) collective-permute-start(bf16[2,2,2,4,768]{4,3,2,1,0:T(4,128)(2,1)S(1)} %get-tuple-element.10), channel_id=1, source_target_pairs={{8,0},{16,8},{24,16},{32,24},{40,32},{48,40},{56,48},{64,56},{72,6... | collective-permute-start | bytes 147464 | tf_op jit(solution)/shard_map/ppermute | solution.py:315
  69.4 16.4 %collective-permute-start.1 = (bf16[2,2,2,4,768]{4,3,2,1,0:T(4,128)(2,1)S(1)}, bf16[2,2,2,4,768]{4,3,2,1,0:T(4,128)(2,1)S(1)}, u32[]{:S(2)}, u32[]{:S(2)}) collective-permute-start(bf16[2,2,2,4,768]{4,3,2,1,0:T(4,128)(2,1)S(1)} %get-tuple-element.11), channel_id=1, source_target_pairs={{0,8},{8,16},{16,24},{24,32},{32,40},{40,48},{48,56},{56,64},{64,7... | collective-permute-start | bytes 147464 | tf_op jit(solution)/shard_map/ppermute | solution.py:314
  71.4 15.1 %collective-permute-start.2 = (bf16[32,2,4,96]{3,2,1,0:T(4,128)(2,1)S(1)}, bf16[32,2,4,96]{3,2,1,0:T(4,128)(2,1)S(1)}, u32[]{:S(2)}, u32[]{:S(2)}) collective-permute-start(bf16[32,2,4,96]{3,2,1,0:T(4,128)(2,1)S(1)} %get-tuple-element.6), channel_id=1, source_target_pairs={{8,0},{16,8},{24,16},{32,24},{40,32},{48,40},{56,48},{64,56},{72,6... | collective-permute-start | bytes 147464 | tf_op jit(solution)/shard_map/ppermute | solution.py:315
  81.7 11.9 %collective-permute-start.3 = (bf16[32,2,4,96]{3,2,1,0:T(4,128)(2,1)S(1)}, bf16[32,2,4,96]{3,2,1,0:T(4,128)(2,1)S(1)}, u32[]{:S(2)}, u32[]{:S(2)}) collective-permute-start(bf16[32,2,4,96]{3,2,1,0:T(4,128)(2,1)S(1)} %get-tuple-element.7), channel_id=1, source_target_pairs={{0,8},{8,16},{16,24},{24,32},{32,40},{40,48},{48,56},{56,64},{64,7... | collective-permute-start | bytes 147464 | tf_op jit(solution)/shard_map/ppermute | solution.py:314
  93.8 0.8 copy-start.2
  98.7 16.6 %copy-start.12 = (bf16[4,16,16]{2,1,0:T(8,128)(2,1)S(1)}, bf16[4,16,16]{2,1,0:T(8,128)(2,1)}, u32[]{:S(2)}) copy-start(bf16[4,16,16]{2,1,0:T(8,128)(2,1)} %param.23) | copy-start | bytes 6148
  98.7 17.3 %copy-start.3 = (bf16[4,3,2,16,3,2,16]{6,3,1,4,5,0,2:T(8,128)(2,1)S(1)}, bf16[4,3,2,16,3,2,16]{6,3,1,4,5,0,2:T(8,128)(2,1)}, u32[]{:S(2)}) copy-start(bf16[4,3,2,16,3,2,16]{6,3,1,4,5,0,2:T(8,128)(2,1)} %maximum_bitcast_fusion) | copy-start | bytes 221188
  98.7 23.6 %all-to-all-start.3 = ((bf16[8,160,128]{2,1,0:T(8,128)(2,1)}), bf16[8,160,128]{2,1,0:T(8,128)(2,1)S(1)}, u32[]{:S(2)}, u32[]{:S(2)}) async-start(bf16[8,160,128]{2,1,0:T(8,128)(2,1)} %bitcast.30), calls=%async_computation.3 | async-start | bytes 655360 | tf_op jit(solution)/shard_map/all_to_all | solution.py:369
  109.0 10.7 %collective-permute-start.4 = (bf16[32,2,40,4]{2,0,3,1:T(8,128)(2,1)S(1)}, bf16[32,2,40,4]{2,0,3,1:T(8,128)(2,1)S(1)}, u32[]{:S(2)}, u32[]{:S(2)}) collective-permute-start(bf16[32,2,40,4]{2,0,3,1:T(8,128)(2,1)S(1)} %copy.24), channel_id=1, source_target_pairs={{1,0},{2,1},{3,2},{4,3},{5,4},{6,5},{7,6},{9,8},{10,9},{11,10},{12... | collective-permute-start | bytes 61448 | tf_op jit(solution)/shard_map/ppermute | solution.py:315
  111.5 8.7 %collective-permute-start.5 = (bf16[32,2,40,4]{2,0,3,1:T(8,128)(2,1)S(1)}, bf16[32,2,40,4]{2,0,3,1:T(8,128)(2,1)S(1)}, u32[]{:S(2)}, u32[]{:S(2)}) collective-permute-start(bf16[32,2,40,4]{2,0,3,1:T(8,128)(2,1)S(1)} %copy.25), channel_id=1, source_target_pairs={{0,1},{1,2},{2,3},{3,4},{4,5},{5,6},{6,7},{8,9},{9,10},{10,11},{11... | collective-permute-start | bytes 61448 | tf_op jit(solution)/shard_map/ppermute | solution.py:314
  122.3 0.8 copy-start.5
where the time goes:
time: 142 us; the launch traced here: 141 us
  starting transfers between devices  63 us (44%)
  Pallas kernels  32.2 us (23%)
  waiting for transfers between devices  21.5 us (15%)
  other arithmetic  11.8 us (8%)
  local copies, waits for them, and re-layouts  11.4 us (8%)
    ppermute x3, starting transfers between devices, swapped_edges(): after = lax.ppermute(head, axis, [(i + 1, i) for i in range(ends)])  21.7 us
    pallas_call x1, Pallas kernels, per_device(): call(couple, [jax.ShapeDtypeStruct(state.shape, BF16), jax.ShapeDtypeStru...  17.7 us
    all_to_all x1, starting transfers between devices, per_device(): spectra = lax.all_to_all(sent, 'space', 0, 0, tiled=True)  10.9 us
    all_to_all x1, starting transfers between devices, per_device(): shares = lax.all_to_all(sent, 'coil', 0, 0, tiled=True)  9.5 us
    all_to_all x1, waiting for transfers between devices, per_device(): spectra = lax.all_to_all(sent, 'space', 0, 0, tiled=True)  8.82 us
    ppermute x3, starting transfers between devices, swapped_edges(): before = lax.ppermute(tail, axis, [(i, i + 1) for i in range(ends)])  7.57 us
    ppermute x3, waiting for transfers between devices, swapped_edges(): before = lax.ppermute(tail, axis, [(i, i + 1) for i in range(ends)])  7.13 us
    convert_element_type x2, other arithmetic, dft_tables(): sin = (sin_a * cos_b + cos_a * sin_b).astype(BF16)  7.06 us
  transfers between devices with their start and end apart: 10, of which 3 were waited for; matrix products, arithmetic and copies ran while one was open for 13% of the time, Pallas kernels for 0%

commit v1 on v0

v1 whole, which is shorter than its diff:
```python
import numpy as np

import jax
import jax.numpy as jnp
from jax import lax
from jax.experimental import pallas as pl
from jax.experimental.pallas import tpu as pltpu
from jax.sharding import PartitionSpec as P

F32 = jnp.float32
BF16 = jnp.bfloat16
REACH = 4
FINE = 32
BATCH = 12
VMEM = pl.BlockSpec(memory_space=pltpu.VMEM)


def call(body, outs, scratch, name, *args):
    specs, values = [], []
    for arg in args:
        where, value = arg if isinstance(arg, tuple) else ("vmem", arg)
        if where != "plain":
            value = pltpu.with_memory_space_constraint(value, pltpu.HBM if where == "hbm" else pltpu.VMEM)
        specs.append(pl.BlockSpec(memory_space=pltpu.HBM) if where == "hbm" else VMEM)
        values.append(value)
    shapes = []
    for out in outs:
        shapes.append(pltpu.VMEM(*out) if isinstance(out, tuple) else out)
    return pl.pallas_call(
        body,
        out_shape=shapes,
        in_specs=specs,
        out_specs=[VMEM] * len(outs),
        scratch_shapes=[each if not isinstance(each, tuple) else pltpu.VMEM(*each) for each in scratch],
        compiler_params=pltpu.CompilerParams(vmem_limit_bytes=20 * 2**20),
        name=name,
    )(*values)


def in_hbm(value):
    return ("hbm", value)


def plain(value):
    return ("plain", value)


def table_copies(pairs, sems, step):
    blocks = []
    for start in range(0, pairs[0][0].shape[1], step):
        here = pl.ds(start, step)
        block = []
        for source, target in pairs:
            copy = pltpu.make_async_copy(source.at[:, here], target.at[:, here], sems.at[len(blocks) * len(pairs) + len(block)])
            copy.start()
            block.append(copy)
        blocks.append(block)
    return blocks


def arrived(block):
    for copy in block:
        copy.wait()


def dft_factors(length, columns, step):
    columns = np.asarray(columns)[None, :]
    coarse = (step * np.arange(length // step))[:, None] * columns % length
    fine = np.arange(step)[:, None] * columns % length
    angle_coarse = coarse * (2.0 * np.pi / length)
    angle_fine = fine * (2.0 * np.pi / length)
    scale = 1.0 / np.sqrt(length)
    parts = (np.cos(angle_coarse) * scale, np.sin(angle_coarse) * scale, np.cos(angle_fine), np.sin(angle_fine))
    return np.concatenate(parts).astype(np.float32)


def dft_tables(factors_ref, cos_ref, sin_ref):
    count = cos_ref.shape[0] // FINE
    cos_b = factors_ref[pl.ds(2 * count, FINE), :]
    sin_b = factors_ref[pl.ds(2 * count + FINE, FINE), :]
    for a in range(count):
        here = pl.ds(a * FINE, FINE)
        cos, sin = factors_ref[pl.ds(a, 1), :], factors_ref[pl.ds(count + a, 1), :]
        cos_ref[here, :] = (cos * cos_b - sin * sin_b).astype(BF16)
        sin_ref[here, :] = (sin * cos_b + cos * sin_b).astype(BF16)


def swap_groups(tiles, group):
    tiles = list(tiles)
    count = len(tiles)
    lane = lax.broadcasted_iota(jnp.int32, tiles[0].shape, 1)
    bit = count // 2
    while bit:
        shift = bit * group
        high = (lane // shift) % 2 == 1
        for low in range(count):
            if low & bit:
                continue
            a, b = tiles[low], tiles[low | bit]
            tiles[low] = jnp.where(high, pltpu.roll(b, shift, 1), a)
            tiles[low | bit] = jnp.where(high, b, pltpu.roll(a, 128 - shift, 1))
        bit //= 2
    return tiles


def nn(a, b):
    return lax.dot_general(a, b, (((1,), (0,)), ((), ())), preferred_element_type=F32)


def nt(a, b):
    return lax.dot_general(a, b, (((1,), (1,)), ((), ())), preferred_element_type=F32)


def forward_columns(est_ref, sens_ref, cos_hbm, sin_hbm, out_ref, img_ref, cos_ref, sin_ref, sems):
    blocks = table_copies([(cos_hbm, cos_ref), (sin_hbm, sin_ref)], sems, cos_ref.shape[1])
    owners = est_ref.shape[0]
    rows = sens_ref.shape[3]
    npar = sens_ref.shape[4]
    width = npar // owners
    lane = lax.broadcasted_iota(jnp.int32, (rows, 128), 1)
    coils, spots = sens_ref.shape[1:3]
    for spot in range(spots):
        for tile in range(npar // 128):
            full = []
            for part in range(2):
                value = None
                for owner in range(128 * tile // width, (128 * tile + 127) // width + 1):
                    at = width * owner - 128 * tile
                    piece = est_ref[owner, part, spot].astype(F32)
                    if at % 128:
                        piece = pltpu.roll(piece, at % 128, 1)
                    value = piece if value is None else jnp.where(lane >= at, piece, value)
                full.append(value)
            est_re, est_im = full
            cols = pl.ds(128 * tile, 128)
            for coil in range(coils):
                sens_re = sens_ref[0, coil, spot, :, cols]
                sens_im = sens_ref[1, coil, spot, :, cols]
                row = (coil * spots + spot) * rows
                img_ref[pl.ds(row, rows), cols] = (sens_re * est_re - sens_im * est_im).astype(BF16)
                img_ref[pl.ds(128 + row, rows), cols] = (sens_re * est_im + sens_im * est_re).astype(BF16)
    img = img_ref[...]
    arrived(blocks[0])
    step = 256
    for start in range(0, npar, step):
        here = pl.ds(start, step)
        by_cos = nt(cos_ref[here, :], img)
        by_sin = nt(sin_ref[here, :], img)
        out_ref[here, 0:128] = (by_cos[:, :128] + by_sin[:, 128:]).astype(BF16)
        out_ref[here, 128:256] = (by_cos[:, 128:] - by_sin[:, :128]).astype(BF16)


def consistency(recv_ref, kdata_ref, mask_ref, cos_hbm, sin_hbm, out_ref, x_ref, res_ref, cos_ref, sin_ref, sems):
    step = 256
    blocks = table_copies([(cos_hbm, cos_ref), (sin_hbm, sin_ref)], sems, step)
    lines = mask_ref.shape[0]
    npe = mask_ref.shape[1]
    sources = recv_ref.shape[0] // lines
    half = 4 * lines
    for quad in range(sources // 4):
        stacked = []
        for part in range(2):
            tiles = [
                recv_ref[pl.ds((4 * quad + s) * lines, lines), pl.ds(128 * part, 128)].astype(F32) for s in range(4)
            ]
            stacked += swap_groups(tiles, 32)
        x_ref[:, pl.ds(128 * quad, 128)] = jnp.concatenate(stacked, axis=0).astype(BF16)
    x = x_ref[...]
    for start in range(0, npe, step):
        here = pl.ds(start, step)
        arrived(blocks[start // step])
        by_cos = nn(x, cos_ref[:, here])
        by_sin = nn(x, sin_ref[:, here])
        sampled = mask_ref[:, here].astype(F32)
        sampled = jnp.concatenate([sampled] * 4, axis=0)
        data = [
            jnp.concatenate([kdata_ref[part, c, p, :, here] for c in range(2) for p in range(2)], axis=0)
            for part in range(2)
        ]
        real = sampled * (by_cos[:half] + by_sin[half:] - data[0])
        imag = sampled * (by_cos[half:] - by_sin[:half] - data[1])
        res_ref[0:half, here] = real.astype(BF16)
        res_ref[half : 2 * half, here] = imag.astype(BF16)
    res = res_ref[...]
    for start in range(0, cos_ref.shape[1], step):
        here = pl.ds(start, step)
        if start >= npe:
            arrived(blocks[start // step])
        by_cos = nn(res, cos_ref[:, here])
        by_sin = nn(res, sin_ref[:, here])
        parts = (by_cos[:half] - by_sin[half:], by_cos[half:] + by_sin[:half])
        for tile in range(step // 128):
            at = slice(128 * tile, 128 * tile + 128)
            tiles = [part[lines * g : lines * (g + 1), at] for part in parts for g in range(4)]
            if start < npe:
                quad = start // 128 + tile
                for part in range(2):
                    for s, value in enumerate(swap_groups(tiles[4 * part : 4 * part + 4], 32)):
                        out_ref[pl.ds((4 * quad + s) * lines, lines), pl.ds(128 * part, 128)] = value.astype(BF16)
            else:
                group = (start - npe) // 128 + tile
                for s, value in enumerate(swap_groups(tiles, 8)):
                    value = value.astype(BF16)
                    for half_id in range(2):
                        owner = 16 * group + 8 * half_id + s
                        out_ref[pl.ds(owner * lines, lines), 256:384] = value


def backward_columns(
    recv_ref, sens_ref, above_ref, below_ref, cos_hbm, sin_hbm, out_ref, part_ref, edge_ref, cos_ref, sin_ref, sems
):
    step = 256
    blocks = table_copies([(cos_hbm, cos_ref), (sin_hbm, sin_ref)], sems, step)
    npar = sens_ref.shape[4]
    coils, spots, rows = sens_ref.shape[1:4]
    cells = coils * spots * rows
    edges = coils * spots * 2 * REACH
    turned = recv_ref[...].astype(F32).T
    low = lax.axis_index("space") // 8 % 2 == 0
    for tile in range(npar // 128):
        here = pl.ds(tile * 2 * coils * spots * REACH, 2 * coils * spots * REACH)
        above, below = above_ref[here, :].astype(F32), below_ref[here, :].astype(F32)
        for k in range(2 * coils * spots):
            at = slice(k * REACH, (k + 1) * REACH)
            part, coil, spot = k // (coils * spots), k // spots % coils, k % spots
            edge_ref[part, coil, spot, :, pl.ds(128 * tile, 128)] = jnp.concatenate([below[at], above[at]], axis=0)
    border = jnp.where(low, turned[2 * cells : 2 * cells + 2 * edges], turned[2 * cells + 2 * edges :])
    x = jnp.concatenate([turned[: 2 * cells], border], axis=0).astype(BF16)
    for start in range(0, npar, step):
        here = pl.ds(start, step)
        arrived(blocks[start // step])
        by_cos = nn(x, cos_ref[:, here])
        by_sin = nn(x, sin_ref[:, here])
        for first, count, profile_ref, offset in ((0, cells, sens_ref, 0), (2 * cells, edges, edge_ref, rows)):
            second = first + count
            last = second + count
            real = by_cos[first:second] - by_sin[second:last]
            imag = by_cos[second:last] + by_sin[first:second]
            per_coil = count // coils
            height = per_coil // spots
            sums = [0.0, 0.0]
            for coil in range(coils):
                profile = [
                    jnp.concatenate([profile_ref[part, coil, spot, :, here] for spot in range(spots)], axis=0).astype(F32)
                    for part in range(2)
                ]
                re = real[coil * per_coil : (coil + 1) * per_coil]
                im = imag[coil * per_coil : (coil + 1) * per_coil]
                sums[0] = sums[0] + (profile[0] * re + profile[1] * im)
                sums[1] = sums[1] + (profile[0] * im - profile[1] * re)
            for part in range(2):
                for spot in range(spots):
                    row = (part * spots + spot) * (rows + 2 * REACH) + offset
                    part_ref[pl.ds(row, height), here] = sums[part][spot * height : (spot + 1) * height]
    total = part_ref.shape[0]
    owners = out_ref.shape[0] // total
    width = npar // owners
    lane = lax.broadcasted_iota(jnp.int32, (total, 128), 1)
    count = npar // 128
    for owner in range(owners):
        tile, off = divmod(width * owner, 128)
        value = part_ref[:, pl.ds(128 * tile, 128)]
        if off:
            value = pltpu.roll(value, 128 - off, 1)
            if tile + 1 < count:
                following = pltpu.roll(part_ref[:, pl.ds(128 * (tile + 1), 128)], 128 - off, 1)
                value = jnp.where((lane >= 128 - off) & (lane < 112), following, value)
        elif tile:
            value = jnp.where(lane >= 112, part_ref[:, pl.ds(128 * (tile - 1), 128)], value)
        out_ref[pl.ds(owner * total, total), :] = value.astype(BF16)


def pack_rows(state_ref, sens_ref, tail_ref, head_ref):
    channels, spots, rows, cols = state_ref.shape
    coils, npar = sens_ref.shape[1], sens_ref.shape[4]
    at = 0
    for tile in range(npar // 128):
        here = pl.ds(128 * tile, 128)
        for part in range(2):
            for coil in range(coils):
                for ref, low in ((tail_ref, rows - 8), (head_ref, 0)):
                    pair = [sens_ref[part, coil, spot, pl.ds(low, 8), here] for spot in range(2)]
                    ref[pl.ds(at, 8), :] = joined_edges(pair, low).astype(BF16)
                at += 8
    for channel in range(channels):
        for ref, low in ((tail_ref, rows - 8), (head_ref, 0)):
            pair = [state_ref[channel, spot, pl.ds(low, 8), :].astype(F32) for spot in range(2)]
            ref[pl.ds(at, 8), 0:cols] = joined_edges(pair, low).astype(BF16)
        at += 8


def joined_edges(pair, low):
    first, second = pair
    if low:
        return jnp.concatenate([first[REACH:], second[REACH:]], axis=0)
    return jnp.concatenate([first[:REACH], second[:REACH]], axis=0)


def tall_state(state_ref, above_ref, below_ref, channel, spot, skip):
    cols = state_ref.shape[3]
    at = skip + 8 * channel
    below = below_ref[pl.ds(at, 8), 0:cols].astype(F32)[spot * REACH : (spot + 1) * REACH]
    above = above_ref[pl.ds(at, 8), 0:cols].astype(F32)[spot * REACH : (spot + 1) * REACH]
    value = jnp.concatenate([state_ref[channel, spot].astype(F32), jnp.concatenate([below, above], axis=0)], axis=0)
    return jnp.concatenate([value, jnp.zeros((value.shape[0], 128 - cols), F32)], axis=1)


def pack_cols(state_ref, above_ref, below_ref, tail_ref, head_ref):
    channels, spots, rows, cols = state_ref.shape
    tall = rows + 2 * REACH
    skip = above_ref.shape[0] - channels * spots * REACH
    per = 128 // REACH
    lane = lax.broadcasted_iota(jnp.int32, (tall, 128), 1)
    for group in range(channels * spots // per):
        tail = head = jnp.zeros((tall, 128), F32)
        for k in range(per):
            channel, spot = divmod(group * per + k, spots)
            value = tall_state(state_ref, above_ref, below_ref, channel, spot, skip)
            here = lane // REACH == k
            tail = jnp.where(here, pltpu.roll(value, (REACH * k - cols + REACH) % 128, 1), tail)
            head = jnp.where(here, pltpu.roll(value, REACH * k, 1) if k else value, head)
        tail_ref[pl.ds(group * tall, tall), :] = tail.astype(BF16)
        head_ref[pl.ds(group * tall, tall), :] = head.astype(BF16)


def spread_state(state_ref, above_ref, below_ref, left_ref, right_ref, out_ref, wide_ref):
    channels, spots, rows, cols = state_ref.shape
    tall = rows + 2 * REACH
    half = channels // 2
    skip = above_ref.shape[0] - channels * spots * REACH
    per = 128 // REACH
    lane = lax.broadcasted_iota(jnp.int32, (tall, 128), 1)
    for channel in range(channels):
        for spot in range(spots):
            group, k = divmod(channel * spots + spot, per)
            value = tall_state(state_ref, above_ref, below_ref, channel, spot, skip)
            here = pl.ds(group * tall, tall)
            right = pltpu.roll(right_ref[here, :].astype(F32), (cols - REACH * k) % 128, 1)
            left = pltpu.roll(left_ref[here, :].astype(F32), (128 - REACH - REACH * k) % 128, 1)
            value = jnp.where((lane >= cols) & (lane < cols + REACH), right, value)
            value = jnp.where(lane >= 128 - REACH, left, value)
            at = ((channel // half * spots + spot) * half + channel % half) * tall
            wide_ref[pl.ds(at, tall), :] = value
    count = channels * spots
    for i in range(tall):
        out_ref[pl.ds(i * count, count), :] = wide_ref[pl.ds((i - REACH) % tall, count, stride=tall), :].astype(BF16)


def coupling_weights(kernels_ref, biases_ref, mixers_ref, inject_ref, weight_ref, mixer_ref, bias_ref, added_ref):
    layers = kernels_ref.shape[0]
    half = kernels_ref.shape[2]
    eye = lax.broadcasted_iota(jnp.int32, (half, half), 0) == lax.broadcasted_iota(jnp.int32, (half, half), 1)
    zero = jnp.zeros((half, half), F32)
    for layer in range(layers):
        for c in range(3):
            for out_spot in range(2):
                blocks = [
                    kernels_ref[layer, 9 * (in_spot - out_spot + 1) + 3 * b + c].astype(F32)
                    for b in range(3)
                    for in_spot in range(2)
                ]
                weight_ref[layer, pl.ds((2 * c + out_spot) * half, half), :] = jnp.concatenate(blocks, axis=1).astype(BF16)
        mixer = mixers_ref[layer].astype(F32)
        mixer_ref[layer, 0:half, :] = jnp.concatenate([mixer, zero], axis=1).astype(BF16)
        mixer_ref[layer, half : 2 * half, :] = jnp.concatenate([zero, mixer], axis=1).astype(BF16)
        row = jnp.broadcast_to(biases_ref[pl.ds(layer, 1), :], (half, half))
        column = jnp.sum(jnp.where(eye, row, 0.0), axis=1, keepdims=True)
        bias_ref[layer] = jnp.broadcast_to(jnp.concatenate([column, column], axis=0), (2 * half, 128))
    wide = lax.broadcasted_iota(jnp.int32, (2 * half, 2 * half), 0) == lax.broadcasted_iota(jnp.int32, (2 * half, 2 * half), 1)
    for part in range(2):
        row = jnp.broadcast_to(inject_ref[pl.ds(part, 1), :], (2 * half, 2 * half))
        column = jnp.broadcast_to(jnp.sum(jnp.where(wide, row, 0.0), axis=1, keepdims=True), (2 * half, 128))
        added_ref[part] = jnp.concatenate(
            [column[:half], column[:half], column[half:], column[half:]], axis=0
        )


def couple(recv_ref, state_ref, weight_ref, mixer_ref, bias_ref, inject_ref, new_ref, grad_ref, wide_ref, a_ref, b_ref):
    channels, spots, rows, cols = new_ref.shape
    tall = rows + 2 * REACH
    half = channels // 2
    block = spots * half
    total = 2 * spots * tall
    owners = recv_ref.shape[0] // total
    grad = recv_ref[0:total, :].astype(F32)
    for owner in range(1, owners):
        grad = grad + recv_ref[pl.ds(owner * total, total), :].astype(F32)
    for part in range(2):
        for spot in range(spots):
            row = (part * spots + spot) * tall
            grad_ref[part, spot] = grad[row : row + rows, :cols]
    space, coil = lax.axis_index("space"), lax.axis_index("coil")
    lane = lax.broadcasted_iota(jnp.int32, (1, 128), 1)
    col_id = coil * cols + jnp.where(lane < 112, lane, lane - 128)
    col_keep = ((col_id >= 0) & (col_id < cols * owners)).astype(F32)
    upper = jnp.where(space > 0, col_keep, 0.0)
    lower = jnp.where(space < lax.axis_size("space") - 1, col_keep, 0.0)

    def keep(i):
        return upper if i < REACH else lower if i >= REACH + rows else col_keep

    scale = [inject_ref[part] for part in range(2)]
    for i in range(tall):
        source = (i - REACH) % tall
        here = [
            jnp.concatenate(
                [
                    jnp.broadcast_to(grad[at : at + 1, :], (half, 128))
                    for at in ((part * spots + spot) * tall + source for spot in range(spots))
                ],
                axis=0,
            )
            for part in range(2)
        ]
        for which, ref in enumerate((a_ref, b_ref)):
            at = slice(which * block, (which + 1) * block)
            value = state_ref[pl.ds((2 * i + which) * block, block), :].astype(F32)
            value = value + (scale[0][at] * here[0] + scale[1][at] * here[1])
            ref[pl.ds(i * block, block), :] = (value * keep(i)).astype(BF16)
    for layer in range(weight_ref.shape[0]):
        source_ref, target_ref = (a_ref, b_ref) if layer % 2 == 0 else (b_ref, a_ref)
        weight = weight_ref[layer]
        mixer = mixer_ref[layer]
        bias = bias_ref[layer]
        first, last = 1 + layer, tall - 1 - layer
        for start in range(first, last, BATCH):
            lines = range(start, min(start + BATCH, last))
            cells = jnp.concatenate([source_ref[pl.ds((i - 1) * block, 3 * block), :] for i in lines], axis=1)
            taps = nn(weight, cells)
            raw = []
            for j in range(len(lines)):
                at = slice(128 * j, 128 * j + 128)
                value = pltpu.roll(taps[0:block, at], 1, 1) + taps[block : 2 * block, at]
                value = value + pltpu.roll(taps[2 * block :, at], 127, 1)
                raw.append(jnp.maximum(value + bias, 0.0).astype(BF16))
            mixed = nn(mixer, jnp.concatenate(raw, axis=1))
            for j, i in enumerate(lines):
                here = pl.ds(i * block, block)
                value = target_ref[here, :].astype(F32) + mixed[:, 128 * j : 128 * j + 128]
                target_ref[here, :] = (value * keep(i)).astype(BF16)
    for i in range(REACH, REACH + rows):
        source = i - REACH
        wide_ref[pl.ds(source, block, stride=rows), :] = a_ref[pl.ds(i * block, block), :].astype(F32)
        wide_ref[pl.ds(block * rows + source, block, stride=rows), :] = b_ref[pl.ds(i * block, block), :].astype(F32)
    for channel in range(channels):
        for spot in range(spots):
            at = (channel // half * block + spot * half + channel % half) * rows
            new_ref[channel, spot] = wide_ref[pl.ds(at, rows), :][:, :cols].astype(BF16)


def passed_on(tail, head, axis):
    ends = lax.axis_size(axis) - 1
    before = lax.ppermute(tail, axis, [(i, i + 1) for i in range(ends)])
    after = lax.ppermute(head, axis, [(i + 1, i) for i in range(ends)])
    return before, after


def per_device(state, sens, kdata, mask, inject, kernels, biases, mixers):
    channels, spots, rows, cols = state.shape
    coils = sens.shape[1]
    npar = sens.shape[4]
    npe = kdata.shape[4]
    lines = kdata.shape[3]
    groups = lax.axis_size("space")
    owners = lax.axis_size("coil")
    tall = rows + 2 * REACH
    cells = coils * spots * rows
    layers = kernels.shape[0]
    block = channels // 2 * spots

    estimate = jnp.pad(state[0:2], ((0, 0), (0, 0), (0, 0), (0, 128 - cols)))
    estimate = jnp.broadcast_to(estimate[None], (owners, *estimate.shape))
    estimate = lax.all_to_all(estimate, "coil", 0, 0, tiled=True)

    edge_columns = [
        (rows * d + r) % npe for d in range(groups) for r in (*range(rows, rows + REACH), *range(-REACH, 0))
    ]
    pe_columns = [*range(npe), *edge_columns]
    def tables(length, columns):
        out = pltpu.HBM((length, len(columns)), BF16)
        factors = jnp.asarray(dft_factors(length, columns, FINE))
        return [in_hbm(table) for table in call(dft_tables, [out, out], [], "dft_tables", plain(factors))]

    def table_scratch(length, columns, blocks):
        return [((length, columns), BF16)] * 2 + [pltpu.SemaphoreType.DMA((2 * blocks,))]

    par_tables = tables(npar, range(npar))
    pe_tables = tables(npe, pe_columns)

    (sent,) = call(
        forward_columns,
        [jax.ShapeDtypeStruct((npar, 2 * cells), BF16)],
        [((2 * cells, npar), BF16), *table_scratch(npar, npar, 1)],
        "forward_columns",
        estimate, sens, *par_tables,
    )
    spectra = lax.all_to_all(sent, "space", 0, 0, tiled=True)

    depth = 2 * coils * spots * REACH * (npar // 128) + channels * spots * REACH
    tail, head = call(pack_rows, [((depth, 128), BF16)] * 2, [], "pack_rows", state, plain(sens))
    above, below = passed_on(tail, head, "space")

    (sent,) = call(
        consistency,
        [jax.ShapeDtypeStruct((npar, 384), BF16)],
        [((8 * lines, npe), BF16)] * 2 + table_scratch(npe, len(pe_columns), len(pe_columns) // 256),
        "consistency",
        spectra, kdata, mask, *pe_tables,
    )
    sent, above, below = lax.optimization_barrier((sent, above, below))
    returned = lax.all_to_all(sent, "space", 0, 0, tiled=True)

    packed = [((channels * spots * REACH // 128 * tall, 128), BF16)] * 2
    tail, head = call(pack_cols, packed, [], "pack_cols", state, above, below)
    left, right = passed_on(tail, head, "coil")

    (sent,) = call(
        backward_columns,
        [jax.ShapeDtypeStruct((owners * 2 * spots * tall, 128), BF16)],
        [
            ((2 * spots * tall, npar), F32),
            ((2, coils, spots, 2 * REACH, npar), F32),
            *table_scratch(npar, npar, npar // 256),
        ],
        "backward_columns",
        returned, sens, above, below, *par_tables,
    )
    sent, left, right = lax.optimization_barrier((sent, left, right))
    shares = lax.all_to_all(sent, "coil", 0, 0, tiled=True)

    (spread,) = call(
        spread_state,
        [((tall * channels * spots, 128), BF16)],
        [((channels * spots * tall, 128), F32)],
        "spread_state",
        state, above, below, left, right,
    )

    weight, mixer, bias, added = call(
        coupling_weights,
        [
            ((layers, 3 * block, 3 * block), BF16),
            ((layers, block, block), BF16),
            ((layers, block, 128), F32),
            ((2, 2 * block, 128), F32),
        ],
        [],
        "coupling_weights",
        plain(kernels), plain(biases), plain(mixers), plain(inject.T),
    )
    new_state, gradient = call(
        couple,
        [jax.ShapeDtypeStruct(state.shape, BF16), jax.ShapeDtypeStruct((2, spots, rows, cols), F32)],
        [((2 * block * rows, 128), F32), ((block * tall, 128), BF16), ((block * tall, 128), BF16)],
        "couple",
        shares, spread, weight, mixer, bias, added,
    )
    return (new_state, gradient)


def solution(mesh):
    return jax.shard_map(
        per_device,
        mesh=mesh,
        in_specs=(
            P(None, None, "space", "coil"),
            P(None, "coil", None, "space", None),
            P(None, "coil", None, "space", None),
            P("space", None),
            P(),
            P(),
            P(),
            P(),
        ),
        out_specs=(P(None, None, "space", "coil"), P(None, None, "space", "coil")),
        check_vma=False,
    )
```

time: 142 us -> 112 us (0.79)
  the two profiles are of different devices: /device:TPU:25 before, /device:TPU:1 now
where the time goes in v1:
time: 112 us; the launch traced here: 111 us
  starting transfers between devices  50.9 us (45%)
  waiting for transfers between devices  27.9 us (25%)
  Pallas kernels  26.4 us (24%)
  local copies, waits for them, and re-layouts  5.3 us (5%)
    pallas_call x10, Pallas kernels, call(): pl.pallas_call(body, out_shape=shapes, in_specs=specs, out_specs=[VMEM] *...  26.4 us
    all_to_all x1, waiting for transfers between devices, per_device(): returned = lax.all_to_all(sent, 'space', 0, 0, tiled=True)  12.2 us
    ppermute x2, starting transfers between devices, passed_on(): before = lax.ppermute(tail, axis, [(i, i + 1) for i in range(ends)])  11.2 us
    all_to_all x1, starting transfers between devices, per_device(): spectra = lax.all_to_all(sent, 'space', 0, 0, tiled=True)  11.1 us
    all_to_all x1, starting transfers between devices, per_device(): returned = lax.all_to_all(sent, 'space', 0, 0, tiled=True)  11 us
    all_to_all x1, waiting for transfers between devices, per_device(): shares = lax.all_to_all(sent, 'coil', 0, 0, tiled=True)  8.43 us
    all_to_all x1, starting transfers between devices, per_device(): estimate = lax.all_to_all(estimate, 'coil', 0, 0, tiled=True)  7.52 us
    all_to_all x1, starting transfers between devices, per_device(): shares = lax.all_to_all(sent, 'coil', 0, 0, tiled=True)  6.87 us
  transfers between devices with their start and end apart: 8, of which 4 were waited for; matrix products, arithmetic and copies ran while one was open for 0% of the time, Pallas kernels for 16%

profile of v1, /device:TPU:1, one launch (start us, length us, event | category | flops | bytes accessed | tf_op | source)
XLA Modules:
  0.0 111.3 jit_solution(17907250687372647855)
XLA Ops:
  0.6 0.8 slice.3
  1.4 0.8 broadcast_in_dim.2
  2.2 0.0 copy-start.1
  2.2 7.5 %all-to-all-start = ((bf16[8,2,2,32,128]{4,3,2,1,0:T(8,128)(2,1)}), bf16[8,2,2,32,128]{4,3,2,1,0:T(8,128)(2,1)S(1)}, u32[]{:S(2)}, u32[]{:S(2)}) async-start(bf16[8,2,2,32,128]{4,3,2,1,0:T(8,128)(2,1)} %broadcast_in_dim.2), calls=%async_computation | async-start | bytes 524288 | tf_op jit(solution)/shard_map/all_to_all | solution.py:473
  9.7 0.0 copy-start.5
  9.7 1.0 copy-done.5
  10.7 2.0 %dft_tables.2 = (bf16[768,768]{1,0:T(8,128)(2,1)}, bf16[768,768]{1,0:T(8,128)(2,1)}) custom-call(f32[112,768]{1,0:T(8,128)S(1)} %copy-done.5), custom_call_target="tpu_custom_call" | custom-call | tf_op jit(solution)/shard_map/dft_tables/pallas_call | solution.py:29
  12.7 5.7 %all-to-all-done.est_ref = bf16[8,2,2,32,128]{4,3,2,1,0:T(8,128)(2,1)S(1)} async-done(((bf16[8,2,2,32,128]{4,3,2,1,0:T(8,128)(2,1)}), bf16[8,2,2,32,128]{4,3,2,1,0:T(8,128)(2,1)S(1)}, u32[]{:S(2)}, u32[]{:S(2)}) %all-to-all-start) | async-done | bytes 262176 | tf_op jit(solution)/shard_map/all_to_all | solution.py:473
  18.4 0.0 copy-start
  18.4 1.1 %copy-done = f32[2,2,2,32,768]{4,3,2,1,0:T(8,128)S(1)} copy-done((f32[2,2,2,32,768]{4,3,2,1,0:T(8,128)S(1)}, f32[2,2,2,32,768]{4,3,2,1,0:T(8,128)}, u32[]{:S(2)}) %copy-start) | copy-done | bytes 786456
  19.5 0.0 copy-start.3
  19.5 0.0 copy-start.6
  19.5 3.4 %forward_columns.1 = bf16[768,256]{1,0:T(8,128)(2,1)} custom-call(bf16[8,2,2,32,128]{4,3,2,1,0:T(8,128)(2,1)S(1)} %all-to-all-done.est_ref, f32[2,2,2,32,768]{4,3,2,1,0:T(8,128)S(1)} %copy-done, bf16[768,768]{1,0:T(8,128)(2,1)} %get-tuple-element.20.cos_hbm, bf16[768,768]{1,0:T(8,128)(2,1)} %get-tuple-element.21.sin_hbm), custom_call_target="tpu_custom_call" | custom-call | tf_op jit(solution)/shard_map/forward_columns/pallas_call | solution.py:29
  22.9 11.1 %all-to-all-start.1 = ((bf16[32,24,256]{2,1,0:T(8,128)(2,1)}), bf16[32,24,256]{2,1,0:T(8,128)(2,1)S(1)}, u32[]{:S(2)}, u32[]{:S(2)}) async-start(bf16[32,24,256]{2,1,0:T(8,128)(2,1)} %bitcast), calls=%async_computation.1 | async-start | bytes 786432 | tf_op jit(solution)/shard_map/all_to_all | solution.py:497
  34.0 0.0 copy-done.1
  34.0 0.0 copy-done.2
  34.0 0.1 pack_rows.1
  34.1 7.0 %collective-permute-start = (bf16[448,128]{1,0:T(8,128)(2,1)S(1)}, bf16[448,128]{1,0:T(8,128)(2,1)S(1)}, u32[]{:S(2)}, u32[]{:S(2)}) collective-permute-start(bf16[448,128]{1,0:T(8,128)(2,1)S(1)} %get-tuple-element.24), channel_id=1, source_target_pairs={{0,8},{8,16},{16,24},{24,32},{32,40},{40,48},{48,56},{56,64},{64,7... | collective-permute-start | bytes 344072 | tf_op jit(solution)/shard_map/ppermute | solution.py:453
  41.2 1.3 %collective-permute-start.1 = (bf16[448,128]{1,0:T(8,128)(2,1)S(1)}, bf16[448,128]{1,0:T(8,128)(2,1)S(1)}, u32[]{:S(2)}, u32[]{:S(2)}) collective-permute-start(bf16[448,128]{1,0:T(8,128)(2,1)S(1)} %get-tuple-element.25), channel_id=1, source_target_pairs={{8,0},{16,8},{24,16},{32,24},{40,32},{48,40},{56,48},{64,56},{72,6... | collective-permute-start | bytes 344072 | tf_op jit(solution)/shard_map/ppermute | solution.py:454
  42.5 0.0 copy-start.4
  42.5 1.1 copy-done.4
  43.5 3.7 %dft_tables.3 = (bf16[1024,1280]{1,0:T(8,128)(2,1)}, bf16[1024,1280]{1,0:T(8,128)(2,1)}) custom-call(f32[128,1280]{1,0:T(8,128)S(1)} %copy-done.4), custom_call_target="tpu_custom_call" | custom-call | tf_op jit(solution)/shard_map/dft_tables/pallas_call | solution.py:29
  47.2 1.5 %all-to-all-done.1 = bf16[32,24,256]{2,1,0:T(8,128)(2,1)S(1)} async-done(((bf16[32,24,256]{2,1,0:T(8,128)(2,1)}), bf16[32,24,256]{2,1,0:T(8,128)(2,1)S(1)}, u32[]{:S(2)}, u32[]{:S(2)}) %all-to-all-start.1) | async-done | bytes 393248 | tf_op jit(solution)/shard_map/all_to_all | solution.py:497
  48.8 0.0 copy-done.3
  48.8 0.0 copy-done.6
  48.8 6.7 %consistency.1 = bf16[768,384]{1,0:T(8,128)(2,1)} custom-call(bf16[768,256]{1,0:T(8,128)(2,1)S(1)} %bitcast.8, f32[2,2,2,24,1024]{4,3,2,1,0:T(8,128)S(1)} %copy-done.3, s32[24,1024]{1,0:T(8,128)S(1)} %copy-done.6, bf16[1024,1280]{1,0:T(8,128)(2,1)} %get-tuple-element.22.cos_hbm, bf16[1024,1280]{1,0:T(8,128)(2,1)} %get-tuple-element.23.sin_hbm), custom_call_target="tpu_custom_call" | custom-call | tf_op jit(solution)/shard_map/consistency/pallas_call | solution.py:29
  55.5 0.0 collective-permute-done.above_ref
  55.5 0.0 collective-permute-done.1.below_ref
  55.5 11.0 %all-to-all-start.2 = ((bf16[32,24,384]{2,1,0:T(8,128)(2,1)}), bf16[32,24,384]{2,1,0:T(8,128)(2,1)S(1)}, u32[]{:S(2)}, u32[]{:S(2)}) async-start(bf16[32,24,384]{2,1,0:T(8,128)(2,1)} %bitcast.2), calls=%async_computation.2 | async-start | bytes 1179648 | tf_op jit(solution)/shard_map/all_to_all | solution.py:511
  66.5 0.4 pack_cols.1
  66.9 0.0 copy-start.10
  66.9 4.2 %collective-permute-start.2 = (bf16[80,128]{1,0:T(8,128)(2,1)S(1)}, bf16[80,128]{1,0:T(8,128)(2,1)S(1)}, u32[]{:S(2)}, u32[]{:S(2)}) collective-permute-start(bf16[80,128]{1,0:T(8,128)(2,1)S(1)} %get-tuple-element.29), channel_id=1, source_target_pairs={{0,1},{1,2},{2,3},{3,4},{4,5},{5,6},{6,7},{8,9},{9,10},{10,11},{11... | collective-permute-start | bytes 61448 | tf_op jit(solution)/shard_map/ppermute | solution.py:453
  71.1 1.9 %collective-permute-start.3 = (bf16[80,128]{1,0:T(8,128)(2,1)S(1)}, bf16[80,128]{1,0:T(8,128)(2,1)S(1)}, u32[]{:S(2)}, u32[]{:S(2)}) collective-permute-start(bf16[80,128]{1,0:T(8,128)(2,1)S(1)} %get-tuple-element.30), channel_id=1, source_target_pairs={{1,0},{2,1},{3,2},{4,3},{5,4},{6,5},{7,6},{9,8},{10,9},{11,10},{12... | collective-permute-start | bytes 61448 | tf_op jit(solution)/shard_map/ppermute | solution.py:454
  73.0 12.2 %all-to-all-done.2 = bf16[32,24,384]{2,1,0:T(8,128)(2,1)S(1)} async-done(((bf16[32,24,384]{2,1,0:T(8,128)(2,1)}), bf16[32,24,384]{2,1,0:T(8,128)(2,1)S(1)}, u32[]{:S(2)}, u32[]{:S(2)}) %all-to-all-start.2) | async-done | bytes 589856 | tf_op jit(solution)/shard_map/all_to_all | solution.py:511
  85.2 0.0 copy-start.7
  85.2 3.9 %backward_columns.1 = bf16[1280,128]{1,0:T(8,128)(2,1)} custom-call(bf16[768,384]{1,0:T(8,128)(2,1)S(1)} %bitcast.7, f32[2,2,2,32,768]{4,3,2,1,0:T(8,128)S(1)} %copy-done.1, bf16[448,128]{1,0:T(8,128)(2,1)S(1)} %collective-permute-done.above_ref, bf16[448,128]{1,0:T(8,128)(2,1)S(1)} %collective-permute-done.1.below_ref, ...), custom_call_target="tpu_custom_call" | custom-call | tf_op jit(solution)/shard_map/backward_columns/pallas_call | solution.py:29
  89.1 0.0 collective-permute-done.2.left_ref
  89.1 0.0 collective-permute-done.3.right_ref
  89.2 6.9 %all-to-all-start.3 = ((bf16[8,160,128]{2,1,0:T(8,128)(2,1)}), bf16[8,160,128]{2,1,0:T(8,128)(2,1)S(1)}, u32[]{:S(2)}, u32[]{:S(2)}) async-start(bf16[8,160,128]{2,1,0:T(8,128)(2,1)} %bitcast.4), calls=%async_computation.3 | async-start | bytes 655360 | tf_op jit(solution)/shard_map/all_to_all | solution.py:529
  96.0 0.0 copy-done.10
  96.0 0.5 copy.12.kernels_ref
  96.6 0.0 copy-done.7
  96.6 0.0 copy-done.8
  96.6 0.0 copy-done.9
  96.6 0.4 coupling_weights.1
  97.0 0.6 spread_state.1.state_ref
  97.6 8.4 %all-to-all-done.3 = bf16[8,160,128]{2,1,0:T(8,128)(2,1)S(1)} async-done(((bf16[8,160,128]{2,1,0:T(8,128)(2,1)}), bf16[8,160,128]{2,1,0:T(8,128)(2,1)S(1)}, u32[]{:S(2)}, u32[]{:S(2)}) %all-to-all-start.3) | async-done | bytes 327712 | tf_op jit(solution)/shard_map/all_to_all | solution.py:529
  106.0 5.3 %couple.1 = (bf16[32,2,32,96]{3,2,1,0:T(8,128)(2,1)}, f32[2,2,32,96]{3,2,1,0:T(8,128)}) custom-call(bf16[1280,128]{1,0:T(8,128)(2,1)S(1)} %bitcast.9, bf16[2560,128]{1,0:T(8,128)(2,1)S(1)} %spread_state.1.state_ref, bf16[4,96,96]{2,1,0:T(8,128)(2,1)S(1)} %get-tuple-element.34.weight_ref, bf16[4,32,32]{2,1,0:T(8,128)(2,1)S(1)} %get-tuple-element.35.mixer_ref, ...), custom_call_target="tpu_custom_call" | custom-call | tf_op jit(solution)/shard_map/couple/pallas_call | solution.py:29
  (4 shorter events, 0.0 us)
Async XLA Ops:
  2.2 31.8 %copy-start.1 = (f32[2,2,2,32,768]{4,3,2,1,0:T(8,128)S(1)}, f32[2,2,2,32,768]{4,3,2,1,0:T(8,128)}, u32[]{:S(2)}) copy-start(f32[2,2,2,32,768]{4,3,2,1,0:T(8,128)} %sens_ref.5) | copy-start | bytes 2359300
  2.2 16.2 %all-to-all-start = ((bf16[8,2,2,32,128]{4,3,2,1,0:T(8,128)(2,1)}), bf16[8,2,2,32,128]{4,3,2,1,0:T(8,128)(2,1)S(1)}, u32[]{:S(2)}, u32[]{:S(2)}) async-start(bf16[8,2,2,32,128]{4,3,2,1,0:T(8,128)(2,1)} %broadcast_in_dim.2), calls=%async_computation | async-start | bytes 524288 | tf_op jit(solution)/shard_map/all_to_all | solution.py:473
  9.7 1.0 copy-start.5
  18.4 1.1 %copy-start = (f32[2,2,2,32,768]{4,3,2,1,0:T(8,128)S(1)}, f32[2,2,2,32,768]{4,3,2,1,0:T(8,128)}, u32[]{:S(2)}) copy-start(f32[2,2,2,32,768]{4,3,2,1,0:T(8,128)} %sens_ref.5) | copy-start | bytes 2359300
  19.5 14.5 %copy-start.2 = (bf16[32,2,32,96]{3,2,1,0:T(8,128)(2,1)S(1)}, bf16[32,2,32,96]{3,2,1,0:T(8,128)(2,1)}, u32[]{:S(2)}) copy-start(bf16[32,2,32,96]{3,2,1,0:T(8,128)(2,1)} %state_ref.5) | copy-start | bytes 1179652
  19.5 29.3 %copy-start.3 = (f32[2,2,2,24,1024]{4,3,2,1,0:T(8,128)S(1)}, f32[2,2,2,24,1024]{4,3,2,1,0:T(8,128)}, u32[]{:S(2)}) copy-start(f32[2,2,2,24,1024]{4,3,2,1,0:T(8,128)} %kdata_ref.1) | copy-start | bytes 2359300
  19.5 29.3 %copy-start.6 = (s32[24,1024]{1,0:T(8,128)S(1)}, s32[24,1024]{1,0:T(8,128)}, u32[]{:S(2)}) copy-start(s32[24,1024]{1,0:T(8,128)} %mask_ref.1) | copy-start | bytes 294916
  22.9 25.9 %all-to-all-start.1 = ((bf16[32,24,256]{2,1,0:T(8,128)(2,1)}), bf16[32,24,256]{2,1,0:T(8,128)(2,1)S(1)}, u32[]{:S(2)}, u32[]{:S(2)}) async-start(bf16[32,24,256]{2,1,0:T(8,128)(2,1)} %bitcast), calls=%async_computation.1 | async-start | bytes 786432 | tf_op jit(solution)/shard_map/all_to_all | solution.py:497
  34.1 21.4 %collective-permute-start = (bf16[448,128]{1,0:T(8,128)(2,1)S(1)}, bf16[448,128]{1,0:T(8,128)(2,1)S(1)}, u32[]{:S(2)}, u32[]{:S(2)}) collective-permute-start(bf16[448,128]{1,0:T(8,128)(2,1)S(1)} %get-tuple-element.24), channel_id=1, source_target_pairs={{0,8},{8,16},{16,24},{24,32},{32,40},{40,48},{48,56},{56,64},{64,7... | collective-permute-start | bytes 344072 | tf_op jit(solution)/shard_map/ppermute | solution.py:453
  41.2 14.4 %collective-permute-start.1 = (bf16[448,128]{1,0:T(8,128)(2,1)S(1)}, bf16[448,128]{1,0:T(8,128)(2,1)S(1)}, u32[]{:S(2)}, u32[]{:S(2)}) collective-permute-start(bf16[448,128]{1,0:T(8,128)(2,1)S(1)} %get-tuple-element.25), channel_id=1, source_target_pairs={{8,0},{16,8},{24,16},{32,24},{40,32},{48,40},{56,48},{64,56},{72,6... | collective-permute-start | bytes 344072 | tf_op jit(solution)/shard_map/ppermute | solution.py:454
  42.5 1.1 copy-start.4
  55.5 29.7 %all-to-all-start.2 = ((bf16[32,24,384]{2,1,0:T(8,128)(2,1)}), bf16[32,24,384]{2,1,0:T(8,128)(2,1)S(1)}, u32[]{:S(2)}, u32[]{:S(2)}) async-start(bf16[32,24,384]{2,1,0:T(8,128)(2,1)} %bitcast.2), calls=%async_computation.2 | async-start | bytes 1179648 | tf_op jit(solution)/shard_map/all_to_all | solution.py:511
  66.9 29.1 %copy-start.10 = (bf16[4,27,16,16]{1,3,2,0:T(8,128)(2,1)S(1)}, bf16[4,27,16,16]{1,3,2,0:T(8,128)(2,1)}, u32[]{:S(2)}) copy-start(bf16[4,27,16,16]{1,3,2,0:T(8,128)(2,1)} %param.15) | copy-start | bytes 165892
  66.9 22.2 %collective-permute-start.2 = (bf16[80,128]{1,0:T(8,128)(2,1)S(1)}, bf16[80,128]{1,0:T(8,128)(2,1)S(1)}, u32[]{:S(2)}, u32[]{:S(2)}) collective-permute-start(bf16[80,128]{1,0:T(8,128)(2,1)S(1)} %get-tuple-element.29), channel_id=1, source_target_pairs={{0,1},{1,2},{2,3},{3,4},{4,5},{5,6},{6,7},{8,9},{9,10},{10,11},{11... | collective-permute-start | bytes 61448 | tf_op jit(solution)/shard_map/ppermute | solution.py:453
  71.1 18.1 %collective-permute-start.3 = (bf16[80,128]{1,0:T(8,128)(2,1)S(1)}, bf16[80,128]{1,0:T(8,128)(2,1)S(1)}, u32[]{:S(2)}, u32[]{:S(2)}) collective-permute-start(bf16[80,128]{1,0:T(8,128)(2,1)S(1)} %get-tuple-element.30), channel_id=1, source_target_pairs={{1,0},{2,1},{3,2},{4,3},{5,4},{6,5},{7,6},{9,8},{10,9},{11,10},{12... | collective-permute-start | bytes 61448 | tf_op jit(solution)/shard_map/ppermute | solution.py:454
  85.2 11.3 %copy-start.7 = (bf16[4,16,16]{2,1,0:T(8,128)(2,1)S(1)}, bf16[4,16,16]{2,1,0:T(8,128)(2,1)}, u32[]{:S(2)}) copy-start(bf16[4,16,16]{2,1,0:T(8,128)(2,1)} %mixers_ref.1) | copy-start | bytes 6148
  85.2 11.3 %copy-start.8 = (f32[4,16]{1,0:T(4,128)S(1)}, f32[4,16]{1,0:T(4,128)}, u32[]{:S(2)}) copy-start(f32[4,16]{1,0:T(4,128)} %biases_ref.1) | copy-start | bytes 772
  85.2 11.4 %copy-start.9 = (f32[32,2]{0,1:T(2,128)S(1)}, f32[32,2]{0,1:T(2,128)}, u32[]{:S(2)}) copy-start(f32[32,2]{0,1:T(2,128)} %param.14) | copy-start | bytes 772
  89.2 16.9 %all-to-all-start.3 = ((bf16[8,160,128]{2,1,0:T(8,128)(2,1)}), bf16[8,160,128]{2,1,0:T(8,128)(2,1)S(1)}, u32[]{:S(2)}, u32[]{:S(2)}) async-start(bf16[8,160,128]{2,1,0:T(8,128)(2,1)} %bitcast.4), calls=%async_computation.3 | async-start | bytes 655360 | tf_op jit(solution)/shard_map/all_to_all | solution.py:529

commit v2 on v1

--- a/solution.py
+++ b/solution.py
@@ -13,6 +13,7 @@
 FINE = 32
 BATCH = 12
 VMEM = pl.BlockSpec(memory_space=pltpu.VMEM)
+HBM = pl.BlockSpec(memory_space=pltpu.HBM)
 
 
 def call(body, outs, scratch, name, *args):
@@ -21,16 +22,15 @@
         where, value = arg if isinstance(arg, tuple) else ("vmem", arg)
         if where != "plain":
             value = pltpu.with_memory_space_constraint(value, pltpu.HBM if where == "hbm" else pltpu.VMEM)
-        specs.append(pl.BlockSpec(memory_space=pltpu.HBM) if where == "hbm" else VMEM)
+        specs.append(HBM if where == "hbm" else VMEM)
         values.append(value)
-    shapes = []
-    for out in outs:
-        shapes.append(pltpu.VMEM(*out) if isinstance(out, tuple) else out)
+    shapes = [pltpu.VMEM(*out) if isinstance(out, tuple) else out for out in outs]
+    placed = [VMEM if isinstance(out, (tuple, jax.ShapeDtypeStruct)) else HBM for out in outs]
     return pl.pallas_call(
         body,
         out_shape=shapes,
         in_specs=specs,
-        out_specs=[VMEM] * len(outs),
+        out_specs=placed,
         scratch_shapes=[each if not isinstance(each, tuple) else pltpu.VMEM(*each) for each in scratch],
         compiler_params=pltpu.CompilerParams(vmem_limit_bytes=20 * 2**20),
         name=name,
@@ -74,15 +74,23 @@
     return np.concatenate(parts).astype(np.float32)
 
 
-def dft_tables(factors_ref, cos_ref, sin_ref):
+def dft_tables(factors_ref, cos_hbm, sin_hbm, cos_ref, sin_ref, sems):
     count = cos_ref.shape[0] // FINE
     cos_b = factors_ref[pl.ds(2 * count, FINE), :]
     sin_b = factors_ref[pl.ds(2 * count + FINE, FINE), :]
+    copies = []
     for a in range(count):
         here = pl.ds(a * FINE, FINE)
         cos, sin = factors_ref[pl.ds(a, 1), :], factors_ref[pl.ds(count + a, 1), :]
         cos_ref[here, :] = (cos * cos_b - sin * sin_b).astype(BF16)
         sin_ref[here, :] = (sin * cos_b + cos * sin_b).astype(BF16)
+        if a % 4 == 3:
+            done = pl.ds((a - 3) * FINE, 4 * FINE)
+            for source, target in ((cos_ref, cos_hbm), (sin_ref, sin_hbm)):
+                copy = pltpu.make_async_copy(source.at[done, :], target.at[done, :], sems.at[len(copies)])
+                copy.start()
+                copies.append(copy)
+    arrived(copies)
 
 
 def swap_groups(tiles, group):
@@ -270,7 +278,16 @@
         out_ref[pl.ds(owner * total, total), :] = value.astype(BF16)
 
 
-def pack_rows(state_ref, sens_ref, tail_ref, head_ref):
+def pack_rows(*refs):
+    count = (len(refs) - 3) // 2
+    tail_ref, head_ref, sems = refs[count], refs[count + 1], refs[-1]
+    copies = []
+    for k in range(count):
+        copy = pltpu.make_async_copy(refs[k], refs[count + 2 + k], sems.at[k])
+        copy.start()
+        copies.append(copy)
+    arrived(copies)
+    state_ref, sens_ref = refs[count + 2], refs[count + 3]
     channels, spots, rows, cols = state_ref.shape
     coils, npar = sens_ref.shape[1], sens_ref.shape[4]
     at = 0
@@ -476,13 +493,25 @@
         (rows * d + r) % npe for d in range(groups) for r in (*range(rows, rows + REACH), *range(-REACH, 0))
     ]
     pe_columns = [*range(npe), *edge_columns]
+    def table_scratch(length, columns, blocks):
+        return [((length, columns), BF16)] * 2 + [pltpu.SemaphoreType.DMA((2 * blocks,))]
+
     def tables(length, columns):
         out = pltpu.HBM((length, len(columns)), BF16)
         factors = jnp.asarray(dft_factors(length, columns, FINE))
-        return [in_hbm(table) for table in call(dft_tables, [out, out], [], "dft_tables", plain(factors))]
-
-    def table_scratch(length, columns, blocks):
-        return [((length, columns), BF16)] * 2 + [pltpu.SemaphoreType.DMA((2 * blocks,))]
+        scratch = table_scratch(length, len(columns), length // FINE // 4)
+        return [in_hbm(table) for table in call(dft_tables, [out, out], scratch, "dft_tables", plain(factors))]
+
+    depth = 2 * coils * spots * REACH * (npar // 128) + channels * spots * REACH
+    brought = [state, sens, jnp.asarray(dft_factors(npar, range(npar), FINE)), jnp.asarray(dft_factors(npe, pe_columns, FINE))]
+    tail, head, state, sens, par_factors, pe_factors = call(
+        pack_rows,
+        [((depth, 128), BF16)] * 2 + [(each.shape, each.dtype) for each in brought],
+        [pltpu.SemaphoreType.DMA((len(brought),))],
+        "pack_rows",
+        *[in_hbm(each) for each in brought],
+    )
+    above, below = passed_on(tail, head, "space")
 
     par_tables = tables(npar, range(npar))
     pe_tables = tables(npe, pe_columns)
@@ -494,11 +523,8 @@
         "forward_columns",
         estimate, sens, *par_tables,
     )
+    sent, above, below = lax.optimization_barrier((sent, above, below))
     spectra = lax.all_to_all(sent, "space", 0, 0, tiled=True)
-
-    depth = 2 * coils * spots * REACH * (npar // 128) + channels * spots * REACH
-    tail, head = call(pack_rows, [((depth, 128), BF16)] * 2, [], "pack_rows", state, plain(sens))
-    above, below = passed_on(tail, head, "space")
 
     (sent,) = call(
         consistency,
@@ -507,7 +533,6 @@
         "consistency",
         spectra, kdata, mask, *pe_tables,
     )
-    sent, above, below = lax.optimization_barrier((sent, above, below))
     returned = lax.all_to_all(sent, "space", 0, 0, tiled=True)
 
     packed = [((channels * spots * REACH // 128 * tall, 128), BF16)] * 2

time: 112 us -> 117 us (1.045)
  starting transfers between devices: 50.9 us -> 56.1 us
  local copies, waits for them, and re-layouts: 5.3 us -> 3.29 us
    all_to_all x1, waiting for transfers between devices: 1.55 us -> 11.3 us  [per_device(): spectra = lax.all_to_all(sent, 'space', 0, 0, tiled=True)]
    all_to_all x1, waiting for transfers between devices: 12.2 us -> 2.58 us  [per_device(): returned = lax.all_to_all(sent, 'space', 0, 0, tiled=True)]
    all_to_all x1, starting transfers between devices: 6.87 us -> 13.9 us  [per_device(): shares = lax.all_to_all(sent, 'coil', 0, 0, tiled=True)]
    all_to_all x1, starting transfers between devices: 11 us -> 3.91 us  [per_device(): returned = lax.all_to_all(sent, 'space', 0, 0, tiled=True)]
    ppermute x2, waiting for transfers between devices: 0.01 us -> 6.67 us  [passed_on(): after = lax.ppermute(head, axis, [(i + 1, i) for i in range(ends)])]
    all_to_all x1, waiting for transfers between devices: 5.69 us -> 0.01 us  [per_device(): estimate = lax.all_to_all(estimate, 'coil', 0, 0, tiled=True)]
    ppermute x2, starting transfers between devices: 11.2 us -> 15.5 us  [passed_on(): before = lax.ppermute(tail, axis, [(i, i + 1) for i in range(ends)])]
    unnamed x23 -> x17, local copies, waits for them, and re-layouts: 3.77 us -> 1.71 us
  transfers between devices with their start and end apart: 8 -> 8, of which waited for: 4 -> 4; matrix products, arithmetic and copies ran while one was open for 0% -> 0% of each run, Pallas kernels for 16% -> 13%
where the time goes in v2:
time: 117 us
  starting transfers between devices  56.1 us (48%)
  waiting for transfers between devices  29 us (25%)
  Pallas kernels  27.3 us (23%)
  local copies, waits for them, and re-layouts  3.29 us (3%)
    pallas_call x10, Pallas kernels, call(): pl.pallas_call(body, out_shape=shapes, in_specs=specs, out_specs=placed,...  27.3 us
    ppermute x2, starting transfers between devices, passed_on(): before = lax.ppermute(tail, axis, [(i, i + 1) for i in range(ends)])  15.5 us
    all_to_all x1, starting transfers between devices, per_device(): shares = lax.all_to_all(sent, 'coil', 0, 0, tiled=True)  13.9 us
    all_to_all x1, starting transfers between devices, per_device(): spectra = lax.all_to_all(sent, 'space', 0, 0, tiled=True)  12.3 us
    all_to_all x1, waiting for transfers between devices, per_device(): spectra = lax.all_to_all(sent, 'space', 0, 0, tiled=True)  11.3 us
    all_to_all x1, waiting for transfers between devices, per_device(): shares = lax.all_to_all(sent, 'coil', 0, 0, tiled=True)  8.43 us
    all_to_all x1, starting transfers between devices, per_device(): estimate = lax.all_to_all(estimate, 'coil', 0, 0, tiled=True)  7.39 us
    ppermute x2, waiting for transfers between devices, passed_on(): after = lax.ppermute(head, axis, [(i + 1, i) for i in range(ends)])  6.67 us
  transfers between devices with their start and end apart: 8, of which 4 were waited for; matrix products, arithmetic and copies ran while one was open for 0% of the time, Pallas kernels for 13%

profile of v2, /device:TPU:1, one launch (start us, length us, event | category | flops | bytes accessed | tf_op | source)
XLA Modules:
  0.0 116.6 jit_solution(12429310068159508751)
XLA Ops:
  0.6 0.0 copy-start.1
  0.6 0.8 slice.3
  1.5 0.8 broadcast_in_dim.2
  2.2 7.4 %all-to-all-start = ((bf16[8,2,2,32,128]{4,3,2,1,0:T(8,128)(2,1)}), bf16[8,2,2,32,128]{4,3,2,1,0:T(8,128)(2,1)S(1)}, u32[]{:S(2)}, u32[]{:S(2)}) async-start(bf16[8,2,2,32,128]{4,3,2,1,0:T(8,128)(2,1)} %broadcast_in_dim.2), calls=%async_computation | async-start | bytes 524288 | tf_op jit(solution)/shard_map/all_to_all | solution.py:490
  9.6 2.6 %pack_rows.1 = (bf16[448,128]{1,0:T(8,128)(2,1)S(1)}, bf16[448,128]{1,0:T(8,128)(2,1)S(1)}, bf16[32,2,32,96]{3,2,1,0:T(8,128)(2,1)S(1)}, f32[2,2,2,32,768]{4,3,2...) custom-call(bf16[32,2,32,96]{3,2,1,0:T(8,128)(2,1)} %refs_0_.1, f32[2,2,2,32,768]{4,3,2,1,0:T(8,128)} %refs_1_.1, ...), custom_call_target="tpu_custom_call" | custom-call | tf_op jit(solution)/shard_map/pack_rows/pallas_call | solution.py:29
  12.2 0.0 copy-start
  12.2 6.4 %collective-permute-start = (bf16[448,128]{1,0:T(8,128)(2,1)S(1)}, bf16[448,128]{1,0:T(8,128)(2,1)S(1)}, u32[]{:S(2)}, u32[]{:S(2)}) collective-permute-start(bf16[448,128]{1,0:T(8,128)(2,1)S(1)} %get-tuple-element.25), channel_id=1, source_target_pairs={{0,8},{8,16},{16,24},{24,32},{32,40},{40,48},{48,56},{56,64},{64,7... | collective-permute-start | bytes 344072 | tf_op jit(solution)/shard_map/ppermute | solution.py:470
  18.6 1.3 %collective-permute-start.1 = (bf16[448,128]{1,0:T(8,128)(2,1)S(1)}, bf16[448,128]{1,0:T(8,128)(2,1)S(1)}, u32[]{:S(2)}, u32[]{:S(2)}) collective-permute-start(bf16[448,128]{1,0:T(8,128)(2,1)S(1)} %get-tuple-element.26), channel_id=1, source_target_pairs={{8,0},{16,8},{24,16},{32,24},{40,32},{48,40},{56,48},{64,56},{72,6... | collective-permute-start | bytes 344072 | tf_op jit(solution)/shard_map/ppermute | solution.py:471
  19.9 0.0 copy-done.1
  19.9 1.6 %dft_tables.2 = (bf16[768,768]{1,0:T(8,128)(2,1)}, bf16[768,768]{1,0:T(8,128)(2,1)}) custom-call(f32[112,768]{1,0:T(8,128)S(1)} %copy-done.1), custom_call_target="tpu_custom_call" | custom-call | tf_op jit(solution)/shard_map/dft_tables/pallas_call | solution.py:29
  21.5 0.0 all-to-all-done.est_ref
  21.5 0.0 copy-start.3
  21.5 3.3 %forward_columns.1 = bf16[768,256]{1,0:T(8,128)(2,1)} custom-call(bf16[8,2,2,32,128]{4,3,2,1,0:T(8,128)(2,1)S(1)} %all-to-all-done.est_ref, f32[2,2,2,32,768]{4,3,2,1,0:T(8,128)S(1)} %get-tuple-element.22.sens_ref, bf16[768,768]{1,0:T(8,128)(2,1)} %get-tuple-element.23.cos_hbm, bf16[768,768]{1,0:T(8,128)(2,1)} %get-tuple-element.24.sin_hbm), custom_call_target="tpu_custom_call" | custom-call | tf_op jit(solution)/shard_map/forward_columns/pallas_call | solution.py:29
  24.8 0.0 collective-permute-done.above_ref
  24.8 6.7 %collective-permute-done.1.below_ref = bf16[448,128]{1,0:T(8,128)(2,1)S(1)} collective-permute-done((bf16[448,128]{1,0:T(8,128)(2,1)S(1)}, bf16[448,128]{1,0:T(8,128)(2,1)S(1)}, u32[]{:S(2)}, u32[]{:S(2)}) %collective-permute-start.1) | collective-permute-done | bytes 114720 | tf_op jit(solution)/shard_map/ppermute | solution.py:471
  31.5 12.3 %all-to-all-start.1 = ((bf16[32,24,256]{2,1,0:T(8,128)(2,1)}), bf16[32,24,256]{2,1,0:T(8,128)(2,1)S(1)}, u32[]{:S(2)}, u32[]{:S(2)}) async-start(bf16[32,24,256]{2,1,0:T(8,128)(2,1)} %bitcast), calls=%async_computation.1 | async-start | bytes 786432 | tf_op jit(solution)/shard_map/all_to_all | solution.py:527
  43.7 0.0 copy-done
  43.7 2.6 %dft_tables.3 = (bf16[1024,1280]{1,0:T(8,128)(2,1)}, bf16[1024,1280]{1,0:T(8,128)(2,1)}) custom-call(f32[128,1280]{1,0:T(8,128)S(1)} %copy-done), custom_call_target="tpu_custom_call" | custom-call | tf_op jit(solution)/shard_map/dft_tables/pallas_call | solution.py:29
  46.3 11.3 %all-to-all-done.1 = bf16[32,24,256]{2,1,0:T(8,128)(2,1)S(1)} async-done(((bf16[32,24,256]{2,1,0:T(8,128)(2,1)}), bf16[32,24,256]{2,1,0:T(8,128)(2,1)S(1)}, u32[]{:S(2)}, u32[]{:S(2)}) %all-to-all-start.1) | async-done | bytes 393248 | tf_op jit(solution)/shard_map/all_to_all | solution.py:527
  57.7 0.0 copy-done.3
  57.7 0.0 copy-start.2
  57.7 1.1 copy-done.2
  58.8 6.7 %consistency.1 = bf16[768,384]{1,0:T(8,128)(2,1)} custom-call(bf16[768,256]{1,0:T(8,128)(2,1)S(1)} %bitcast.8, f32[2,2,2,24,1024]{4,3,2,1,0:T(8,128)S(1)} %copy-done.2, s32[24,1024]{1,0:T(8,128)S(1)} %copy-done.3, bf16[1024,1280]{1,0:T(8,128)(2,1)} %get-tuple-element.28.cos_hbm, bf16[1024,1280]{1,0:T(8,128)(2,1)} %get-tuple-element.29.sin_hbm), custom_call_target="tpu_custom_call" | custom-call | tf_op jit(solution)/shard_map/consistency/pallas_call | solution.py:29
  65.5 3.9 %all-to-all-start.2 = ((bf16[32,24,384]{2,1,0:T(8,128)(2,1)}), bf16[32,24,384]{2,1,0:T(8,128)(2,1)S(1)}, u32[]{:S(2)}, u32[]{:S(2)}) async-start(bf16[32,24,384]{2,1,0:T(8,128)(2,1)} %bitcast.2), calls=%async_computation.2 | async-start | bytes 1179648 | tf_op jit(solution)/shard_map/all_to_all | solution.py:536
  69.5 0.4 pack_cols.1
  69.9 0.0 copy-start.7
  69.9 9.1 %collective-permute-start.2 = (bf16[80,128]{1,0:T(8,128)(2,1)S(1)}, bf16[80,128]{1,0:T(8,128)(2,1)S(1)}, u32[]{:S(2)}, u32[]{:S(2)}) collective-permute-start(bf16[80,128]{1,0:T(8,128)(2,1)S(1)} %get-tuple-element.33), channel_id=1, source_target_pairs={{0,1},{1,2},{2,3},{3,4},{4,5},{5,6},{6,7},{8,9},{9,10},{10,11},{11... | collective-permute-start | bytes 61448 | tf_op jit(solution)/shard_map/ppermute | solution.py:470
  79.0 1.9 %collective-permute-start.3 = (bf16[80,128]{1,0:T(8,128)(2,1)S(1)}, bf16[80,128]{1,0:T(8,128)(2,1)S(1)}, u32[]{:S(2)}, u32[]{:S(2)}) collective-permute-start(bf16[80,128]{1,0:T(8,128)(2,1)S(1)} %get-tuple-element.34), channel_id=1, source_target_pairs={{1,0},{2,1},{3,2},{4,3},{5,4},{6,5},{7,6},{9,8},{10,9},{11,10},{12... | collective-permute-start | bytes 61448 | tf_op jit(solution)/shard_map/ppermute | solution.py:471
  80.9 2.6 %all-to-all-done.2 = bf16[32,24,384]{2,1,0:T(8,128)(2,1)S(1)} async-done(((bf16[32,24,384]{2,1,0:T(8,128)(2,1)}), bf16[32,24,384]{2,1,0:T(8,128)(2,1)S(1)}, u32[]{:S(2)}, u32[]{:S(2)}) %all-to-all-start.2) | async-done | bytes 589856 | tf_op jit(solution)/shard_map/all_to_all | solution.py:536
  83.5 0.0 copy-start.4
  83.5 0.0 copy-start.5
  83.5 0.0 copy-start.6
  83.5 3.9 %backward_columns.1 = bf16[1280,128]{1,0:T(8,128)(2,1)} custom-call(bf16[768,384]{1,0:T(8,128)(2,1)S(1)} %bitcast.7, f32[2,2,2,32,768]{4,3,2,1,0:T(8,128)S(1)} %get-tuple-element.22.sens_ref, bf16[448,128]{1,0:T(8,128)(2,1)S(1)} %collective-permute-done.above_ref, bf16[448,128]{1,0:T(8,128)(2,1)S(1)} %collective-permute-done.1.below_ref, ...), custom_call_target="tpu_custom_call" | custom-call | tf_op jit(solution)/shard_map/backward_columns/pallas_call | solution.py:29
  87.4 0.0 collective-permute-done.2.left_ref
  87.4 0.0 collective-permute-done.3.right_ref
  87.4 13.9 %all-to-all-start.3 = ((bf16[8,160,128]{2,1,0:T(8,128)(2,1)}), bf16[8,160,128]{2,1,0:T(8,128)(2,1)S(1)}, u32[]{:S(2)}, u32[]{:S(2)}) async-start(bf16[8,160,128]{2,1,0:T(8,128)(2,1)} %bitcast.4), calls=%async_computation.3 | async-start | bytes 655360 | tf_op jit(solution)/shard_map/all_to_all | solution.py:554
  101.3 0.0 copy-done.7
  101.4 0.5 copy.14.kernels_ref
  101.9 0.0 copy-done.4
  101.9 0.0 copy-done.5
  101.9 0.0 copy-done.6
  101.9 0.4 coupling_weights.1
  102.3 0.6 spread_state.1.state_ref
  102.9 8.4 %all-to-all-done.3 = bf16[8,160,128]{2,1,0:T(8,128)(2,1)S(1)} async-done(((bf16[8,160,128]{2,1,0:T(8,128)(2,1)}), bf16[8,160,128]{2,1,0:T(8,128)(2,1)S(1)}, u32[]{:S(2)}, u32[]{:S(2)}) %all-to-all-start.3) | async-done | bytes 327712 | tf_op jit(solution)/shard_map/all_to_all | solution.py:554
  111.3 5.3 %couple.1 = (bf16[32,2,32,96]{3,2,1,0:T(8,128)(2,1)}, f32[2,2,32,96]{3,2,1,0:T(8,128)}) custom-call(bf16[1280,128]{1,0:T(8,128)(2,1)S(1)} %bitcast.9, bf16[2560,128]{1,0:T(8,128)(2,1)S(1)} %spread_state.1.state_ref, bf16[4,96,96]{2,1,0:T(8,128)(2,1)S(1)} %get-tuple-element.38.weight_ref, bf16[4,32,32]{2,1,0:T(8,128)(2,1)S(1)} %get-tuple-element.39.mixer_ref, ...), custom_call_target="tpu_custom_call" | custom-call | tf_op jit(solution)/shard_map/couple/pallas_call | solution.py:29
  (1 shorter events, 0.0 us)
Async XLA Ops:
  0.6 19.3 %copy-start.1 = (f32[112,768]{1,0:T(8,128)S(1)}, f32[112,768]{1,0:T(8,128)}, u32[]{:S(2)}) copy-start(f32[112,768]{1,0:T(8,128)} %constant.7.clone.refs_2_.factors_ref) | copy-start | bytes 1032196
  2.2 19.3 %all-to-all-start = ((bf16[8,2,2,32,128]{4,3,2,1,0:T(8,128)(2,1)}), bf16[8,2,2,32,128]{4,3,2,1,0:T(8,128)(2,1)S(1)}, u32[]{:S(2)}, u32[]{:S(2)}) async-start(bf16[8,2,2,32,128]{4,3,2,1,0:T(8,128)(2,1)} %broadcast_in_dim.2), calls=%async_computation | async-start | bytes 524288 | tf_op jit(solution)/shard_map/all_to_all | solution.py:490
  12.2 31.5 %copy-start = (f32[128,1280]{1,0:T(8,128)S(1)}, f32[128,1280]{1,0:T(8,128)}, u32[]{:S(2)}) copy-start(f32[128,1280]{1,0:T(8,128)} %constant.8.clone.refs_3_.factors_ref) | copy-start | bytes 1966084
  12.2 12.6 %collective-permute-start = (bf16[448,128]{1,0:T(8,128)(2,1)S(1)}, bf16[448,128]{1,0:T(8,128)(2,1)S(1)}, u32[]{:S(2)}, u32[]{:S(2)}) collective-permute-start(bf16[448,128]{1,0:T(8,128)(2,1)S(1)} %get-tuple-element.25), channel_id=1, source_target_pairs={{0,8},{8,16},{16,24},{24,32},{32,40},{40,48},{48,56},{56,64},{64,7... | collective-permute-start | bytes 344072 | tf_op jit(solution)/shard_map/ppermute | solution.py:470
  18.6 12.9 %collective-permute-start.1 = (bf16[448,128]{1,0:T(8,128)(2,1)S(1)}, bf16[448,128]{1,0:T(8,128)(2,1)S(1)}, u32[]{:S(2)}, u32[]{:S(2)}) collective-permute-start(bf16[448,128]{1,0:T(8,128)(2,1)S(1)} %get-tuple-element.26), channel_id=1, source_target_pairs={{8,0},{16,8},{24,16},{32,24},{40,32},{48,40},{56,48},{64,56},{72,6... | collective-permute-start | bytes 344072 | tf_op jit(solution)/shard_map/ppermute | solution.py:471
  21.5 36.2 %copy-start.3 = (s32[24,1024]{1,0:T(8,128)S(1)}, s32[24,1024]{1,0:T(8,128)}, u32[]{:S(2)}) copy-start(s32[24,1024]{1,0:T(8,128)} %mask_ref.1) | copy-start | bytes 294916
  31.5 26.2 %all-to-all-start.1 = ((bf16[32,24,256]{2,1,0:T(8,128)(2,1)}), bf16[32,24,256]{2,1,0:T(8,128)(2,1)S(1)}, u32[]{:S(2)}, u32[]{:S(2)}) async-start(bf16[32,24,256]{2,1,0:T(8,128)(2,1)} %bitcast), calls=%async_computation.1 | async-start | bytes 786432 | tf_op jit(solution)/shard_map/all_to_all | solution.py:527
  57.7 1.1 copy-start.2
  65.5 18.0 %all-to-all-start.2 = ((bf16[32,24,384]{2,1,0:T(8,128)(2,1)}), bf16[32,24,384]{2,1,0:T(8,128)(2,1)S(1)}, u32[]{:S(2)}, u32[]{:S(2)}) async-start(bf16[32,24,384]{2,1,0:T(8,128)(2,1)} %bitcast.2), calls=%async_computation.2 | async-start | bytes 1179648 | tf_op jit(solution)/shard_map/all_to_all | solution.py:536
  69.9 31.5 %copy-start.7 = (bf16[4,27,16,16]{1,3,2,0:T(8,128)(2,1)S(1)}, bf16[4,27,16,16]{1,3,2,0:T(8,128)(2,1)}, u32[]{:S(2)}) copy-start(bf16[4,27,16,16]{1,3,2,0:T(8,128)(2,1)} %param.17) | copy-start | bytes 165892
  69.9 17.5 %collective-permute-start.2 = (bf16[80,128]{1,0:T(8,128)(2,1)S(1)}, bf16[80,128]{1,0:T(8,128)(2,1)S(1)}, u32[]{:S(2)}, u32[]{:S(2)}) collective-permute-start(bf16[80,128]{1,0:T(8,128)(2,1)S(1)} %get-tuple-element.33), channel_id=1, source_target_pairs={{0,1},{1,2},{2,3},{3,4},{4,5},{5,6},{6,7},{8,9},{9,10},{10,11},{11... | collective-permute-start | bytes 61448 | tf_op jit(solution)/shard_map/ppermute | solution.py:470
  79.0 8.4 %collective-permute-start.3 = (bf16[80,128]{1,0:T(8,128)(2,1)S(1)}, bf16[80,128]{1,0:T(8,128)(2,1)S(1)}, u32[]{:S(2)}, u32[]{:S(2)}) collective-permute-start(bf16[80,128]{1,0:T(8,128)(2,1)S(1)} %get-tuple-element.34), channel_id=1, source_target_pairs={{1,0},{2,1},{3,2},{4,3},{5,4},{6,5},{7,6},{9,8},{10,9},{11,10},{12... | collective-permute-start | bytes 61448 | tf_op jit(solution)/shard_map/ppermute | solution.py:471
  83.5 18.4 %copy-start.4 = (bf16[4,16,16]{2,1,0:T(8,128)(2,1)S(1)}, bf16[4,16,16]{2,1,0:T(8,128)(2,1)}, u32[]{:S(2)}) copy-start(bf16[4,16,16]{2,1,0:T(8,128)(2,1)} %mixers_ref.1) | copy-start | bytes 6148
  83.5 18.4 %copy-start.5 = (f32[4,16]{1,0:T(4,128)S(1)}, f32[4,16]{1,0:T(4,128)}, u32[]{:S(2)}) copy-start(f32[4,16]{1,0:T(4,128)} %biases_ref.1) | copy-start | bytes 772
  83.5 18.4 %copy-start.6 = (f32[32,2]{0,1:T(2,128)S(1)}, f32[32,2]{0,1:T(2,128)}, u32[]{:S(2)}) copy-start(f32[32,2]{0,1:T(2,128)} %param.16) | copy-start | bytes 772
  87.4 23.9 %all-to-all-start.3 = ((bf16[8,160,128]{2,1,0:T(8,128)(2,1)}), bf16[8,160,128]{2,1,0:T(8,128)(2,1)S(1)}, u32[]{:S(2)}, u32[]{:S(2)}) async-start(bf16[8,160,128]{2,1,0:T(8,128)(2,1)} %bitcast.4), calls=%async_computation.3 | async-start | bytes 655360 | tf_op jit(solution)/shard_map/all_to_all | solution.py:554

commit v3 on v2

--- a/solution.py
+++ b/solution.py
@@ -74,7 +74,7 @@
     return np.concatenate(parts).astype(np.float32)
 
 
-def dft_tables(factors_ref, cos_hbm, sin_hbm, cos_ref, sin_ref, sems):
+def fill_tables(factors_ref, cos_hbm, sin_hbm, cos_ref, sin_ref, sems):
     count = cos_ref.shape[0] // FINE
     cos_b = factors_ref[pl.ds(2 * count, FINE), :]
     sin_b = factors_ref[pl.ds(2 * count + FINE, FINE), :]
@@ -90,7 +90,27 @@
                 copy = pltpu.make_async_copy(source.at[done, :], target.at[done, :], sems.at[len(copies)])
                 copy.start()
                 copies.append(copy)
-    arrived(copies)
+    return copies
+
+
+def prepare(
+    state_hbm, sens_hbm, par_hbm, pe_hbm,
+    tail_ref, head_ref, state_ref, sens_ref, par_cos_hbm, par_sin_hbm, pe_cos_hbm, pe_sin_hbm,
+    par_ref, pe_ref, par_cos, par_sin, pe_cos, pe_sin, sems, par_sems, pe_sems,
+):
+    pairs = ((par_hbm, par_ref), (pe_hbm, pe_ref), (state_hbm, state_ref), (sens_hbm, sens_ref))
+    copies = []
+    for k, (source, target) in enumerate(pairs):
+        copy = pltpu.make_async_copy(source, target, sems.at[k])
+        copy.start()
+        copies.append(copy)
+    arrived(copies[0:1])
+    sent = fill_tables(par_ref, par_cos_hbm, par_sin_hbm, par_cos, par_sin, par_sems)
+    arrived(copies[1:2])
+    sent = sent + fill_tables(pe_ref, pe_cos_hbm, pe_sin_hbm, pe_cos, pe_sin, pe_sems)
+    arrived(copies[2:])
+    pack_rows(state_ref, sens_ref, tail_ref, head_ref)
+    arrived(sent)
 
 
 def swap_groups(tiles, group):
@@ -278,16 +298,7 @@
         out_ref[pl.ds(owner * total, total), :] = value.astype(BF16)
 
 
-def pack_rows(*refs):
-    count = (len(refs) - 3) // 2
-    tail_ref, head_ref, sems = refs[count], refs[count + 1], refs[-1]
-    copies = []
-    for k in range(count):
-        copy = pltpu.make_async_copy(refs[k], refs[count + 2 + k], sems.at[k])
-        copy.start()
-        copies.append(copy)
-    arrived(copies)
-    state_ref, sens_ref = refs[count + 2], refs[count + 3]
+def pack_rows(state_ref, sens_ref, tail_ref, head_ref):
     channels, spots, rows, cols = state_ref.shape
     coils, npar = sens_ref.shape[1], sens_ref.shape[4]
     at = 0
@@ -465,11 +476,12 @@
             new_ref[channel, spot] = wide_ref[pl.ds(at, rows), :][:, :cols].astype(BF16)
 
 
-def passed_on(tail, head, axis):
-    ends = lax.axis_size(axis) - 1
-    before = lax.ppermute(tail, axis, [(i, i + 1) for i in range(ends)])
-    after = lax.ppermute(head, axis, [(i + 1, i) for i in range(ends)])
-    return before, after
+def from_previous(tail, axis):
+    return lax.ppermute(tail, axis, [(i, i + 1) for i in range(lax.axis_size(axis) - 1)])
+
+
+def from_next(head, axis):
+    return lax.ppermute(head, axis, [(i + 1, i) for i in range(lax.axis_size(axis) - 1)])
 
 
 def per_device(state, sens, kdata, mask, inject, kernels, biases, mixers):
@@ -503,18 +515,34 @@
         return [in_hbm(table) for table in call(dft_tables, [out, out], scratch, "dft_tables", plain(factors))]
 
     depth = 2 * coils * spots * REACH * (npar // 128) + channels * spots * REACH
-    brought = [state, sens, jnp.asarray(dft_factors(npar, range(npar), FINE)), jnp.asarray(dft_factors(npe, pe_columns, FINE))]
-    tail, head, state, sens, par_factors, pe_factors = call(
-        pack_rows,
-        [((depth, 128), BF16)] * 2 + [(each.shape, each.dtype) for each in brought],
-        [pltpu.SemaphoreType.DMA((len(brought),))],
-        "pack_rows",
-        *[in_hbm(each) for each in brought],
-    )
-    above, below = passed_on(tail, head, "space")
-
-    par_tables = tables(npar, range(npar))
-    pe_tables = tables(npe, pe_columns)
+    par_factors = jnp.asarray(dft_factors(npar, range(npar), FINE))
+    pe_factors = jnp.asarray(dft_factors(npe, pe_columns, FINE))
+
+    def table_scratch(length, columns, blocks):
+        return [((length, columns), BF16)] * 2 + [pltpu.SemaphoreType.DMA((2 * blocks,))]
+
+    par_scratch = table_scratch(npar, npar, npar // FINE // 4)
+    pe_scratch = table_scratch(npe, len(pe_columns), npe // FINE // 4)
+    tail, head, state, sens, *tables = call(
+        prepare,
+        [((depth, 128), BF16)] * 2
+        + [(state.shape, BF16), (sens.shape, F32)]
+        + [pltpu.HBM((npar, npar), BF16)] * 2
+        + [pltpu.HBM((npe, len(pe_columns)), BF16)] * 2,
+        [
+            (par_factors.shape, F32),
+            (pe_factors.shape, F32),
+            *par_scratch[:2],
+            *pe_scratch[:2],
+            pltpu.SemaphoreType.DMA((4,)),
+            par_scratch[2],
+            pe_scratch[2],
+        ],
+        "prepare",
+        in_hbm(state), in_hbm(sens), in_hbm(par_factors), in_hbm(pe_factors),
+    )
+    par_tables = [in_hbm(table) for table in tables[:2]]
+    pe_tables = [in_hbm(table) for table in tables[2:]]
 
     (sent,) = call(
         forward_columns,
@@ -523,8 +551,9 @@
         "forward_columns",
         estimate, sens, *par_tables,
     )
-    sent, above, below = lax.optimization_barrier((sent, above, below))
+    sent, tail = lax.optimization_barrier((sent, tail))
     spectra = lax.all_to_all(sent, "space", 0, 0, tiled=True)
+    above = from_previous(tail, "space")
 
     (sent,) = call(
         consistency,
@@ -533,11 +562,9 @@
         "consistency",
         spectra, kdata, mask, *pe_tables,
     )
+    sent, above, head = lax.optimization_barrier((sent, above, head))
     returned = lax.all_to_all(sent, "space", 0, 0, tiled=True)
-
-    packed = [((channels * spots * REACH // 128 * tall, 128), BF16)] * 2
-    tail, head = call(pack_cols, packed, [], "pack_cols", state, above, below)
-    left, right = passed_on(tail, head, "coil")
+    below = from_next(head, "space")
 
     (sent,) = call(
         backward_columns,
@@ -550,8 +577,12 @@
         "backward_columns",
         returned, sens, above, below, *par_tables,
     )
-    sent, left, right = lax.optimization_barrier((sent, left, right))
+    sent, above, below = lax.optimization_barrier((sent, above, below))
     shares = lax.all_to_all(sent, "coil", 0, 0, tiled=True)
+
+    packed = [((channels * spots * REACH // 128 * tall, 128), BF16)] * 2
+    tail, head = call(pack_cols, packed, [], "pack_cols", state, above, below)
+    left, right = from_previous(tail, "coil"), from_next(head, "coil")
 
     (spread,) = call(
         spread_state,

time: 117 us -> 108 us (0.923)
  starting transfers between devices: 56.1 us -> 49.7 us
  Pallas kernels: 27.3 us -> 24.9 us
  waiting for transfers between devices: 29 us -> 30.2 us
  local copies, waits for them, and re-layouts: 3.29 us -> 2.1 us
    ppermute x4, waiting for transfers between devices: 6.68 us -> 16.5 us  [the longest x2 16.5 us: from_next(): lax.ppermute(head, axis, [(i + 1, i) for i in range(lax.axis_size(axis) -...]
    all_to_all x1, waiting for transfers between devices: 8.43 us -> 0.31 us  [per_device(): shares = lax.all_to_all(sent, 'coil', 0, 0, tiled=True)]
    ppermute x4, starting transfers between devices: 18.7 us -> 14 us  [the longest x2 10.6 us: from_previous(): lax.ppermute(tail, axis, [(i, i + 1) for i in range(lax.axis_size(axis) -...]
    all_to_all x1, waiting for transfers between devices: 0.01 us -> 4.28 us  [per_device(): estimate = lax.all_to_all(estimate, 'coil', 0, 0, tiled=True)]
    all_to_all x1, waiting for transfers between devices: 11.3 us -> 7.69 us  [per_device(): spectra = lax.all_to_all(sent, 'space', 0, 0, tiled=True)]
    pallas_call x10 -> x8, Pallas kernels: 27.3 us -> 24.9 us  [call(): pl.pallas_call(body, out_shape=shapes, in_specs=specs, out_specs=placed,...]
    all_to_all x1, starting transfers between devices: 13.9 us -> 12.2 us  [per_device(): shares = lax.all_to_all(sent, 'coil', 0, 0, tiled=True)]
  transfers between devices with their start and end apart: 8 -> 8, of which waited for: 4 -> 6; matrix products, arithmetic and copies ran while one was open for 0% -> 1% of each run, Pallas kernels for 13% -> 12%
where the time goes in v3:
time: 108 us
  starting transfers between devices  49.7 us (46%)
  waiting for transfers between devices  30.2 us (28%)
  Pallas kernels  24.9 us (23%)
  local copies, waits for them, and re-layouts  2.1 us (2%)
    pallas_call x8, Pallas kernels, call(): pl.pallas_call(body, out_shape=shapes, in_specs=specs, out_specs=placed,...  24.9 us
    ppermute x2, waiting for transfers between devices, from_next(): lax.ppermute(head, axis, [(i + 1, i) for i in range(lax.axis_size(axis) -...  16.5 us
    all_to_all x1, starting transfers between devices, per_device(): shares = lax.all_to_all(sent, 'coil', 0, 0, tiled=True)  12.2 us
    all_to_all x1, starting transfers between devices, per_device(): spectra = lax.all_to_all(sent, 'space', 0, 0, tiled=True)  11.1 us
    ppermute x2, starting transfers between devices, from_previous(): lax.ppermute(tail, axis, [(i, i + 1) for i in range(lax.axis_size(axis) -...  10.6 us
    all_to_all x1, waiting for transfers between devices, per_device(): spectra = lax.all_to_all(sent, 'space', 0, 0, tiled=True)  7.69 us
    all_to_all x1, starting transfers between devices, per_device(): estimate = lax.all_to_all(estimate, 'coil', 0, 0, tiled=True)  7.39 us
    all_to_all x1, starting transfers between devices, per_device(): returned = lax.all_to_all(sent, 'space', 0, 0, tiled=True)  5.02 us
  transfers between devices with their start and end apart: 8, of which 6 were waited for; matrix products, arithmetic and copies ran while one was open for 1% of the time, Pallas kernels for 12%

profile of v3, /device:TPU:1, one launch (start us, length us, event | category | flops | bytes accessed | tf_op | source)
XLA Modules:
  0.0 107.7 jit_solution(12597165734746804528)
XLA Ops:
  0.6 0.8 slice.3
  1.4 0.8 broadcast_in_dim.2
  2.2 7.4 %all-to-all-start = ((bf16[8,2,2,32,128]{4,3,2,1,0:T(8,128)(2,1)}), bf16[8,2,2,32,128]{4,3,2,1,0:T(8,128)(2,1)S(1)}, u32[]{:S(2)}, u32[]{:S(2)}) async-start(bf16[8,2,2,32,128]{4,3,2,1,0:T(8,128)(2,1)} %broadcast_in_dim.2), calls=%async_computation | async-start | bytes 524288 | tf_op jit(solution)/shard_map/all_to_all | solution.py:502
  9.6 4.4 %prepare.1 = (bf16[448,128]{1,0:T(8,128)(2,1)S(1)}, bf16[448,128]{1,0:T(8,128)(2,1)S(1)}, bf16[32,2,32,96]{3,2,1,0:T(8,128)(2,1)S(1)}, f32[2,2,2,32,768]{4,3,2,1...) custom-call(bf16[32,2,32,96]{3,2,1,0:T(8,128)(2,1)} %state_hbm.1, ...), custom_call_target="tpu_custom_call" | custom-call | tf_op jit(solution)/shard_map/prepare/pallas_call | solution.py:29
  13.9 0.0 copy-start
  13.9 0.0 copy-start.1
  13.9 4.3 %all-to-all-done.est_ref = bf16[8,2,2,32,128]{4,3,2,1,0:T(8,128)(2,1)S(1)} async-done(((bf16[8,2,2,32,128]{4,3,2,1,0:T(8,128)(2,1)}), bf16[8,2,2,32,128]{4,3,2,1,0:T(8,128)(2,1)S(1)}, u32[]{:S(2)}, u32[]{:S(2)}) %all-to-all-start) | async-done | bytes 262176 | tf_op jit(solution)/shard_map/all_to_all | solution.py:502
  18.2 3.3 %forward_columns.1 = bf16[768,256]{1,0:T(8,128)(2,1)} custom-call(bf16[8,2,2,32,128]{4,3,2,1,0:T(8,128)(2,1)S(1)} %all-to-all-done.est_ref, f32[2,2,2,32,768]{4,3,2,1,0:T(8,128)S(1)} %get-tuple-element.24.sens_ref, bf16[768,768]{1,0:T(8,128)(2,1)} %get-tuple-element.25.cos_hbm, bf16[768,768]{1,0:T(8,128)(2,1)} %get-tuple-element.26.sin_hbm), custom_call_target="tpu_custom_call" | custom-call | tf_op jit(solution)/shard_map/forward_columns/pallas_call | solution.py:29
  21.5 11.1 %all-to-all-start.1 = ((bf16[32,24,256]{2,1,0:T(8,128)(2,1)}), bf16[32,24,256]{2,1,0:T(8,128)(2,1)S(1)}, u32[]{:S(2)}, u32[]{:S(2)}) async-start(bf16[32,24,256]{2,1,0:T(8,128)(2,1)} %bitcast), calls=%async_computation.1 | async-start | bytes 786432 | tf_op jit(solution)/shard_map/all_to_all | solution.py:555
  32.6 7.0 %collective-permute-start = (bf16[448,128]{1,0:T(8,128)(2,1)S(1)}, bf16[448,128]{1,0:T(8,128)(2,1)S(1)}, u32[]{:S(2)}, u32[]{:S(2)}) collective-permute-start(bf16[448,128]{1,0:T(8,128)(2,1)S(1)} %get-tuple-element.31), channel_id=1, source_target_pairs={{0,8},{8,16},{16,24},{24,32},{32,40},{40,48},{48,56},{56,64},{64,7... | collective-permute-start | bytes 344072 | tf_op jit(solution)/shard_map/ppermute | solution.py:480
  39.7 7.7 %all-to-all-done.1 = bf16[32,24,256]{2,1,0:T(8,128)(2,1)S(1)} async-done(((bf16[32,24,256]{2,1,0:T(8,128)(2,1)}), bf16[32,24,256]{2,1,0:T(8,128)(2,1)S(1)}, u32[]{:S(2)}, u32[]{:S(2)}) %all-to-all-start.1) | async-done | bytes 393248 | tf_op jit(solution)/shard_map/all_to_all | solution.py:555
  47.4 0.0 copy-done
  47.4 0.0 copy-done.1
  47.4 6.7 %consistency.1 = bf16[768,384]{1,0:T(8,128)(2,1)} custom-call(bf16[768,256]{1,0:T(8,128)(2,1)S(1)} %bitcast.8, f32[2,2,2,24,1024]{4,3,2,1,0:T(8,128)S(1)} %copy-done, s32[24,1024]{1,0:T(8,128)S(1)} %copy-done.1, bf16[1024,1280]{1,0:T(8,128)(2,1)} %get-tuple-element.29.cos_hbm, bf16[1024,1280]{1,0:T(8,128)(2,1)} %get-tuple-element.30.sin_hbm), custom_call_target="tpu_custom_call" | custom-call | tf_op jit(solution)/shard_map/consistency/pallas_call | solution.py:29
  54.1 0.0 collective-permute-done.above_ref
  54.1 5.0 %all-to-all-start.2 = ((bf16[32,24,384]{2,1,0:T(8,128)(2,1)}), bf16[32,24,384]{2,1,0:T(8,128)(2,1)S(1)}, u32[]{:S(2)}, u32[]{:S(2)}) async-start(bf16[32,24,384]{2,1,0:T(8,128)(2,1)} %bitcast.2), calls=%async_computation.2 | async-start | bytes 1179648 | tf_op jit(solution)/shard_map/all_to_all | solution.py:566
  59.1 1.3 %collective-permute-start.1 = (bf16[448,128]{1,0:T(8,128)(2,1)S(1)}, bf16[448,128]{1,0:T(8,128)(2,1)S(1)}, u32[]{:S(2)}, u32[]{:S(2)}) collective-permute-start(bf16[448,128]{1,0:T(8,128)(2,1)S(1)} %get-tuple-element.35), channel_id=1, source_target_pairs={{8,0},{16,8},{24,16},{32,24},{40,32},{48,40},{56,48},{64,56},{72,6... | collective-permute-start | bytes 344072 | tf_op jit(solution)/shard_map/ppermute | solution.py:484
  60.4 14.4 %collective-permute-done.1.below_ref = bf16[448,128]{1,0:T(8,128)(2,1)S(1)} collective-permute-done((bf16[448,128]{1,0:T(8,128)(2,1)S(1)}, bf16[448,128]{1,0:T(8,128)(2,1)S(1)}, u32[]{:S(2)}, u32[]{:S(2)}) %collective-permute-start.1) | collective-permute-done | bytes 114720 | tf_op jit(solution)/shard_map/ppermute | solution.py:484
  74.9 1.5 %all-to-all-done.2 = bf16[32,24,384]{2,1,0:T(8,128)(2,1)S(1)} async-done(((bf16[32,24,384]{2,1,0:T(8,128)(2,1)}), bf16[32,24,384]{2,1,0:T(8,128)(2,1)S(1)}, u32[]{:S(2)}, u32[]{:S(2)}) %all-to-all-start.2) | async-done | bytes 589856 | tf_op jit(solution)/shard_map/all_to_all | solution.py:566
  76.3 0.0 copy-start.5
  76.3 0.0 copy-start.2
  76.3 0.0 copy-start.3
  76.3 0.0 copy-start.4
  76.3 3.9 %backward_columns.1 = bf16[1280,128]{1,0:T(8,128)(2,1)} custom-call(bf16[768,384]{1,0:T(8,128)(2,1)S(1)} %bitcast.7, f32[2,2,2,32,768]{4,3,2,1,0:T(8,128)S(1)} %get-tuple-element.24.sens_ref, bf16[448,128]{1,0:T(8,128)(2,1)S(1)} %collective-permute-done.above_ref, bf16[448,128]{1,0:T(8,128)(2,1)S(1)} %collective-permute-done.1.below_ref, ...), custom_call_target="tpu_custom_call" | custom-call | tf_op jit(solution)/shard_map/backward_columns/pallas_call | solution.py:29
  80.3 12.2 %all-to-all-start.3 = ((bf16[8,160,128]{2,1,0:T(8,128)(2,1)}), bf16[8,160,128]{2,1,0:T(8,128)(2,1)S(1)}, u32[]{:S(2)}, u32[]{:S(2)}) async-start(bf16[8,160,128]{2,1,0:T(8,128)(2,1)} %bitcast.4), calls=%async_computation.3 | async-start | bytes 655360 | tf_op jit(solution)/shard_map/all_to_all | solution.py:581
  92.4 0.4 pack_cols.1
  92.8 3.5 %collective-permute-start.2 = (bf16[80,128]{1,0:T(8,128)(2,1)S(1)}, bf16[80,128]{1,0:T(8,128)(2,1)S(1)}, u32[]{:S(2)}, u32[]{:S(2)}) collective-permute-start(bf16[80,128]{1,0:T(8,128)(2,1)S(1)} %get-tuple-element.40), channel_id=1, source_target_pairs={{0,1},{1,2},{2,3},{3,4},{4,5},{5,6},{6,7},{8,9},{9,10},{10,11},{11... | collective-permute-start | bytes 61448 | tf_op jit(solution)/shard_map/ppermute | solution.py:480
  96.4 2.1 %collective-permute-start.3 = (bf16[80,128]{1,0:T(8,128)(2,1)S(1)}, bf16[80,128]{1,0:T(8,128)(2,1)S(1)}, u32[]{:S(2)}, u32[]{:S(2)}) collective-permute-start(bf16[80,128]{1,0:T(8,128)(2,1)S(1)} %get-tuple-element.41), channel_id=1, source_target_pairs={{1,0},{2,1},{3,2},{4,3},{5,4},{6,5},{7,6},{9,8},{10,9},{11,10},{12... | collective-permute-start | bytes 61448 | tf_op jit(solution)/shard_map/ppermute | solution.py:484
  98.5 0.0 copy-done.5
  98.5 0.5 copy.12.kernels_ref
  99.0 0.0 copy-done.2
  99.0 0.0 copy-done.3
  99.1 0.0 copy-done.4
  99.1 0.4 coupling_weights.1
  99.4 0.0 collective-permute-done.2.left_ref
  99.4 2.0 %collective-permute-done.3.right_ref = bf16[80,128]{1,0:T(8,128)(2,1)S(1)} collective-permute-done((bf16[80,128]{1,0:T(8,128)(2,1)S(1)}, bf16[80,128]{1,0:T(8,128)(2,1)S(1)}, u32[]{:S(2)}, u32[]{:S(2)}) %collective-permute-start.3) | collective-permute-done | bytes 20512 | tf_op jit(solution)/shard_map/ppermute | solution.py:484
  101.5 0.6 spread_state.1.state_ref
  102.1 0.3 all-to-all-done.3
  102.4 5.3 %couple.1 = (bf16[32,2,32,96]{3,2,1,0:T(8,128)(2,1)}, f32[2,2,32,96]{3,2,1,0:T(8,128)}) custom-call(bf16[1280,128]{1,0:T(8,128)(2,1)S(1)} %bitcast.9, bf16[2560,128]{1,0:T(8,128)(2,1)S(1)} %spread_state.1.state_ref, bf16[4,96,96]{2,1,0:T(8,128)(2,1)S(1)} %get-tuple-element.42.weight_ref, bf16[4,32,32]{2,1,0:T(8,128)(2,1)S(1)} %get-tuple-element.43.mixer_ref, ...), custom_call_target="tpu_custom_call" | custom-call | tf_op jit(solution)/shard_map/couple/pallas_call | solution.py:29
  (1 shorter events, 0.0 us)
Async XLA Ops:
  2.2 16.1 %all-to-all-start = ((bf16[8,2,2,32,128]{4,3,2,1,0:T(8,128)(2,1)}), bf16[8,2,2,32,128]{4,3,2,1,0:T(8,128)(2,1)S(1)}, u32[]{:S(2)}, u32[]{:S(2)}) async-start(bf16[8,2,2,32,128]{4,3,2,1,0:T(8,128)(2,1)} %broadcast_in_dim.2), calls=%async_computation | async-start | bytes 524288 | tf_op jit(solution)/shard_map/all_to_all | solution.py:502
  13.9 33.5 %copy-start = (f32[2,2,2,24,1024]{4,3,2,1,0:T(8,128)S(1)}, f32[2,2,2,24,1024]{4,3,2,1,0:T(8,128)}, u32[]{:S(2)}) copy-start(f32[2,2,2,24,1024]{4,3,2,1,0:T(8,128)} %kdata_ref.1) | copy-start | bytes 2359300
  13.9 33.4 %copy-start.1 = (s32[24,1024]{1,0:T(8,128)S(1)}, s32[24,1024]{1,0:T(8,128)}, u32[]{:S(2)}) copy-start(s32[24,1024]{1,0:T(8,128)} %mask_ref.1) | copy-start | bytes 294916
  21.5 25.9 %all-to-all-start.1 = ((bf16[32,24,256]{2,1,0:T(8,128)(2,1)}), bf16[32,24,256]{2,1,0:T(8,128)(2,1)S(1)}, u32[]{:S(2)}, u32[]{:S(2)}) async-start(bf16[32,24,256]{2,1,0:T(8,128)(2,1)} %bitcast), calls=%async_computation.1 | async-start | bytes 786432 | tf_op jit(solution)/shard_map/all_to_all | solution.py:555
  32.6 21.5 %collective-permute-start = (bf16[448,128]{1,0:T(8,128)(2,1)S(1)}, bf16[448,128]{1,0:T(8,128)(2,1)S(1)}, u32[]{:S(2)}, u32[]{:S(2)}) collective-permute-start(bf16[448,128]{1,0:T(8,128)(2,1)S(1)} %get-tuple-element.31), channel_id=1, source_target_pairs={{0,8},{8,16},{16,24},{24,32},{32,40},{40,48},{48,56},{56,64},{64,7... | collective-permute-start | bytes 344072 | tf_op jit(solution)/shard_map/ppermute | solution.py:480
  54.1 22.2 %all-to-all-start.2 = ((bf16[32,24,384]{2,1,0:T(8,128)(2,1)}), bf16[32,24,384]{2,1,0:T(8,128)(2,1)S(1)}, u32[]{:S(2)}, u32[]{:S(2)}) async-start(bf16[32,24,384]{2,1,0:T(8,128)(2,1)} %bitcast.2), calls=%async_computation.2 | async-start | bytes 1179648 | tf_op jit(solution)/shard_map/all_to_all | solution.py:566
  59.1 15.7 %collective-permute-start.1 = (bf16[448,128]{1,0:T(8,128)(2,1)S(1)}, bf16[448,128]{1,0:T(8,128)(2,1)S(1)}, u32[]{:S(2)}, u32[]{:S(2)}) collective-permute-start(bf16[448,128]{1,0:T(8,128)(2,1)S(1)} %get-tuple-element.35), channel_id=1, source_target_pairs={{8,0},{16,8},{24,16},{32,24},{40,32},{48,40},{56,48},{64,56},{72,6... | collective-permute-start | bytes 344072 | tf_op jit(solution)/shard_map/ppermute | solution.py:484
  76.3 22.1 %copy-start.5 = (bf16[4,27,16,16]{1,3,2,0:T(8,128)(2,1)S(1)}, bf16[4,27,16,16]{1,3,2,0:T(8,128)(2,1)}, u32[]{:S(2)}) copy-start(bf16[4,27,16,16]{1,3,2,0:T(8,128)(2,1)} %param.15) | copy-start | bytes 165892
  76.3 22.7 %copy-start.2 = (bf16[4,16,16]{2,1,0:T(8,128)(2,1)S(1)}, bf16[4,16,16]{2,1,0:T(8,128)(2,1)}, u32[]{:S(2)}) copy-start(bf16[4,16,16]{2,1,0:T(8,128)(2,1)} %mixers_ref.1) | copy-start | bytes 6148
  76.3 22.7 %copy-start.3 = (f32[4,16]{1,0:T(4,128)S(1)}, f32[4,16]{1,0:T(4,128)}, u32[]{:S(2)}) copy-start(f32[4,16]{1,0:T(4,128)} %biases_ref.1) | copy-start | bytes 772
  76.3 22.7 %copy-start.4 = (f32[32,2]{0,1:T(2,128)S(1)}, f32[32,2]{0,1:T(2,128)}, u32[]{:S(2)}) copy-start(f32[32,2]{0,1:T(2,128)} %param.14) | copy-start | bytes 772
  80.3 22.2 %all-to-all-start.3 = ((bf16[8,160,128]{2,1,0:T(8,128)(2,1)}), bf16[8,160,128]{2,1,0:T(8,128)(2,1)S(1)}, u32[]{:S(2)}, u32[]{:S(2)}) async-start(bf16[8,160,128]{2,1,0:T(8,128)(2,1)} %bitcast.4), calls=%async_computation.3 | async-start | bytes 655360 | tf_op jit(solution)/shard_map/all_to_all | solution.py:581
  92.8 6.6 %collective-permute-start.2 = (bf16[80,128]{1,0:T(8,128)(2,1)S(1)}, bf16[80,128]{1,0:T(8,128)(2,1)S(1)}, u32[]{:S(2)}, u32[]{:S(2)}) collective-permute-start(bf16[80,128]{1,0:T(8,128)(2,1)S(1)} %get-tuple-element.40), channel_id=1, source_target_pairs={{0,1},{1,2},{2,3},{3,4},{4,5},{5,6},{6,7},{8,9},{9,10},{10,11},{11... | collective-permute-start | bytes 61448 | tf_op jit(solution)/shard_map/ppermute | solution.py:480
  96.4 5.1 %collective-permute-start.3 = (bf16[80,128]{1,0:T(8,128)(2,1)S(1)}, bf16[80,128]{1,0:T(8,128)(2,1)S(1)}, u32[]{:S(2)}, u32[]{:S(2)}) collective-permute-start(bf16[80,128]{1,0:T(8,128)(2,1)S(1)} %get-tuple-element.41), channel_id=1, source_target_pairs={{1,0},{2,1},{3,2},{4,3},{5,4},{6,5},{7,6},{9,8},{10,9},{11,10},{12... | collective-permute-start | bytes 61448 | tf_op jit(solution)/shard_map/ppermute | solution.py:484

commit v4 on v3

--- a/solution.py
+++ b/solution.py
@@ -11,7 +11,7 @@
 BF16 = jnp.bfloat16
 REACH = 4
 FINE = 32
-BATCH = 12
+BATCH = 38
 VMEM = pl.BlockSpec(memory_space=pltpu.VMEM)
 HBM = pl.BlockSpec(memory_space=pltpu.HBM)
 
@@ -95,7 +95,7 @@
 
 def prepare(
     state_hbm, sens_hbm, par_hbm, pe_hbm,
-    tail_ref, head_ref, state_ref, sens_ref, par_cos_hbm, par_sin_hbm, pe_cos_hbm, pe_sin_hbm,
+    first_ref, second_ref, state_ref, sens_ref, par_cos_hbm, par_sin_hbm, pe_cos_hbm, pe_sin_hbm,
     par_ref, pe_ref, par_cos, par_sin, pe_cos, pe_sin, sems, par_sems, pe_sems,
 ):
     pairs = ((par_hbm, par_ref), (pe_hbm, pe_ref), (state_hbm, state_ref), (sens_hbm, sens_ref))
@@ -109,7 +109,7 @@
     arrived(copies[1:2])
     sent = sent + fill_tables(pe_ref, pe_cos_hbm, pe_sin_hbm, pe_cos, pe_sin, pe_sems)
     arrived(copies[2:])
-    pack_rows(state_ref, sens_ref, tail_ref, head_ref)
+    pack_rows(state_ref, sens_ref, first_ref, second_ref)
     arrived(sent)
 
 
@@ -235,7 +235,7 @@
 
 
 def backward_columns(
-    recv_ref, sens_ref, above_ref, below_ref, cos_hbm, sin_hbm, out_ref, part_ref, edge_ref, cos_ref, sin_ref, sems
+    recv_ref, sens_ref, first_ref, second_ref, cos_hbm, sin_hbm, out_ref, part_ref, edge_ref, cos_ref, sin_ref, sems
 ):
     step = 256
     blocks = table_copies([(cos_hbm, cos_ref), (sin_hbm, sin_ref)], sems, step)
@@ -247,7 +247,7 @@
     low = lax.axis_index("space") // 8 % 2 == 0
     for tile in range(npar // 128):
         here = pl.ds(tile * 2 * coils * spots * REACH, 2 * coils * spots * REACH)
-        above, below = above_ref[here, :].astype(F32), below_ref[here, :].astype(F32)
+        above, below = around(first_ref, second_ref, here, slice(0, 128))
         for k in range(2 * coils * spots):
             at = slice(k * REACH, (k + 1) * REACH)
             part, coil, spot = k // (coils * spots), k // spots % coils, k % spots
@@ -298,22 +298,32 @@
         out_ref[pl.ds(owner * total, total), :] = value.astype(BF16)
 
 
-def pack_rows(state_ref, sens_ref, tail_ref, head_ref):
+def pack_rows(state_ref, sens_ref, first_ref, second_ref):
     channels, spots, rows, cols = state_ref.shape
     coils, npar = sens_ref.shape[1], sens_ref.shape[4]
+    even = lax.axis_index("space") % 2 == 0
     at = 0
+
+    def store(tail, head, width):
+        first_ref[pl.ds(at, 8), 0:width] = jnp.where(even, tail, head).astype(BF16)
+        second_ref[pl.ds(at, 8), 0:width] = jnp.where(even, head, tail).astype(BF16)
+
     for tile in range(npar // 128):
         here = pl.ds(128 * tile, 128)
         for part in range(2):
             for coil in range(coils):
-                for ref, low in ((tail_ref, rows - 8), (head_ref, 0)):
-                    pair = [sens_ref[part, coil, spot, pl.ds(low, 8), here] for spot in range(2)]
-                    ref[pl.ds(at, 8), :] = joined_edges(pair, low).astype(BF16)
+                pair = [
+                    joined_edges([sens_ref[part, coil, spot, pl.ds(low, 8), here] for spot in range(2)], low)
+                    for low in (rows - 8, 0)
+                ]
+                store(*pair, 128)
                 at += 8
     for channel in range(channels):
-        for ref, low in ((tail_ref, rows - 8), (head_ref, 0)):
-            pair = [state_ref[channel, spot, pl.ds(low, 8), :].astype(F32) for spot in range(2)]
-            ref[pl.ds(at, 8), 0:cols] = joined_edges(pair, low).astype(BF16)
+        pair = [
+            joined_edges([state_ref[channel, spot, pl.ds(low, 8), :].astype(F32) for spot in range(2)], low)
+            for low in (rows - 8, 0)
+        ]
+        store(*pair, cols)
         at += 8
 
 
@@ -324,26 +334,32 @@
     return jnp.concatenate([first[:REACH], second[:REACH]], axis=0)
 
 
-def tall_state(state_ref, above_ref, below_ref, channel, spot, skip):
+def around(first_ref, second_ref, here, cols):
+    even = lax.axis_index("space") % 2 == 0
+    first, second = first_ref[here, cols].astype(F32), second_ref[here, cols].astype(F32)
+    return jnp.where(even, second, first), jnp.where(even, first, second)
+
+
+def tall_state(state_ref, first_ref, second_ref, channel, spot, skip):
     cols = state_ref.shape[3]
-    at = skip + 8 * channel
-    below = below_ref[pl.ds(at, 8), 0:cols].astype(F32)[spot * REACH : (spot + 1) * REACH]
-    above = above_ref[pl.ds(at, 8), 0:cols].astype(F32)[spot * REACH : (spot + 1) * REACH]
+    above, below = around(first_ref, second_ref, pl.ds(skip + 8 * channel, 8), slice(0, cols))
+    below = below[spot * REACH : (spot + 1) * REACH]
+    above = above[spot * REACH : (spot + 1) * REACH]
     value = jnp.concatenate([state_ref[channel, spot].astype(F32), jnp.concatenate([below, above], axis=0)], axis=0)
     return jnp.concatenate([value, jnp.zeros((value.shape[0], 128 - cols), F32)], axis=1)
 
 
-def pack_cols(state_ref, above_ref, below_ref, tail_ref, head_ref):
+def pack_cols(state_ref, first_ref, second_ref, tail_ref, head_ref):
     channels, spots, rows, cols = state_ref.shape
     tall = rows + 2 * REACH
-    skip = above_ref.shape[0] - channels * spots * REACH
+    skip = first_ref.shape[0] - channels * spots * REACH
     per = 128 // REACH
     lane = lax.broadcasted_iota(jnp.int32, (tall, 128), 1)
     for group in range(channels * spots // per):
         tail = head = jnp.zeros((tall, 128), F32)
         for k in range(per):
             channel, spot = divmod(group * per + k, spots)
-            value = tall_state(state_ref, above_ref, below_ref, channel, spot, skip)
+            value = tall_state(state_ref, first_ref, second_ref, channel, spot, skip)
             here = lane // REACH == k
             tail = jnp.where(here, pltpu.roll(value, (REACH * k - cols + REACH) % 128, 1), tail)
             head = jnp.where(here, pltpu.roll(value, REACH * k, 1) if k else value, head)
@@ -351,17 +367,17 @@
         head_ref[pl.ds(group * tall, tall), :] = head.astype(BF16)
 
 
-def spread_state(state_ref, above_ref, below_ref, left_ref, right_ref, out_ref, wide_ref):
+def spread_state(state_ref, first_ref, second_ref, left_ref, right_ref, out_ref, wide_ref):
     channels, spots, rows, cols = state_ref.shape
     tall = rows + 2 * REACH
     half = channels // 2
-    skip = above_ref.shape[0] - channels * spots * REACH
+    skip = first_ref.shape[0] - channels * spots * REACH
     per = 128 // REACH
     lane = lax.broadcasted_iota(jnp.int32, (tall, 128), 1)
     for channel in range(channels):
         for spot in range(spots):
             group, k = divmod(channel * spots + spot, per)
-            value = tall_state(state_ref, above_ref, below_ref, channel, spot, skip)
+            value = tall_state(state_ref, first_ref, second_ref, channel, spot, skip)
             here = pl.ds(group * tall, tall)
             right = pltpu.roll(right_ref[here, :].astype(F32), (cols - REACH * k) % 128, 1)
             left = pltpu.roll(left_ref[here, :].astype(F32), (128 - REACH - REACH * k) % 128, 1)
@@ -484,6 +500,12 @@
     return lax.ppermute(head, axis, [(i + 1, i) for i in range(lax.axis_size(axis) - 1)])
 
 
+def swapped(array, axis, start):
+    count = lax.axis_size(axis)
+    pairs = [(i, i + 1) for i in range(start, count - 1, 2)]
+    return lax.ppermute(array, axis, pairs + [(j, i) for i, j in pairs])
+
+
 def per_device(state, sens, kdata, mask, inject, kernels, biases, mixers):
     channels, spots, rows, cols = state.shape
     coils = sens.shape[1]
@@ -523,7 +545,7 @@
 
     par_scratch = table_scratch(npar, npar, npar // FINE // 4)
     pe_scratch = table_scratch(npe, len(pe_columns), npe // FINE // 4)
-    tail, head, state, sens, *tables = call(
+    first, second, state, sens, *tables = call(
         prepare,
         [((depth, 128), BF16)] * 2
         + [(state.shape, BF16), (sens.shape, F32)]
@@ -551,9 +573,9 @@
         "forward_columns",
         estimate, sens, *par_tables,
     )
-    sent, tail = lax.optimization_barrier((sent, tail))
+    sent, first, second = lax.optimization_barrier((sent, first, second))
     spectra = lax.all_to_all(sent, "space", 0, 0, tiled=True)
-    above = from_previous(tail, "space")
+    first, second = swapped(first, "space", 0), swapped(second, "space", 1)
 
     (sent,) = call(
         consistency,
@@ -562,9 +584,12 @@
         "consistency",
         spectra, kdata, mask, *pe_tables,
     )
-    sent, above, head = lax.optimization_barrier((sent, above, head))
+    sent, first, second = lax.optimization_barrier((sent, first, second))
     returned = lax.all_to_all(sent, "space", 0, 0, tiled=True)
-    below = from_next(head, "space")
+
+    packed = [((channels * spots * REACH // 128 * tall, 128), BF16)] * 2
+    tail, head = call(pack_cols, packed, [], "pack_cols", state, first, second)
+    left, right = from_previous(tail, "coil"), from_next(head, "coil")
 
     (sent,) = call(
         backward_columns,
@@ -575,21 +600,17 @@
             *table_scratch(npar, npar, npar // 256),
         ],
         "backward_columns",
-        returned, sens, above, below, *par_tables,
-    )
-    sent, above, below = lax.optimization_barrier((sent, above, below))
+        returned, sens, first, second, *par_tables,
+    )
+    sent, left, right = lax.optimization_barrier((sent, left, right))
     shares = lax.all_to_all(sent, "coil", 0, 0, tiled=True)
-
-    packed = [((channels * spots * REACH // 128 * tall, 128), BF16)] * 2
-    tail, head = call(pack_cols, packed, [], "pack_cols", state, above, below)
-    left, right = from_previous(tail, "coil"), from_next(head, "coil")
 
     (spread,) = call(
         spread_state,
         [((tall * channels * spots, 128), BF16)],
         [((channels * spots * tall, 128), F32)],
         "spread_state",
-        state, above, below, left, right,
+        state, first, second, left, right,
     )
 
     weight, mixer, bias, added = call(

time: 108 us -> 105 us (0.972)
  waiting for transfers between devices: 30.2 us -> 27.1 us
  starting transfers between devices: 49.7 us -> 51.3 us
  Pallas kernels: 24.9 us -> 23.5 us
    ppermute x2 -> x1, waiting for transfers between devices: 16.5 us -> 0.01 us  [from_next(): lax.ppermute(head, axis, [(i + 1, i) for i in range(lax.axis_size(axis) -...]
    all_to_all x1, waiting for transfers between devices: 0.31 us -> 8.44 us  [per_device(): shares = lax.all_to_all(sent, 'coil', 0, 0, tiled=True)]
    ppermute x0 -> x2, starting transfers between devices: none -> 5.88 us  [swapped(): return lax.ppermute(array, axis, pairs + [(j, i) for i, j in pairs])]
    all_to_all x1, waiting for transfers between devices: 7.69 us -> 10.9 us  [per_device(): spectra = lax.all_to_all(sent, 'space', 0, 0, tiled=True)]
    all_to_all x1, starting transfers between devices: 12.2 us -> 9.52 us  [per_device(): shares = lax.all_to_all(sent, 'coil', 0, 0, tiled=True)]
    all_to_all x1, waiting for transfers between devices: 1.45 us -> 3.48 us  [per_device(): returned = lax.all_to_all(sent, 'space', 0, 0, tiled=True)]
    ppermute x2 -> x1, starting transfers between devices: 10.6 us -> 8.82 us  [from_previous(): lax.ppermute(tail, axis, [(i, i + 1) for i in range(lax.axis_size(axis) -...]
    all_to_all x1, starting transfers between devices: 5.02 us -> 6.64 us  [per_device(): returned = lax.all_to_all(sent, 'space', 0, 0, tiled=True)]
  transfers between devices with their start and end apart: 8 -> 8, of which waited for: 6 -> 4; matrix products, arithmetic and copies ran while one was open for 1% -> 1% of each run, Pallas kernels for 12% -> 16%
where the time goes in v4:
time: 105 us
  starting transfers between devices  51.3 us (49%)
  waiting for transfers between devices  27.1 us (26%)
  Pallas kernels  23.5 us (22%)
  local copies, waits for them, and re-layouts  2.1 us (2%)
    pallas_call x8, Pallas kernels, call(): pl.pallas_call(body, out_shape=shapes, in_specs=specs, out_specs=placed,...  23.5 us
    all_to_all x1, starting transfers between devices, per_device(): spectra = lax.all_to_all(sent, 'space', 0, 0, tiled=True)  11.1 us
    all_to_all x1, waiting for transfers between devices, per_device(): spectra = lax.all_to_all(sent, 'space', 0, 0, tiled=True)  10.9 us
    all_to_all x1, starting transfers between devices, per_device(): shares = lax.all_to_all(sent, 'coil', 0, 0, tiled=True)  9.52 us
    ppermute x1, starting transfers between devices, from_previous(): lax.ppermute(tail, axis, [(i, i + 1) for i in range(lax.axis_size(axis) -...  8.82 us
    all_to_all x1, waiting for transfers between devices, per_device(): shares = lax.all_to_all(sent, 'coil', 0, 0, tiled=True)  8.44 us
    all_to_all x1, starting transfers between devices, per_device(): estimate = lax.all_to_all(estimate, 'coil', 0, 0, tiled=True)  7.39 us
    all_to_all x1, starting transfers between devices, per_device(): returned = lax.all_to_all(sent, 'space', 0, 0, tiled=True)  6.64 us
  transfers between devices with their start and end apart: 8, of which 4 were waited for; matrix products, arithmetic and copies ran while one was open for 1% of the time, Pallas kernels for 16%

profile of v4, /device:TPU:1, one launch (start us, length us, event | category | flops | bytes accessed | tf_op | source)
XLA Modules:
  0.0 104.7 jit_solution(11833171299298022204)
XLA Ops:
  0.6 0.8 slice.3
  1.4 0.8 broadcast_in_dim.2
  2.2 7.4 %all-to-all-start = ((bf16[8,2,2,32,128]{4,3,2,1,0:T(8,128)(2,1)}), bf16[8,2,2,32,128]{4,3,2,1,0:T(8,128)(2,1)S(1)}, u32[]{:S(2)}, u32[]{:S(2)}) async-start(bf16[8,2,2,32,128]{4,3,2,1,0:T(8,128)(2,1)} %broadcast_in_dim.2), calls=%async_computation | async-start | bytes 524288 | tf_op jit(solution)/shard_map/all_to_all | solution.py:524
  9.6 4.4 %prepare.1 = (bf16[448,128]{1,0:T(8,128)(2,1)S(1)}, bf16[448,128]{1,0:T(8,128)(2,1)S(1)}, bf16[32,2,32,96]{3,2,1,0:T(8,128)(2,1)S(1)}, f32[2,2,2,32,768]{4,3,2,1...) custom-call(bf16[32,2,32,96]{3,2,1,0:T(8,128)(2,1)} %state_hbm.1, ...), custom_call_target="tpu_custom_call" | custom-call | tf_op jit(solution)/shard_map/prepare/pallas_call | solution.py:29
  13.9 0.0 copy-start
  13.9 0.0 copy-start.1
  13.9 4.3 %all-to-all-done.est_ref = bf16[8,2,2,32,128]{4,3,2,1,0:T(8,128)(2,1)S(1)} async-done(((bf16[8,2,2,32,128]{4,3,2,1,0:T(8,128)(2,1)}), bf16[8,2,2,32,128]{4,3,2,1,0:T(8,128)(2,1)S(1)}, u32[]{:S(2)}, u32[]{:S(2)}) %all-to-all-start) | async-done | bytes 262176 | tf_op jit(solution)/shard_map/all_to_all | solution.py:524
  18.2 3.3 %forward_columns.1 = bf16[768,256]{1,0:T(8,128)(2,1)} custom-call(bf16[8,2,2,32,128]{4,3,2,1,0:T(8,128)(2,1)S(1)} %all-to-all-done.est_ref, f32[2,2,2,32,768]{4,3,2,1,0:T(8,128)S(1)} %get-tuple-element.25.sens_ref, bf16[768,768]{1,0:T(8,128)(2,1)} %get-tuple-element.26.cos_hbm, bf16[768,768]{1,0:T(8,128)(2,1)} %get-tuple-element.27.sin_hbm), custom_call_target="tpu_custom_call" | custom-call | tf_op jit(solution)/shard_map/forward_columns/pallas_call | solution.py:29
  21.5 11.1 %all-to-all-start.1 = ((bf16[32,24,256]{2,1,0:T(8,128)(2,1)}), bf16[32,24,256]{2,1,0:T(8,128)(2,1)S(1)}, u32[]{:S(2)}, u32[]{:S(2)}) async-start(bf16[32,24,256]{2,1,0:T(8,128)(2,1)} %bitcast), calls=%async_computation.1 | async-start | bytes 786432 | tf_op jit(solution)/shard_map/all_to_all | solution.py:577
  32.6 5.2 %collective-permute-start = (bf16[448,128]{1,0:T(8,128)(2,1)S(1)}, bf16[448,128]{1,0:T(8,128)(2,1)S(1)}, u32[]{:S(2)}, u32[]{:S(2)}) collective-permute-start(bf16[448,128]{1,0:T(8,128)(2,1)S(1)} %get-tuple-element.33), channel_id=1, source_target_pairs={{0,8},{16,24},{32,40},{48,56},{64,72},{80,88},{96,104},{112,120},{... | collective-permute-start | bytes 344072 | tf_op jit(solution)/shard_map/ppermute | solution.py:506
  37.9 0.7 collective-permute-start.1
  38.5 10.9 %all-to-all-done.1 = bf16[32,24,256]{2,1,0:T(8,128)(2,1)S(1)} async-done(((bf16[32,24,256]{2,1,0:T(8,128)(2,1)}), bf16[32,24,256]{2,1,0:T(8,128)(2,1)S(1)}, u32[]{:S(2)}, u32[]{:S(2)}) %all-to-all-start.1) | async-done | bytes 393248 | tf_op jit(solution)/shard_map/all_to_all | solution.py:577
  49.4 0.0 copy-done
  49.4 0.0 copy-done.1
  49.4 6.7 %consistency.1 = bf16[768,384]{1,0:T(8,128)(2,1)} custom-call(bf16[768,256]{1,0:T(8,128)(2,1)S(1)} %bitcast.8, f32[2,2,2,24,1024]{4,3,2,1,0:T(8,128)S(1)} %copy-done, s32[24,1024]{1,0:T(8,128)S(1)} %copy-done.1, bf16[1024,1280]{1,0:T(8,128)(2,1)} %get-tuple-element.31.cos_hbm, bf16[1024,1280]{1,0:T(8,128)(2,1)} %get-tuple-element.32.sin_hbm), custom_call_target="tpu_custom_call" | custom-call | tf_op jit(solution)/shard_map/consistency/pallas_call | solution.py:29
  56.1 0.0 collective-permute-done.first_ref
  56.1 0.0 collective-permute-done.1.second_ref
  56.1 6.6 %all-to-all-start.2 = ((bf16[32,24,384]{2,1,0:T(8,128)(2,1)}), bf16[32,24,384]{2,1,0:T(8,128)(2,1)S(1)}, u32[]{:S(2)}, u32[]{:S(2)}) async-start(bf16[32,24,384]{2,1,0:T(8,128)(2,1)} %bitcast.2), calls=%async_computation.2 | async-start | bytes 1179648 | tf_op jit(solution)/shard_map/all_to_all | solution.py:588
  62.8 0.4 pack_cols.1
  63.2 0.0 copy-start.5
  63.2 8.8 %collective-permute-start.2 = (bf16[80,128]{1,0:T(8,128)(2,1)S(1)}, bf16[80,128]{1,0:T(8,128)(2,1)S(1)}, u32[]{:S(2)}, u32[]{:S(2)}) collective-permute-start(bf16[80,128]{1,0:T(8,128)(2,1)S(1)} %get-tuple-element.39), channel_id=1, source_target_pairs={{0,1},{1,2},{2,3},{3,4},{4,5},{5,6},{6,7},{8,9},{9,10},{10,11},{11... | collective-permute-start | bytes 61448 | tf_op jit(solution)/shard_map/ppermute | solution.py:496
  72.0 1.9 %collective-permute-start.3 = (bf16[80,128]{1,0:T(8,128)(2,1)S(1)}, bf16[80,128]{1,0:T(8,128)(2,1)S(1)}, u32[]{:S(2)}, u32[]{:S(2)}) collective-permute-start(bf16[80,128]{1,0:T(8,128)(2,1)S(1)} %get-tuple-element.40), channel_id=1, source_target_pairs={{1,0},{2,1},{3,2},{4,3},{5,4},{6,5},{7,6},{9,8},{10,9},{11,10},{12... | collective-permute-start | bytes 61448 | tf_op jit(solution)/shard_map/ppermute | solution.py:500
  74.0 3.5 %all-to-all-done.2 = bf16[32,24,384]{2,1,0:T(8,128)(2,1)S(1)} async-done(((bf16[32,24,384]{2,1,0:T(8,128)(2,1)}), bf16[32,24,384]{2,1,0:T(8,128)(2,1)S(1)}, u32[]{:S(2)}, u32[]{:S(2)}) %all-to-all-start.2) | async-done | bytes 589856 | tf_op jit(solution)/shard_map/all_to_all | solution.py:588
  77.4 0.0 copy-start.2
  77.4 0.0 copy-start.3
  77.4 0.0 copy-start.4
  77.5 3.9 %backward_columns.1 = bf16[1280,128]{1,0:T(8,128)(2,1)} custom-call(bf16[768,384]{1,0:T(8,128)(2,1)S(1)} %bitcast.7, f32[2,2,2,32,768]{4,3,2,1,0:T(8,128)S(1)} %get-tuple-element.25.sens_ref, bf16[448,128]{1,0:T(8,128)(2,1)S(1)} %collective-permute-done.first_ref, bf16[448,128]{1,0:T(8,128)(2,1)S(1)} %collective-permute-done.1.second_ref, ...), custom_call_target="tpu_custom_call" | custom-call | tf_op jit(solution)/shard_map/backward_columns/pallas_call | solution.py:29
  81.4 0.0 collective-permute-done.2.left_ref
  81.4 0.0 collective-permute-done.3.right_ref
  81.4 9.5 %all-to-all-start.3 = ((bf16[8,160,128]{2,1,0:T(8,128)(2,1)}), bf16[8,160,128]{2,1,0:T(8,128)(2,1)S(1)}, u32[]{:S(2)}, u32[]{:S(2)}) async-start(bf16[8,160,128]{2,1,0:T(8,128)(2,1)} %bitcast.4), calls=%async_computation.3 | async-start | bytes 655360 | tf_op jit(solution)/shard_map/all_to_all | solution.py:606
  90.9 0.0 copy-done.5
  90.9 0.5 copy.12.kernels_ref
  91.4 0.0 copy-done.2
  91.5 0.0 copy-done.3
  91.5 0.0 copy-done.4
  91.5 0.4 coupling_weights.1
  91.8 0.6 spread_state.1.state_ref
  92.5 8.4 %all-to-all-done.3 = bf16[8,160,128]{2,1,0:T(8,128)(2,1)S(1)} async-done(((bf16[8,160,128]{2,1,0:T(8,128)(2,1)}), bf16[8,160,128]{2,1,0:T(8,128)(2,1)S(1)}, u32[]{:S(2)}, u32[]{:S(2)}) %all-to-all-start.3) | async-done | bytes 327712 | tf_op jit(solution)/shard_map/all_to_all | solution.py:606
  100.9 3.8 %couple.1 = (bf16[32,2,32,96]{3,2,1,0:T(8,128)(2,1)}, f32[2,2,32,96]{3,2,1,0:T(8,128)}) custom-call(bf16[1280,128]{1,0:T(8,128)(2,1)S(1)} %bitcast.9, bf16[2560,128]{1,0:T(8,128)(2,1)S(1)} %spread_state.1.state_ref, bf16[4,96,96]{2,1,0:T(8,128)(2,1)S(1)} %get-tuple-element.44.weight_ref, bf16[4,32,32]{2,1,0:T(8,128)(2,1)S(1)} %get-tuple-element.45.mixer_ref, ...), custom_call_target="tpu_custom_call" | custom-call | tf_op jit(solution)/shard_map/couple/pallas_call | solution.py:29
  (1 shorter events, 0.0 us)
Async XLA Ops:
  2.2 16.1 %all-to-all-start = ((bf16[8,2,2,32,128]{4,3,2,1,0:T(8,128)(2,1)}), bf16[8,2,2,32,128]{4,3,2,1,0:T(8,128)(2,1)S(1)}, u32[]{:S(2)}, u32[]{:S(2)}) async-start(bf16[8,2,2,32,128]{4,3,2,1,0:T(8,128)(2,1)} %broadcast_in_dim.2), calls=%async_computation | async-start | bytes 524288 | tf_op jit(solution)/shard_map/all_to_all | solution.py:524
  13.9 35.5 %copy-start = (f32[2,2,2,24,1024]{4,3,2,1,0:T(8,128)S(1)}, f32[2,2,2,24,1024]{4,3,2,1,0:T(8,128)}, u32[]{:S(2)}) copy-start(f32[2,2,2,24,1024]{4,3,2,1,0:T(8,128)} %kdata_ref.1) | copy-start | bytes 2359300
  13.9 35.5 %copy-start.1 = (s32[24,1024]{1,0:T(8,128)S(1)}, s32[24,1024]{1,0:T(8,128)}, u32[]{:S(2)}) copy-start(s32[24,1024]{1,0:T(8,128)} %mask_ref.1) | copy-start | bytes 294916
  21.5 27.9 %all-to-all-start.1 = ((bf16[32,24,256]{2,1,0:T(8,128)(2,1)}), bf16[32,24,256]{2,1,0:T(8,128)(2,1)S(1)}, u32[]{:S(2)}, u32[]{:S(2)}) async-start(bf16[32,24,256]{2,1,0:T(8,128)(2,1)} %bitcast), calls=%async_computation.1 | async-start | bytes 786432 | tf_op jit(solution)/shard_map/all_to_all | solution.py:577
  32.6 23.5 %collective-permute-start = (bf16[448,128]{1,0:T(8,128)(2,1)S(1)}, bf16[448,128]{1,0:T(8,128)(2,1)S(1)}, u32[]{:S(2)}, u32[]{:S(2)}) collective-permute-start(bf16[448,128]{1,0:T(8,128)(2,1)S(1)} %get-tuple-element.33), channel_id=1, source_target_pairs={{0,8},{16,24},{32,40},{48,56},{64,72},{80,88},{96,104},{112,120},{... | collective-permute-start | bytes 344072 | tf_op jit(solution)/shard_map/ppermute | solution.py:506
  37.9 18.3 %collective-permute-start.1 = (bf16[448,128]{1,0:T(8,128)(2,1)S(1)}, bf16[448,128]{1,0:T(8,128)(2,1)S(1)}, u32[]{:S(2)}, u32[]{:S(2)}) collective-permute-start(bf16[448,128]{1,0:T(8,128)(2,1)S(1)} %get-tuple-element.34), channel_id=1, source_target_pairs={{8,16},{24,32},{40,48},{56,64},{72,80},{88,96},{104,112},{120,128}... | collective-permute-start | bytes 344072 | tf_op jit(solution)/shard_map/ppermute | solution.py:506
  56.1 21.3 %all-to-all-start.2 = ((bf16[32,24,384]{2,1,0:T(8,128)(2,1)}), bf16[32,24,384]{2,1,0:T(8,128)(2,1)S(1)}, u32[]{:S(2)}, u32[]{:S(2)}) async-start(bf16[32,24,384]{2,1,0:T(8,128)(2,1)} %bitcast.2), calls=%async_computation.2 | async-start | bytes 1179648 | tf_op jit(solution)/shard_map/all_to_all | solution.py:588
  63.2 27.7 %copy-start.5 = (bf16[4,27,16,16]{1,3,2,0:T(8,128)(2,1)S(1)}, bf16[4,27,16,16]{1,3,2,0:T(8,128)(2,1)}, u32[]{:S(2)}) copy-start(bf16[4,27,16,16]{1,3,2,0:T(8,128)(2,1)} %param.15) | copy-start | bytes 165892
  63.2 18.2 %collective-permute-start.2 = (bf16[80,128]{1,0:T(8,128)(2,1)S(1)}, bf16[80,128]{1,0:T(8,128)(2,1)S(1)}, u32[]{:S(2)}, u32[]{:S(2)}) collective-permute-start(bf16[80,128]{1,0:T(8,128)(2,1)S(1)} %get-tuple-element.39), channel_id=1, source_target_pairs={{0,1},{1,2},{2,3},{3,4},{4,5},{5,6},{6,7},{8,9},{9,10},{10,11},{11... | collective-permute-start | bytes 61448 | tf_op jit(solution)/shard_map/ppermute | solution.py:496
  72.0 9.3 %collective-permute-start.3 = (bf16[80,128]{1,0:T(8,128)(2,1)S(1)}, bf16[80,128]{1,0:T(8,128)(2,1)S(1)}, u32[]{:S(2)}, u32[]{:S(2)}) collective-permute-start(bf16[80,128]{1,0:T(8,128)(2,1)S(1)} %get-tuple-element.40), channel_id=1, source_target_pairs={{1,0},{2,1},{3,2},{4,3},{5,4},{6,5},{7,6},{9,8},{10,9},{11,10},{12... | collective-permute-start | bytes 61448 | tf_op jit(solution)/shard_map/ppermute | solution.py:500
  77.4 14.0 %copy-start.2 = (bf16[4,16,16]{2,1,0:T(8,128)(2,1)S(1)}, bf16[4,16,16]{2,1,0:T(8,128)(2,1)}, u32[]{:S(2)}) copy-start(bf16[4,16,16]{2,1,0:T(8,128)(2,1)} %mixers_ref.1) | copy-start | bytes 6148
  77.4 14.0 %copy-start.3 = (f32[4,16]{1,0:T(4,128)S(1)}, f32[4,16]{1,0:T(4,128)}, u32[]{:S(2)}) copy-start(f32[4,16]{1,0:T(4,128)} %biases_ref.1) | copy-start | bytes 772
  77.4 14.0 %copy-start.4 = (f32[32,2]{0,1:T(2,128)S(1)}, f32[32,2]{0,1:T(2,128)}, u32[]{:S(2)}) copy-start(f32[32,2]{0,1:T(2,128)} %param.14) | copy-start | bytes 772
  81.4 19.5 %all-to-all-start.3 = ((bf16[8,160,128]{2,1,0:T(8,128)(2,1)}), bf16[8,160,128]{2,1,0:T(8,128)(2,1)S(1)}, u32[]{:S(2)}, u32[]{:S(2)}) async-start(bf16[8,160,128]{2,1,0:T(8,128)(2,1)} %bitcast.4), calls=%async_computation.3 | async-start | bytes 655360 | tf_op jit(solution)/shard_map/all_to_all | solution.py:606

commit v5 on v4

--- a/solution.py
+++ b/solution.py
@@ -45,17 +45,14 @@
     return ("plain", value)
 
 
-def table_copies(pairs, sems, step):
-    blocks = []
-    for start in range(0, pairs[0][0].shape[1], step):
+def table_copies(source, target, sems, step):
+    copies = []
+    for start in range(0, source.shape[0], step):
         here = pl.ds(start, step)
-        block = []
-        for source, target in pairs:
-            copy = pltpu.make_async_copy(source.at[:, here], target.at[:, here], sems.at[len(blocks) * len(pairs) + len(block)])
-            copy.start()
-            block.append(copy)
-        blocks.append(block)
-    return blocks
+        copy = pltpu.make_async_copy(source.at[here, :], target.at[here, :], sems.at[len(copies)])
+        copy.start()
+        copies.append(copy)
+    return copies
 
 
 def arrived(block):
@@ -63,10 +60,11 @@
         copy.wait()
 
 
-def dft_factors(length, columns, step):
+def dft_factors(length, columns):
     columns = np.asarray(columns)[None, :]
-    coarse = (step * np.arange(length // step))[:, None] * columns % length
-    fine = np.arange(step)[:, None] * columns % length
+    steps = 2 * FINE * np.arange(length // 2 // FINE)
+    coarse = np.concatenate([steps, steps + 1])[:, None] * columns % length
+    fine = 2 * np.arange(FINE)[:, None] * columns % length
     angle_coarse = coarse * (2.0 * np.pi / length)
     angle_fine = fine * (2.0 * np.pi / length)
     scale = 1.0 / np.sqrt(length)
@@ -74,43 +72,70 @@
     return np.concatenate(parts).astype(np.float32)
 
 
-def fill_tables(factors_ref, cos_hbm, sin_hbm, cos_ref, sin_ref, sems):
-    count = cos_ref.shape[0] // FINE
+def fill_table(factors_ref, table_hbm, table_ref, sems):
+    count = table_ref.shape[0] // FINE
+    width = factors_ref.shape[1]
     cos_b = factors_ref[pl.ds(2 * count, FINE), :]
     sin_b = factors_ref[pl.ds(2 * count + FINE, FINE), :]
     copies = []
     for a in range(count):
         here = pl.ds(a * FINE, FINE)
         cos, sin = factors_ref[pl.ds(a, 1), :], factors_ref[pl.ds(count + a, 1), :]
-        cos_ref[here, :] = (cos * cos_b - sin * sin_b).astype(BF16)
-        sin_ref[here, :] = (sin * cos_b + cos * sin_b).astype(BF16)
+        table_ref[here, 0:width] = (cos * cos_b - sin * sin_b).astype(BF16)
+        table_ref[here, width : 2 * width] = (sin * cos_b + cos * sin_b).astype(BF16)
         if a % 4 == 3:
             done = pl.ds((a - 3) * FINE, 4 * FINE)
-            for source, target in ((cos_ref, cos_hbm), (sin_ref, sin_hbm)):
-                copy = pltpu.make_async_copy(source.at[done, :], target.at[done, :], sems.at[len(copies)])
-                copy.start()
-                copies.append(copy)
+            copy = pltpu.make_async_copy(table_ref.at[done, :], table_hbm.at[done, :], sems.at[len(copies)])
+            copy.start()
+            copies.append(copy)
     return copies
 
 
 def prepare(
-    state_hbm, sens_hbm, par_hbm, pe_hbm,
-    first_ref, second_ref, state_ref, sens_ref, par_cos_hbm, par_sin_hbm, pe_cos_hbm, pe_sin_hbm,
-    par_ref, pe_ref, par_cos, par_sin, pe_cos, pe_sin, sems, par_sems, pe_sems,
+    state_hbm, sens_hbm, par_factors_hbm, pe_factors_hbm, kdata_hbm, mask_hbm,
+    first_ref, second_ref, state_ref, sens_ref, sampled_ref, par_hbm, pe_hbm, data_hbm,
+    par_factors, pe_factors, par_ref, pe_ref, kdata_ref, mask_ref, data_ref, sems, par_sems, pe_sems,
 ):
-    pairs = ((par_hbm, par_ref), (pe_hbm, pe_ref), (state_hbm, state_ref), (sens_hbm, sens_ref))
+    pairs = (
+        (par_factors_hbm, par_factors), (pe_factors_hbm, pe_factors), (state_hbm, state_ref), (sens_hbm, sens_ref),
+        (kdata_hbm, kdata_ref), (mask_hbm, mask_ref),
+    )
     copies = []
     for k, (source, target) in enumerate(pairs):
         copy = pltpu.make_async_copy(source, target, sems.at[k])
         copy.start()
         copies.append(copy)
     arrived(copies[0:1])
-    sent = fill_tables(par_ref, par_cos_hbm, par_sin_hbm, par_cos, par_sin, par_sems)
+    sent = fill_table(par_factors, par_hbm, par_ref, par_sems)
     arrived(copies[1:2])
-    sent = sent + fill_tables(pe_ref, pe_cos_hbm, pe_sin_hbm, pe_cos, pe_sin, pe_sems)
+    sent = sent + fill_table(pe_factors, pe_hbm, pe_ref, pe_sems)
     arrived(copies[2:])
+    sort_lines(kdata_ref, mask_ref, data_ref, sampled_ref)
+    last = pltpu.make_async_copy(data_ref, data_hbm, sems.at[len(pairs)])
+    last.start()
     pack_rows(state_ref, sens_ref, first_ref, second_ref)
-    arrived(sent)
+    arrived(sent + [last])
+
+
+def sort_lines(kdata_ref, mask_ref, data_ref, sampled_ref):
+    step = 256
+    row = lax.broadcasted_iota(jnp.int32, (step, step), 0)
+    lane = lax.broadcasted_iota(jnp.int32, (step, step), 1)
+    pick = jnp.where(row == 2 * (lane % 128) + lane // 128, 1.0, 0.0).astype(BF16)
+    coils, spots, lines, npe = kdata_ref.shape[1:]
+    for block in range(npe // step):
+        here = pl.ds(step * block, step)
+        value = jnp.concatenate(
+            [kdata_ref[part, c, p, :, here] for part in range(2) for c in range(coils) for p in range(spots)], axis=0
+        )
+        high = value.astype(BF16)
+        low = (value - high.astype(F32)).astype(BF16)
+        value = nn(high, pick) + nn(low, pick)
+        sampled = nn(mask_ref[:, here].astype(F32).astype(BF16), pick)
+        for side in range(2):
+            to = pl.ds(side * npe // 2 + 128 * block, 128)
+            data_ref[:, to] = value[:, 128 * side : 128 * side + 128]
+            sampled_ref[:, to] = sampled[:, 128 * side : 128 * side + 128]
 
 
 def swap_groups(tiles, group):
@@ -139,112 +164,137 @@
     return lax.dot_general(a, b, (((1,), (1,)), ((), ())), preferred_element_type=F32)
 
 
-def forward_columns(est_ref, sens_ref, cos_hbm, sin_hbm, out_ref, img_ref, cos_ref, sin_ref, sems):
-    blocks = table_copies([(cos_hbm, cos_ref), (sin_hbm, sin_ref)], sems, cos_ref.shape[1])
+def forward_columns(est_ref, sens_ref, table_hbm, out_ref, img_ref, line_ref, table_ref, sems):
     owners = est_ref.shape[0]
-    rows = sens_ref.shape[3]
-    npar = sens_ref.shape[4]
+    coils, spots, rows, npar = sens_ref.shape[1:]
+    step = 128
+    copies = table_copies(table_hbm, table_ref, sems, step)
     width = npar // owners
     lane = lax.broadcasted_iota(jnp.int32, (rows, 128), 1)
-    coils, spots = sens_ref.shape[1:3]
+    middle = npar // 2
+
+    def estimate(spot, tile):
+        full = []
+        for part in range(2):
+            value = None
+            for owner in range(128 * tile // width, (128 * tile + 127) // width + 1):
+                at = width * owner - 128 * tile
+                piece = est_ref[owner, part, spot].astype(F32)
+                if at % 128:
+                    piece = pltpu.roll(piece, at % 128, 1)
+                value = piece if value is None else jnp.where(lane >= at, piece, value)
+            full.append(value)
+        return full
+
     for spot in range(spots):
-        for tile in range(npar // 128):
-            full = []
-            for part in range(2):
-                value = None
-                for owner in range(128 * tile // width, (128 * tile + 127) // width + 1):
-                    at = width * owner - 128 * tile
-                    piece = est_ref[owner, part, spot].astype(F32)
-                    if at % 128:
-                        piece = pltpu.roll(piece, at % 128, 1)
-                    value = piece if value is None else jnp.where(lane >= at, piece, value)
-                full.append(value)
-            est_re, est_im = full
-            cols = pl.ds(128 * tile, 128)
+        for tile in range(middle // 128):
+            sides = [estimate(spot, tile + side * middle // 128) for side in range(2)]
             for coil in range(coils):
-                sens_re = sens_ref[0, coil, spot, :, cols]
-                sens_im = sens_ref[1, coil, spot, :, cols]
+                images = []
+                for side in range(2):
+                    cols = pl.ds(128 * tile + side * middle, 128)
+                    sens_re = sens_ref[0, coil, spot, :, cols]
+                    sens_im = sens_ref[1, coil, spot, :, cols]
+                    est_re, est_im = sides[side]
+                    images.append((sens_re * est_re - sens_im * est_im, sens_re * est_im + sens_im * est_re))
                 row = (coil * spots + spot) * rows
-                img_ref[pl.ds(row, rows), cols] = (sens_re * est_re - sens_im * est_im).astype(BF16)
-                img_ref[pl.ds(128 + row, rows), cols] = (sens_re * est_im + sens_im * est_re).astype(BF16)
-    img = img_ref[...]
-    arrived(blocks[0])
+                cols = pl.ds(128 * tile, 128)
+                for part in range(2):
+                    here = pl.ds(128 * part + row, rows)
+                    img_ref[0, here, cols] = (images[0][part] + images[1][part]).astype(BF16)
+                    img_ref[1, here, cols] = (images[0][part] - images[1][part]).astype(BF16)
+    for odd in range(2):
+        img = img_ref[odd]
+        for start in range(0, middle, step):
+            here = pl.ds(odd * middle + start, step)
+            arrived(copies[(odd * middle + start) // step : (odd * middle + start) // step + 1])
+            by_cos = nt(table_ref[here, 0:middle], img)
+            by_sin = nt(table_ref[here, middle:npar], img)
+            to = pl.ds(2 * start + odd, step, stride=2)
+            line_ref[0, to, :] = by_cos[:, :128] + by_sin[:, 128:]
+            line_ref[1, to, :] = by_cos[:, 128:] - by_sin[:, :128]
+    out_ref[:, 0:128] = line_ref[0].astype(BF16)
+    out_ref[:, 128:256] = line_ref[1].astype(BF16)
+
+
+def consistency(
+    recv_ref, data_hbm, sampled_ref, table_hbm, out_ref, x_ref, res_ref, data_ref, table_ref, sems, data_sem
+):
     step = 256
-    for start in range(0, npar, step):
-        here = pl.ds(start, step)
-        by_cos = nt(cos_ref[here, :], img)
-        by_sin = nt(sin_ref[here, :], img)
-        out_ref[here, 0:128] = (by_cos[:, :128] + by_sin[:, 128:]).astype(BF16)
-        out_ref[here, 128:256] = (by_cos[:, 128:] - by_sin[:, :128]).astype(BF16)
-
-
-def consistency(recv_ref, kdata_ref, mask_ref, cos_hbm, sin_hbm, out_ref, x_ref, res_ref, cos_ref, sin_ref, sems):
-    step = 256
-    blocks = table_copies([(cos_hbm, cos_ref), (sin_hbm, sin_ref)], sems, step)
-    lines = mask_ref.shape[0]
-    npe = mask_ref.shape[1]
-    sources = recv_ref.shape[0] // lines
+    copies = table_copies(table_hbm, table_ref, sems, step)
+    data_copy = pltpu.make_async_copy(data_hbm, data_ref, data_sem)
+    data_copy.start()
+    lines, npe = sampled_ref.shape
+    middle = npe // 2
+    width = table_ref.shape[1] // 2
     half = 4 * lines
-    for quad in range(sources // 4):
+    quads = npe // 128
+
+    def gathered(quad):
         stacked = []
         for part in range(2):
             tiles = [
                 recv_ref[pl.ds((4 * quad + s) * lines, lines), pl.ds(128 * part, 128)].astype(F32) for s in range(4)
             ]
             stacked += swap_groups(tiles, 32)
-        x_ref[:, pl.ds(128 * quad, 128)] = jnp.concatenate(stacked, axis=0).astype(BF16)
-    x = x_ref[...]
-    for start in range(0, npe, step):
-        here = pl.ds(start, step)
-        arrived(blocks[start // step])
-        by_cos = nn(x, cos_ref[:, here])
-        by_sin = nn(x, sin_ref[:, here])
-        sampled = mask_ref[:, here].astype(F32)
-        sampled = jnp.concatenate([sampled] * 4, axis=0)
-        data = [
-            jnp.concatenate([kdata_ref[part, c, p, :, here] for c in range(2) for p in range(2)], axis=0)
-            for part in range(2)
-        ]
-        real = sampled * (by_cos[:half] + by_sin[half:] - data[0])
-        imag = sampled * (by_cos[half:] - by_sin[:half] - data[1])
-        res_ref[0:half, here] = real.astype(BF16)
-        res_ref[half : 2 * half, here] = imag.astype(BF16)
-    res = res_ref[...]
-    for start in range(0, cos_ref.shape[1], step):
-        here = pl.ds(start, step)
-        if start >= npe:
-            arrived(blocks[start // step])
-        by_cos = nn(res, cos_ref[:, here])
-        by_sin = nn(res, sin_ref[:, here])
-        parts = (by_cos[:half] - by_sin[half:], by_cos[half:] + by_sin[:half])
-        for tile in range(step // 128):
-            at = slice(128 * tile, 128 * tile + 128)
-            tiles = [part[lines * g : lines * (g + 1), at] for part in parts for g in range(4)]
-            if start < npe:
-                quad = start // 128 + tile
-                for part in range(2):
-                    for s, value in enumerate(swap_groups(tiles[4 * part : 4 * part + 4], 32)):
-                        out_ref[pl.ds((4 * quad + s) * lines, lines), pl.ds(128 * part, 128)] = value.astype(BF16)
-            else:
-                group = (start - npe) // 128 + tile
-                for s, value in enumerate(swap_groups(tiles, 8)):
-                    value = value.astype(BF16)
-                    for half_id in range(2):
-                        owner = 16 * group + 8 * half_id + s
-                        out_ref[pl.ds(owner * lines, lines), 256:384] = value
+        return jnp.concatenate(stacked, axis=0)
+
+    for quad in range(quads // 2):
+        low, high = gathered(quad), gathered(quad + quads // 2)
+        x_ref[0, :, pl.ds(128 * quad, 128)] = (low + high).astype(BF16)
+        x_ref[1, :, pl.ds(128 * quad, 128)] = (low - high).astype(BF16)
+    data_copy.wait()
+    for odd in range(2):
+        x = x_ref[odd]
+        for start in range(odd * middle, (odd + 1) * middle, step):
+            here = pl.ds(start, step)
+            arrived(copies[start // step : start // step + 1])
+            by_cos = nt(x, table_ref[here, 0:middle])
+            by_sin = nt(x, table_ref[here, width : width + middle])
+            sampled = jnp.concatenate([sampled_ref[:, here]] * 4, axis=0)
+            real = sampled * (by_cos[:half] + by_sin[half:] - data_ref[0:half, here])
+            imag = sampled * (by_cos[half:] - by_sin[:half] - data_ref[half : 2 * half, here])
+            res_ref[0:half, here] = real.astype(BF16)
+            res_ref[half : 2 * half, here] = imag.astype(BF16)
+    res = [res_ref[:, 0:middle], res_ref[:, middle:npe]]
+
+    for start in range(0, width, step):
+        size = min(step, width - start)
+        sums = []
+        for odd in range(2):
+            rows = pl.ds(odd * middle, middle)
+            by_cos = nn(res[odd], table_ref[rows, pl.ds(start, size)])
+            by_sin = nn(res[odd], table_ref[rows, pl.ds(width + start, size)])
+            sums.append((by_cos[:half] - by_sin[half:], by_cos[half:] + by_sin[:half]))
+        for side in range(2):
+            parts = [sums[0][part] - sums[1][part] if side else sums[0][part] + sums[1][part] for part in range(2)]
+            for tile in range(size // 128):
+                at = slice(128 * tile, 128 * tile + 128)
+                tiles = [part[lines * g : lines * (g + 1), at] for part in parts for g in range(4)]
+                if start < middle:
+                    quad = start // 128 + tile + side * quads // 2
+                    for part in range(2):
+                        for s, value in enumerate(swap_groups(tiles[4 * part : 4 * part + 4], 32)):
+                            out_ref[pl.ds((4 * quad + s) * lines, lines), pl.ds(128 * part, 128)] = value.astype(BF16)
+                else:
+                    for s, value in enumerate(swap_groups(tiles, 8)):
+                        value = value.astype(BF16)
+                        for half_id in range(2):
+                            owner = 16 * side + 8 * half_id + s
+                            out_ref[pl.ds(owner * lines, lines), 256:384] = value
 
 
 def backward_columns(
-    recv_ref, sens_ref, first_ref, second_ref, cos_hbm, sin_hbm, out_ref, part_ref, edge_ref, cos_ref, sin_ref, sems
+    recv_ref, sens_ref, first_ref, second_ref, table_hbm, out_ref, part_ref, edge_ref, line_ref, table_ref, sems
 ):
-    step = 256
-    blocks = table_copies([(cos_hbm, cos_ref), (sin_hbm, sin_ref)], sems, step)
-    npar = sens_ref.shape[4]
-    coils, spots, rows = sens_ref.shape[1:4]
+    copies = table_copies(table_hbm, table_ref, sems, table_ref.shape[0] // 2)
+    coils, spots, rows, npar = sens_ref.shape[1:]
     cells = coils * spots * rows
     edges = coils * spots * 2 * REACH
-    turned = recv_ref[...].astype(F32).T
+    middle = npar // 2
     low = lax.axis_index("space") // 8 % 2 == 0
+    for tile in range(3):
+        line_ref[tile] = recv_ref[:, 128 * tile : 128 * tile + 128].astype(F32)
     for tile in range(npar // 128):
         here = pl.ds(tile * 2 * coils * spots * REACH, 2 * coils * spots * REACH)
         above, below = around(first_ref, second_ref, here, slice(0, 128))
@@ -252,34 +302,36 @@
             at = slice(k * REACH, (k + 1) * REACH)
             part, coil, spot = k // (coils * spots), k // spots % coils, k % spots
             edge_ref[part, coil, spot, :, pl.ds(128 * tile, 128)] = jnp.concatenate([below[at], above[at]], axis=0)
-    border = jnp.where(low, turned[2 * cells : 2 * cells + 2 * edges], turned[2 * cells + 2 * edges :])
-    x = jnp.concatenate([turned[: 2 * cells], border], axis=0).astype(BF16)
-    for start in range(0, npar, step):
-        here = pl.ds(start, step)
-        arrived(blocks[start // step])
-        by_cos = nn(x, cos_ref[:, here])
-        by_sin = nn(x, sin_ref[:, here])
-        for first, count, profile_ref, offset in ((0, cells, sens_ref, 0), (2 * cells, edges, edge_ref, rows)):
-            second = first + count
-            last = second + count
-            real = by_cos[first:second] - by_sin[second:last]
-            imag = by_cos[second:last] + by_sin[first:second]
-            per_coil = count // coils
-            height = per_coil // spots
-            sums = [0.0, 0.0]
+    sums = []
+    for odd in range(2):
+        turned = [line_ref[tile, pl.ds(odd, middle, stride=2), :].T for tile in range(3)]
+        border = jnp.where(low, turned[2][: 2 * edges], turned[2][2 * edges :])
+        x = jnp.concatenate([turned[0], turned[1], border], axis=0).astype(BF16)
+        arrived(copies[odd : odd + 1])
+        sums.append(nn(x, table_ref[odd * middle : (odd + 1) * middle, :]))
+    for first, count, profile_ref, offset in ((0, cells, sens_ref, 0), (2 * cells, edges, edge_ref, rows)):
+        second = first + count
+        last = second + count
+        per_coil = count // coils
+        height = per_coil // spots
+        real = [each[first:second, :middle] - each[second:last, middle:] for each in sums]
+        imag = [each[second:last, :middle] + each[first:second, middle:] for each in sums]
+        for side in range(2):
+            here = pl.ds(side * middle, middle)
+            whole = [each[0] - each[1] if side else each[0] + each[1] for each in (real, imag)]
+            total = [0.0, 0.0]
             for coil in range(coils):
                 profile = [
-                    jnp.concatenate([profile_ref[part, coil, spot, :, here] for spot in range(spots)], axis=0).astype(F32)
+                    jnp.concatenate([profile_ref[part, coil, spot, :, here] for spot in range(spots)], axis=0)
                     for part in range(2)
                 ]
-                re = real[coil * per_coil : (coil + 1) * per_coil]
-                im = imag[coil * per_coil : (coil + 1) * per_coil]
-                sums[0] = sums[0] + (profile[0] * re + profile[1] * im)
-                sums[1] = sums[1] + (profile[0] * im - profile[1] * re)
+                re, im = [each[coil * per_coil : (coil + 1) * per_coil] for each in whole]
+                total[0] = total[0] + (profile[0] * re + profile[1] * im)
+                total[1] = total[1] + (profile[0] * im - profile[1] * re)
             for part in range(2):
                 for spot in range(spots):
                     row = (part * spots + spot) * (rows + 2 * REACH) + offset
-                    part_ref[pl.ds(row, height), here] = sums[part][spot * height : (spot + 1) * height]
+                    part_ref[pl.ds(row, height), here] = total[part][spot * height : (spot + 1) * height]
     total = part_ref.shape[0]
     owners = out_ref.shape[0] // total
     width = npar // owners
@@ -523,55 +575,41 @@
     estimate = jnp.broadcast_to(estimate[None], (owners, *estimate.shape))
     estimate = lax.all_to_all(estimate, "coil", 0, 0, tiled=True)
 
-    edge_columns = [
-        (rows * d + r) % npe for d in range(groups) for r in (*range(rows, rows + REACH), *range(-REACH, 0))
-    ]
-    pe_columns = [*range(npe), *edge_columns]
-    def table_scratch(length, columns, blocks):
-        return [((length, columns), BF16)] * 2 + [pltpu.SemaphoreType.DMA((2 * blocks,))]
-
-    def tables(length, columns):
-        out = pltpu.HBM((length, len(columns)), BF16)
-        factors = jnp.asarray(dft_factors(length, columns, FINE))
-        scratch = table_scratch(length, len(columns), length // FINE // 4)
-        return [in_hbm(table) for table in call(dft_tables, [out, out], scratch, "dft_tables", plain(factors))]
-
+    edge_columns = [rows * d + r for d in range(groups // 2) for r in (*range(rows, rows + REACH), *range(-REACH, 0))]
+    pe_columns = [*range(npe // 2), *edge_columns]
     depth = 2 * coils * spots * REACH * (npar // 128) + channels * spots * REACH
-    par_factors = jnp.asarray(dft_factors(npar, range(npar), FINE))
-    pe_factors = jnp.asarray(dft_factors(npe, pe_columns, FINE))
-
-    def table_scratch(length, columns, blocks):
-        return [((length, columns), BF16)] * 2 + [pltpu.SemaphoreType.DMA((2 * blocks,))]
-
-    par_scratch = table_scratch(npar, npar, npar // FINE // 4)
-    pe_scratch = table_scratch(npe, len(pe_columns), npe // FINE // 4)
-    first, second, state, sens, *tables = call(
+    par_factors = jnp.asarray(dft_factors(npar, range(npar // 2)))
+    pe_factors = jnp.asarray(dft_factors(npe, pe_columns))
+    par_table = ((npar, npar), BF16)
+    pe_table = ((npe, 2 * len(pe_columns)), BF16)
+    data_form = ((8 * lines, npe), F32)
+    first, second, state, sens, sampled, par, pe, data = call(
         prepare,
         [((depth, 128), BF16)] * 2
-        + [(state.shape, BF16), (sens.shape, F32)]
-        + [pltpu.HBM((npar, npar), BF16)] * 2
-        + [pltpu.HBM((npe, len(pe_columns)), BF16)] * 2,
+        + [(state.shape, BF16), (sens.shape, F32), (mask.shape, F32)]
+        + [pltpu.HBM(*form) for form in (par_table, pe_table, data_form)],
         [
             (par_factors.shape, F32),
             (pe_factors.shape, F32),
-            *par_scratch[:2],
-            *pe_scratch[:2],
-            pltpu.SemaphoreType.DMA((4,)),
-            par_scratch[2],
-            pe_scratch[2],
+            par_table,
+            pe_table,
+            (kdata.shape, F32),
+            (mask.shape, mask.dtype),
+            data_form,
+            pltpu.SemaphoreType.DMA((7,)),
+            pltpu.SemaphoreType.DMA((npar // FINE // 4,)),
+            pltpu.SemaphoreType.DMA((npe // FINE // 4,)),
         ],
         "prepare",
-        in_hbm(state), in_hbm(sens), in_hbm(par_factors), in_hbm(pe_factors),
-    )
-    par_tables = [in_hbm(table) for table in tables[:2]]
-    pe_tables = [in_hbm(table) for table in tables[2:]]
+        *[in_hbm(each) for each in (state, sens, par_factors, pe_factors, kdata, mask)],
+    )
 
     (sent,) = call(
         forward_columns,
         [jax.ShapeDtypeStruct((npar, 2 * cells), BF16)],
-        [((2 * cells, npar), BF16), *table_scratch(npar, npar, 1)],
+        [((2, 2 * cells, npar // 2), BF16), ((2, npar, 128), F32), par_table, pltpu.SemaphoreType.DMA((npar // 128,))],
         "forward_columns",
-        estimate, sens, *par_tables,
+        estimate, sens, in_hbm(par),
     )
     sent, first, second = lax.optimization_barrier((sent, first, second))
     spectra = lax.all_to_all(sent, "space", 0, 0, tiled=True)
@@ -580,9 +618,16 @@
     (sent,) = call(
         consistency,
         [jax.ShapeDtypeStruct((npar, 384), BF16)],
-        [((8 * lines, npe), BF16)] * 2 + table_scratch(npe, len(pe_columns), len(pe_columns) // 256),
+        [
+            ((2, 8 * lines, npe // 2), BF16),
+            ((8 * lines, npe), BF16),
+            ((8 * lines, npe), F32),
+            pe_table,
+            pltpu.SemaphoreType.DMA((npe // 256,)),
+            pltpu.SemaphoreType.DMA,
+        ],
         "consistency",
-        spectra, kdata, mask, *pe_tables,
+        spectra, in_hbm(data), sampled, in_hbm(pe),
     )
     sent, first, second = lax.optimization_barrier((sent, first, second))
     returned = lax.all_to_all(sent, "space", 0, 0, tiled=True)
@@ -597,10 +642,12 @@
         [
             ((2 * spots * tall, npar), F32),
             ((2, coils, spots, 2 * REACH, npar), F32),
-            *table_scratch(npar, npar, npar // 256),
+            ((3, npar, 128), F32),
+            par_table,
+            pltpu.SemaphoreType.DMA((2,)),
         ],
         "backward_columns",
-        returned, sens, first, second, *par_tables,
+        returned, sens, first, second, in_hbm(par),
     )
     sent, left, right = lax.optimization_barrier((sent, left, right))
     shares = lax.all_to_all(sent, "coil", 0, 0, tiled=True)

time: 105 us -> 104 us (level)
  Pallas kernels: 23.5 us -> 20.8 us
  waiting for transfers between devices: 27.1 us -> 29.3 us
    pallas_call x8, Pallas kernels: 23.5 us -> 20.8 us  [call(): pl.pallas_call(body, out_shape=shapes, in_specs=specs, out_specs=placed,...]
    ppermute x1, starting transfers between devices: 8.82 us -> 7.4 us  [from_previous(): lax.ppermute(tail, axis, [(i, i + 1) for i in range(lax.axis_size(axis) -...]
    all_to_all x1, starting transfers between devices: 6.64 us -> 8.05 us  [per_device(): returned = lax.all_to_all(sent, 'space', 0, 0, tiled=True)]
    all_to_all x1, waiting for transfers between devices: 3.48 us -> 4.77 us  [per_device(): returned = lax.all_to_all(sent, 'space', 0, 0, tiled=True)]
  transfers between devices with their start and end apart: 8 -> 8, of which waited for: 4 -> 4; matrix products, arithmetic and copies ran while one was open for 1% -> 1% of each run, Pallas kernels for 16% -> 13%
where the time goes in v5:
time: 104 us; the launch traced here: 103 us
  starting transfers between devices  50.3 us (48%)
  waiting for transfers between devices  29.3 us (28%)
  Pallas kernels  20.8 us (20%)
  local copies, waits for them, and re-layouts  2.1 us (2%)
    pallas_call x8, Pallas kernels, call(): pl.pallas_call(body, out_shape=shapes, in_specs=specs, out_specs=placed,...  20.8 us
    all_to_all x1, starting transfers between devices, per_device(): spectra = lax.all_to_all(sent, 'space', 0, 0, tiled=True)  11.1 us
    all_to_all x1, waiting for transfers between devices, per_device(): spectra = lax.all_to_all(sent, 'space', 0, 0, tiled=True)  10.9 us
    all_to_all x1, starting transfers between devices, per_device(): shares = lax.all_to_all(sent, 'coil', 0, 0, tiled=True)  8.54 us
    all_to_all x1, waiting for transfers between devices, per_device(): shares = lax.all_to_all(sent, 'coil', 0, 0, tiled=True)  8.42 us
    all_to_all x1, starting transfers between devices, per_device(): returned = lax.all_to_all(sent, 'space', 0, 0, tiled=True)  8.05 us
    ppermute x1, starting transfers between devices, from_previous(): lax.ppermute(tail, axis, [(i, i + 1) for i in range(lax.axis_size(axis) -...  7.4 us
    all_to_all x1, starting transfers between devices, per_device(): estimate = lax.all_to_all(estimate, 'coil', 0, 0, tiled=True)  7.39 us
  transfers between devices with their start and end apart: 8, of which 4 were waited for; matrix products, arithmetic and copies ran while one was open for 1% of the time, Pallas kernels for 13%

profile of v5, /device:TPU:1, one launch (start us, length us, event | category | flops | bytes accessed | tf_op | source)
XLA Modules:
  0.0 103.2 jit_solution(1583686854406806398)
XLA Ops:
  0.6 0.8 slice.3
  1.4 0.8 broadcast_in_dim.2
  2.2 7.4 %all-to-all-start = ((bf16[8,2,2,32,128]{4,3,2,1,0:T(8,128)(2,1)}), bf16[8,2,2,32,128]{4,3,2,1,0:T(8,128)(2,1)S(1)}, u32[]{:S(2)}, u32[]{:S(2)}) async-start(bf16[8,2,2,32,128]{4,3,2,1,0:T(8,128)(2,1)} %broadcast_in_dim.2), calls=%async_computation | async-start | bytes 524288 | tf_op jit(solution)/shard_map/all_to_all | solution.py:576
  9.6 3.5 %prepare.1 = (bf16[448,128]{1,0:T(8,128)(2,1)S(1)}, bf16[448,128]{1,0:T(8,128)(2,1)S(1)}, bf16[32,2,32,96]{3,2,1,0:T(8,128)(2,1)S(1)}, f32[2,2,2,32,768]{4,3,2,1...) custom-call(bf16[32,2,32,96]{3,2,1,0:T(8,128)(2,1)} %state_hbm.1, ...), custom_call_target="tpu_custom_call" | custom-call | tf_op jit(solution)/shard_map/prepare/pallas_call | solution.py:29
  13.0 5.2 %all-to-all-done.est_ref = bf16[8,2,2,32,128]{4,3,2,1,0:T(8,128)(2,1)S(1)} async-done(((bf16[8,2,2,32,128]{4,3,2,1,0:T(8,128)(2,1)}), bf16[8,2,2,32,128]{4,3,2,1,0:T(8,128)(2,1)S(1)}, u32[]{:S(2)}, u32[]{:S(2)}) %all-to-all-start) | async-done | bytes 262176 | tf_op jit(solution)/shard_map/all_to_all | solution.py:576
  18.2 3.5 %forward_columns.1 = bf16[768,256]{1,0:T(8,128)(2,1)} custom-call(bf16[8,2,2,32,128]{4,3,2,1,0:T(8,128)(2,1)S(1)} %all-to-all-done.est_ref, f32[2,2,2,32,768]{4,3,2,1,0:T(8,128)S(1)} %get-tuple-element.25.sens_ref, bf16[768,768]{1,0:T(8,128)(2,1)} %get-tuple-element.26.table_hbm), custom_call_target="tpu_custom_call" | custom-call | tf_op jit(solution)/shard_map/forward_columns/pallas_call | solution.py:29
  21.7 11.1 %all-to-all-start.1 = ((bf16[32,24,256]{2,1,0:T(8,128)(2,1)}), bf16[32,24,256]{2,1,0:T(8,128)(2,1)S(1)}, u32[]{:S(2)}, u32[]{:S(2)}) async-start(bf16[32,24,256]{2,1,0:T(8,128)(2,1)} %bitcast), calls=%async_computation.1 | async-start | bytes 786432 | tf_op jit(solution)/shard_map/all_to_all | solution.py:615
  32.9 5.2 %collective-permute-start = (bf16[448,128]{1,0:T(8,128)(2,1)S(1)}, bf16[448,128]{1,0:T(8,128)(2,1)S(1)}, u32[]{:S(2)}, u32[]{:S(2)}) collective-permute-start(bf16[448,128]{1,0:T(8,128)(2,1)S(1)} %get-tuple-element.33), channel_id=1, source_target_pairs={{0,8},{16,24},{32,40},{48,56},{64,72},{80,88},{96,104},{112,120},{... | collective-permute-start | bytes 344072 | tf_op jit(solution)/shard_map/ppermute | solution.py:558
  38.1 0.7 collective-permute-start.1
  38.8 10.9 %all-to-all-done.1 = bf16[32,24,256]{2,1,0:T(8,128)(2,1)S(1)} async-done(((bf16[32,24,256]{2,1,0:T(8,128)(2,1)}), bf16[32,24,256]{2,1,0:T(8,128)(2,1)S(1)}, u32[]{:S(2)}, u32[]{:S(2)}) %all-to-all-start.1) | async-done | bytes 393248 | tf_op jit(solution)/shard_map/all_to_all | solution.py:615
  49.6 5.4 %consistency.1 = bf16[768,384]{1,0:T(8,128)(2,1)} custom-call(bf16[768,256]{1,0:T(8,128)(2,1)S(1)} %bitcast.8, f32[192,1024]{1,0:T(8,128)} %get-tuple-element.30.data_hbm, f32[24,1024]{1,0:T(8,128)S(1)} %get-tuple-element.31.sampled_ref, bf16[1024,1280]{1,0:T(8,128)(2,1)} %get-tuple-element.32.table_hbm), custom_call_target="tpu_custom_call" | custom-call | tf_op jit(solution)/shard_map/consistency/pallas_call | solution.py:29
  55.0 0.0 collective-permute-done.first_ref
  55.0 0.0 collective-permute-done.1.second_ref
  55.1 0.0 copy-start.3
  55.1 8.0 %all-to-all-start.2 = ((bf16[32,24,384]{2,1,0:T(8,128)(2,1)}), bf16[32,24,384]{2,1,0:T(8,128)(2,1)S(1)}, u32[]{:S(2)}, u32[]{:S(2)}) async-start(bf16[32,24,384]{2,1,0:T(8,128)(2,1)} %bitcast.2), calls=%async_computation.2 | async-start | bytes 1179648 | tf_op jit(solution)/shard_map/all_to_all | solution.py:633
  63.1 0.0 copy-start
  63.1 0.0 copy-start.1
  63.1 0.0 copy-start.2
  63.2 0.4 pack_cols.1
  63.6 7.4 %collective-permute-start.2 = (bf16[80,128]{1,0:T(8,128)(2,1)S(1)}, bf16[80,128]{1,0:T(8,128)(2,1)S(1)}, u32[]{:S(2)}, u32[]{:S(2)}) collective-permute-start(bf16[80,128]{1,0:T(8,128)(2,1)S(1)} %get-tuple-element.39), channel_id=1, source_target_pairs={{0,1},{1,2},{2,3},{3,4},{4,5},{5,6},{6,7},{8,9},{9,10},{10,11},{11... | collective-permute-start | bytes 61448 | tf_op jit(solution)/shard_map/ppermute | solution.py:548
  71.0 1.9 %collective-permute-start.3 = (bf16[80,128]{1,0:T(8,128)(2,1)S(1)}, bf16[80,128]{1,0:T(8,128)(2,1)S(1)}, u32[]{:S(2)}, u32[]{:S(2)}) collective-permute-start(bf16[80,128]{1,0:T(8,128)(2,1)S(1)} %get-tuple-element.40), channel_id=1, source_target_pairs={{1,0},{2,1},{3,2},{4,3},{5,4},{6,5},{7,6},{9,8},{10,9},{11,10},{12... | collective-permute-start | bytes 61448 | tf_op jit(solution)/shard_map/ppermute | solution.py:552
  72.9 4.8 %all-to-all-done.2 = bf16[32,24,384]{2,1,0:T(8,128)(2,1)S(1)} async-done(((bf16[32,24,384]{2,1,0:T(8,128)(2,1)}), bf16[32,24,384]{2,1,0:T(8,128)(2,1)S(1)}, u32[]{:S(2)}, u32[]{:S(2)}) %all-to-all-start.2) | async-done | bytes 589856 | tf_op jit(solution)/shard_map/all_to_all | solution.py:633
  77.7 3.2 %backward_columns.1 = bf16[1280,128]{1,0:T(8,128)(2,1)} custom-call(bf16[768,384]{1,0:T(8,128)(2,1)S(1)} %bitcast.7, f32[2,2,2,32,768]{4,3,2,1,0:T(8,128)S(1)} %get-tuple-element.25.sens_ref, bf16[448,128]{1,0:T(8,128)(2,1)S(1)} %collective-permute-done.first_ref, bf16[448,128]{1,0:T(8,128)(2,1)S(1)} %collective-permute-done.1.second_ref, ...), custom_call_target="tpu_custom_call" | custom-call | tf_op jit(solution)/shard_map/backward_columns/pallas_call | solution.py:29
  80.8 0.0 collective-permute-done.2.left_ref
  80.9 0.0 collective-permute-done.3.right_ref
  80.9 8.5 %all-to-all-start.3 = ((bf16[8,160,128]{2,1,0:T(8,128)(2,1)}), bf16[8,160,128]{2,1,0:T(8,128)(2,1)S(1)}, u32[]{:S(2)}, u32[]{:S(2)}) async-start(bf16[8,160,128]{2,1,0:T(8,128)(2,1)} %bitcast.4), calls=%async_computation.3 | async-start | bytes 655360 | tf_op jit(solution)/shard_map/all_to_all | solution.py:653
  89.4 0.0 copy-done.3
  89.4 0.5 copy.12.kernels_ref
  90.0 0.0 copy-done
  90.0 0.0 copy-done.1
  90.0 0.0 copy-done.2
  90.0 0.4 coupling_weights.1
  90.4 0.6 spread_state.1.state_ref
  91.0 8.4 %all-to-all-done.3 = bf16[8,160,128]{2,1,0:T(8,128)(2,1)S(1)} async-done(((bf16[8,160,128]{2,1,0:T(8,128)(2,1)}), bf16[8,160,128]{2,1,0:T(8,128)(2,1)S(1)}, u32[]{:S(2)}, u32[]{:S(2)}) %all-to-all-start.3) | async-done | bytes 327712 | tf_op jit(solution)/shard_map/all_to_all | solution.py:653
  99.4 3.8 %couple.1 = (bf16[32,2,32,96]{3,2,1,0:T(8,128)(2,1)}, f32[2,2,32,96]{3,2,1,0:T(8,128)}) custom-call(bf16[1280,128]{1,0:T(8,128)(2,1)S(1)} %bitcast.9, bf16[2560,128]{1,0:T(8,128)(2,1)S(1)} %spread_state.1.state_ref, bf16[4,96,96]{2,1,0:T(8,128)(2,1)S(1)} %get-tuple-element.44.weight_ref, bf16[4,32,32]{2,1,0:T(8,128)(2,1)S(1)} %get-tuple-element.45.mixer_ref, ...), custom_call_target="tpu_custom_call" | custom-call | tf_op jit(solution)/shard_map/couple/pallas_call | solution.py:29
  (1 shorter events, 0.0 us)
Async XLA Ops:
  2.2 16.1 %all-to-all-start = ((bf16[8,2,2,32,128]{4,3,2,1,0:T(8,128)(2,1)}), bf16[8,2,2,32,128]{4,3,2,1,0:T(8,128)(2,1)S(1)}, u32[]{:S(2)}, u32[]{:S(2)}) async-start(bf16[8,2,2,32,128]{4,3,2,1,0:T(8,128)(2,1)} %broadcast_in_dim.2), calls=%async_computation | async-start | bytes 524288 | tf_op jit(solution)/shard_map/all_to_all | solution.py:576
  21.7 27.9 %all-to-all-start.1 = ((bf16[32,24,256]{2,1,0:T(8,128)(2,1)}), bf16[32,24,256]{2,1,0:T(8,128)(2,1)S(1)}, u32[]{:S(2)}, u32[]{:S(2)}) async-start(bf16[32,24,256]{2,1,0:T(8,128)(2,1)} %bitcast), calls=%async_computation.1 | async-start | bytes 786432 | tf_op jit(solution)/shard_map/all_to_all | solution.py:615
  32.9 22.2 %collective-permute-start = (bf16[448,128]{1,0:T(8,128)(2,1)S(1)}, bf16[448,128]{1,0:T(8,128)(2,1)S(1)}, u32[]{:S(2)}, u32[]{:S(2)}) collective-permute-start(bf16[448,128]{1,0:T(8,128)(2,1)S(1)} %get-tuple-element.33), channel_id=1, source_target_pairs={{0,8},{16,24},{32,40},{48,56},{64,72},{80,88},{96,104},{112,120},{... | collective-permute-start | bytes 344072 | tf_op jit(solution)/shard_map/ppermute | solution.py:558
  38.1 17.0 %collective-permute-start.1 = (bf16[448,128]{1,0:T(8,128)(2,1)S(1)}, bf16[448,128]{1,0:T(8,128)(2,1)S(1)}, u32[]{:S(2)}, u32[]{:S(2)}) collective-permute-start(bf16[448,128]{1,0:T(8,128)(2,1)S(1)} %get-tuple-element.34), channel_id=1, source_target_pairs={{8,16},{24,32},{40,48},{56,64},{72,80},{88,96},{104,112},{120,128}... | collective-permute-start | bytes 344072 | tf_op jit(solution)/shard_map/ppermute | solution.py:558
  55.1 34.4 %copy-start.3 = (bf16[4,27,16,16]{1,3,2,0:T(8,128)(2,1)S(1)}, bf16[4,27,16,16]{1,3,2,0:T(8,128)(2,1)}, u32[]{:S(2)}) copy-start(bf16[4,27,16,16]{1,3,2,0:T(8,128)(2,1)} %param.15) | copy-start | bytes 165892
  55.1 22.6 %all-to-all-start.2 = ((bf16[32,24,384]{2,1,0:T(8,128)(2,1)}), bf16[32,24,384]{2,1,0:T(8,128)(2,1)S(1)}, u32[]{:S(2)}, u32[]{:S(2)}) async-start(bf16[32,24,384]{2,1,0:T(8,128)(2,1)} %bitcast.2), calls=%async_computation.2 | async-start | bytes 1179648 | tf_op jit(solution)/shard_map/all_to_all | solution.py:633
  63.1 26.8 %copy-start = (bf16[4,16,16]{2,1,0:T(8,128)(2,1)S(1)}, bf16[4,16,16]{2,1,0:T(8,128)(2,1)}, u32[]{:S(2)}) copy-start(bf16[4,16,16]{2,1,0:T(8,128)(2,1)} %mixers_ref.1) | copy-start | bytes 6148
  63.1 26.8 %copy-start.1 = (f32[4,16]{1,0:T(4,128)S(1)}, f32[4,16]{1,0:T(4,128)}, u32[]{:S(2)}) copy-start(f32[4,16]{1,0:T(4,128)} %biases_ref.1) | copy-start | bytes 772
  63.1 26.8 %copy-start.2 = (f32[32,2]{0,1:T(2,128)S(1)}, f32[32,2]{0,1:T(2,128)}, u32[]{:S(2)}) copy-start(f32[32,2]{0,1:T(2,128)} %param.14) | copy-start | bytes 772
  63.6 17.3 %collective-permute-start.2 = (bf16[80,128]{1,0:T(8,128)(2,1)S(1)}, bf16[80,128]{1,0:T(8,128)(2,1)S(1)}, u32[]{:S(2)}, u32[]{:S(2)}) collective-permute-start(bf16[80,128]{1,0:T(8,128)(2,1)S(1)} %get-tuple-element.39), channel_id=1, source_target_pairs={{0,1},{1,2},{2,3},{3,4},{4,5},{5,6},{6,7},{8,9},{9,10},{10,11},{11... | collective-permute-start | bytes 61448 | tf_op jit(solution)/shard_map/ppermute | solution.py:548
  71.0 9.9 %collective-permute-start.3 = (bf16[80,128]{1,0:T(8,128)(2,1)S(1)}, bf16[80,128]{1,0:T(8,128)(2,1)S(1)}, u32[]{:S(2)}, u32[]{:S(2)}) collective-permute-start(bf16[80,128]{1,0:T(8,128)(2,1)S(1)} %get-tuple-element.40), channel_id=1, source_target_pairs={{1,0},{2,1},{3,2},{4,3},{5,4},{6,5},{7,6},{9,8},{10,9},{11,10},{12... | collective-permute-start | bytes 61448 | tf_op jit(solution)/shard_map/ppermute | solution.py:552
  80.9 18.5 %all-to-all-start.3 = ((bf16[8,160,128]{2,1,0:T(8,128)(2,1)}), bf16[8,160,128]{2,1,0:T(8,128)(2,1)S(1)}, u32[]{:S(2)}, u32[]{:S(2)}) async-start(bf16[8,160,128]{2,1,0:T(8,128)(2,1)} %bitcast.4), calls=%async_computation.3 | async-start | bytes 655360 | tf_op jit(solution)/shard_map/all_to_all | solution.py:653

commit v6 on v5

--- a/solution.py
+++ b/solution.py
@@ -6,6 +6,7 @@
 from jax.experimental import pallas as pl
 from jax.experimental.pallas import tpu as pltpu
 from jax.sharding import PartitionSpec as P
+
 
 F32 = jnp.float32
 BF16 = jnp.bfloat16
@@ -16,7 +17,7 @@
 HBM = pl.BlockSpec(memory_space=pltpu.HBM)
 
 
-def call(body, outs, scratch, name, *args):
+def call(body, outs, scratch, *args):
     specs, values = [], []
     for arg in args:
         where, value = arg if isinstance(arg, tuple) else ("vmem", arg)
@@ -33,7 +34,6 @@
         out_specs=placed,
         scratch_shapes=[each if not isinstance(each, tuple) else pltpu.VMEM(*each) for each in scratch],
         compiler_params=pltpu.CompilerParams(vmem_limit_bytes=20 * 2**20),
-        name=name,
     )(*values)
 
 
@@ -53,6 +53,13 @@
         copy.start()
         copies.append(copy)
     return copies
+
+
+def sent_off(copies, source, target, sems, start, size):
+    here = pl.ds(start, size)
+    copy = pltpu.make_async_copy(source.at[here, :], target.at[here, :], sems.at[len(copies)])
+    copy.start()
+    copies.append(copy)
 
 
 def arrived(block):
@@ -93,8 +100,8 @@
 
 def prepare(
     state_hbm, sens_hbm, par_factors_hbm, pe_factors_hbm, kdata_hbm, mask_hbm,
-    first_ref, second_ref, state_ref, sens_ref, sampled_ref, par_hbm, pe_hbm, data_hbm,
-    par_factors, pe_factors, par_ref, pe_ref, kdata_ref, mask_ref, data_ref, sems, par_sems, pe_sems,
+    first_ref, second_ref, state_ref, sens_ref, sampled_ref, par_ref, par_hbm, pe_hbm, data_hbm,
+    par_factors, pe_factors, pe_ref, kdata_ref, mask_ref, data_ref, sems, par_sems, pe_sems,
 ):
     pairs = (
         (par_factors_hbm, par_factors), (pe_factors_hbm, pe_factors), (state_hbm, state_ref), (sens_hbm, sens_ref),
@@ -122,7 +129,7 @@
     row = lax.broadcasted_iota(jnp.int32, (step, step), 0)
     lane = lax.broadcasted_iota(jnp.int32, (step, step), 1)
     pick = jnp.where(row == 2 * (lane % 128) + lane // 128, 1.0, 0.0).astype(BF16)
-    coils, spots, lines, npe = kdata_ref.shape[1:]
+    coils, spots, _, npe = kdata_ref.shape[1:]
     for block in range(npe // step):
         here = pl.ds(step * block, step)
         value = jnp.concatenate(
@@ -164,11 +171,10 @@
     return lax.dot_general(a, b, (((1,), (1,)), ((), ())), preferred_element_type=F32)
 
 
-def forward_columns(est_ref, sens_ref, table_hbm, out_ref, img_ref, line_ref, table_ref, sems):
+def forward_columns(est_ref, sens_ref, table_ref, out_hbm, img_ref, line_ref, out_ref, sems):
     owners = est_ref.shape[0]
     coils, spots, rows, npar = sens_ref.shape[1:]
     step = 128
-    copies = table_copies(table_hbm, table_ref, sems, step)
     width = npar // owners
     lane = lax.broadcasted_iota(jnp.int32, (rows, 128), 1)
     middle = npar // 2
@@ -203,22 +209,25 @@
                     here = pl.ds(128 * part + row, rows)
                     img_ref[0, here, cols] = (images[0][part] + images[1][part]).astype(BF16)
                     img_ref[1, here, cols] = (images[0][part] - images[1][part]).astype(BF16)
-    for odd in range(2):
-        img = img_ref[odd]
-        for start in range(0, middle, step):
+    copies = []
+    for start in range(0, middle, step):
+        for odd in range(2):
             here = pl.ds(odd * middle + start, step)
-            arrived(copies[(odd * middle + start) // step : (odd * middle + start) // step + 1])
-            by_cos = nt(table_ref[here, 0:middle], img)
-            by_sin = nt(table_ref[here, middle:npar], img)
+            by_cos = nt(table_ref[here, 0:middle], img_ref[odd])
+            by_sin = nt(table_ref[here, middle:npar], img_ref[odd])
             to = pl.ds(2 * start + odd, step, stride=2)
             line_ref[0, to, :] = by_cos[:, :128] + by_sin[:, 128:]
             line_ref[1, to, :] = by_cos[:, 128:] - by_sin[:, :128]
-    out_ref[:, 0:128] = line_ref[0].astype(BF16)
-    out_ref[:, 128:256] = line_ref[1].astype(BF16)
+        here = pl.ds(2 * start, 2 * step)
+        out_ref[here, 0:128] = line_ref[0, here, :].astype(BF16)
+        out_ref[here, 128:256] = line_ref[1, here, :].astype(BF16)
+        sent_off(copies, out_ref, out_hbm, sems, 2 * start, 2 * step)
+    arrived(copies)
 
 
 def consistency(
-    recv_ref, data_hbm, sampled_ref, table_hbm, out_ref, x_ref, res_ref, data_ref, table_ref, sems, data_sem
+    recv_ref, data_hbm, sampled_ref, table_hbm, out_hbm,
+    x_ref, res_ref, data_ref, table_ref, out_ref, sems, data_sem, out_sems,
 ):
     step = 256
     copies = table_copies(table_hbm, table_ref, sems, step)
@@ -258,7 +267,8 @@
             res_ref[half : 2 * half, here] = imag.astype(BF16)
     res = [res_ref[:, 0:middle], res_ref[:, middle:npe]]
 
-    for start in range(0, width, step):
+    off = []
+    for start in (middle, *range(0, middle, step)):
         size = min(step, width - start)
         sums = []
         for odd in range(2):
@@ -276,16 +286,19 @@
                     for part in range(2):
                         for s, value in enumerate(swap_groups(tiles[4 * part : 4 * part + 4], 32)):
                             out_ref[pl.ds((4 * quad + s) * lines, lines), pl.ds(128 * part, 128)] = value.astype(BF16)
+                    sent_off(off, out_ref, out_hbm, out_sems, 4 * quad * lines, 4 * lines)
                 else:
                     for s, value in enumerate(swap_groups(tiles, 8)):
                         value = value.astype(BF16)
                         for half_id in range(2):
                             owner = 16 * side + 8 * half_id + s
                             out_ref[pl.ds(owner * lines, lines), 256:384] = value
+    arrived(off)
 
 
 def backward_columns(
-    recv_ref, sens_ref, first_ref, second_ref, table_hbm, out_ref, part_ref, edge_ref, line_ref, table_ref, sems
+    recv_ref, sens_ref, first_ref, second_ref, table_hbm, out_hbm,
+    part_ref, edge_ref, line_ref, table_ref, out_ref, sems, out_sems,
 ):
     copies = table_copies(table_hbm, table_ref, sems, table_ref.shape[0] // 2)
     coils, spots, rows, npar = sens_ref.shape[1:]
@@ -337,6 +350,7 @@
     width = npar // owners
     lane = lax.broadcasted_iota(jnp.int32, (total, 128), 1)
     count = npar // 128
+    copies = []
     for owner in range(owners):
         tile, off = divmod(width * owner, 128)
         value = part_ref[:, pl.ds(128 * tile, 128)]
@@ -348,10 +362,12 @@
         elif tile:
             value = jnp.where(lane >= 112, part_ref[:, pl.ds(128 * (tile - 1), 128)], value)
         out_ref[pl.ds(owner * total, total), :] = value.astype(BF16)
+        sent_off(copies, out_ref, out_hbm, out_sems, owner * total, total)
+    arrived(copies)
 
 
 def pack_rows(state_ref, sens_ref, first_ref, second_ref):
-    channels, spots, rows, cols = state_ref.shape
+    channels, _, rows, cols = state_ref.shape
     coils, npar = sens_ref.shape[1], sens_ref.shape[4]
     even = lax.axis_index("space") % 2 == 0
     at = 0
@@ -558,7 +574,7 @@
     return lax.ppermute(array, axis, pairs + [(j, i) for i, j in pairs])
 
 
-def per_device(state, sens, kdata, mask, inject, kernels, biases, mixers):
+def step(state, sens, kdata, mask, inject, kernels, biases, mixers):
     channels, spots, rows, cols = state.shape
     coils = sens.shape[1]
     npar = sens.shape[4]
@@ -583,15 +599,14 @@
     par_table = ((npar, npar), BF16)
     pe_table = ((npe, 2 * len(pe_columns)), BF16)
     data_form = ((8 * lines, npe), F32)
-    first, second, state, sens, sampled, par, pe, data = call(
+    first, second, state, sens, sampled, near_par, par, pe, data = call(
         prepare,
         [((depth, 128), BF16)] * 2
-        + [(state.shape, BF16), (sens.shape, F32), (mask.shape, F32)]
+        + [(state.shape, BF16), (sens.shape, F32), (mask.shape, F32), par_table]
         + [pltpu.HBM(*form) for form in (par_table, pe_table, data_form)],
         [
             (par_factors.shape, F32),
             (pe_factors.shape, F32),
-            par_table,
             pe_table,
             (kdata.shape, F32),
             (mask.shape, mask.dtype),
@@ -600,53 +615,59 @@
             pltpu.SemaphoreType.DMA((npar // FINE // 4,)),
             pltpu.SemaphoreType.DMA((npe // FINE // 4,)),
         ],
-        "prepare",
         *[in_hbm(each) for each in (state, sens, par_factors, pe_factors, kdata, mask)],
     )
 
     (sent,) = call(
         forward_columns,
-        [jax.ShapeDtypeStruct((npar, 2 * cells), BF16)],
-        [((2, 2 * cells, npar // 2), BF16), ((2, npar, 128), F32), par_table, pltpu.SemaphoreType.DMA((npar // 128,))],
-        "forward_columns",
-        estimate, sens, in_hbm(par),
-    )
-    sent, first, second = lax.optimization_barrier((sent, first, second))
+        [pltpu.HBM((npar, 2 * cells), BF16)],
+        [
+            ((2, 2 * cells, npar // 2), BF16),
+            ((2, npar, 128), F32),
+            ((npar, 2 * cells), BF16),
+            pltpu.SemaphoreType.DMA((npar // 256,)),
+        ],
+        estimate, sens, near_par,
+    )
+    first = swapped(first, "space", 0)
+    sent, second = lax.optimization_barrier((sent, second))
     spectra = lax.all_to_all(sent, "space", 0, 0, tiled=True)
-    first, second = swapped(first, "space", 0), swapped(second, "space", 1)
+    second = swapped(second, "space", 1)
 
     (sent,) = call(
         consistency,
-        [jax.ShapeDtypeStruct((npar, 384), BF16)],
+        [pltpu.HBM((npar, 384), BF16)],
         [
             ((2, 8 * lines, npe // 2), BF16),
             ((8 * lines, npe), BF16),
             ((8 * lines, npe), F32),
             pe_table,
+            ((npar, 384), BF16),
             pltpu.SemaphoreType.DMA((npe // 256,)),
             pltpu.SemaphoreType.DMA,
+            pltpu.SemaphoreType.DMA((npe // 128,)),
         ],
-        "consistency",
         spectra, in_hbm(data), sampled, in_hbm(pe),
     )
     sent, first, second = lax.optimization_barrier((sent, first, second))
     returned = lax.all_to_all(sent, "space", 0, 0, tiled=True)
 
     packed = [((channels * spots * REACH // 128 * tall, 128), BF16)] * 2
-    tail, head = call(pack_cols, packed, [], "pack_cols", state, first, second)
+    tail, head = call(pack_cols, packed, [], state, first, second)
     left, right = from_previous(tail, "coil"), from_next(head, "coil")
 
     (sent,) = call(
         backward_columns,
-        [jax.ShapeDtypeStruct((owners * 2 * spots * tall, 128), BF16)],
+        [pltpu.HBM((owners * 2 * spots * tall, 128), BF16)],
         [
             ((2 * spots * tall, npar), F32),
             ((2, coils, spots, 2 * REACH, npar), F32),
             ((3, npar, 128), F32),
             par_table,
+            ((owners * 2 * spots * tall, 128), BF16),
             pltpu.SemaphoreType.DMA((2,)),
+            pltpu.SemaphoreType.DMA((owners,)),
         ],
-        "backward_columns",
         returned, sens, first, second, in_hbm(par),
     )
     sent, left, right = lax.optimization_barrier((sent, left, right))
@@ -656,7 +677,6 @@
         spread_state,
         [((tall * channels * spots, 128), BF16)],
         [((channels * spots * tall, 128), F32)],
-        "spread_state",
         state, first, second, left, right,
     )
 
@@ -669,14 +689,12 @@
             ((2, 2 * block, 128), F32),
         ],
         [],
-        "coupling_weights",
         plain(kernels), plain(biases), plain(mixers), plain(inject.T),
     )
     new_state, gradient = call(
         couple,
         [jax.ShapeDtypeStruct(state.shape, BF16), jax.ShapeDtypeStruct((2, spots, rows, cols), F32)],
         [((2 * block * rows, 128), F32), ((block * tall, 128), BF16), ((block * tall, 128), BF16)],
-        "couple",
         shares, spread, weight, mixer, bias, added,
     )
     return (new_state, gradient)
@@ -684,7 +702,7 @@
 
 def solution(mesh):
     return jax.shard_map(
-        per_device,
+        step,
         mesh=mesh,
         in_specs=(
             P(None, None, "space", "coil"),

time: 104 us -> 102 us (0.981)
  Pallas kernels: 20.8 us -> 18.9 us
    pallas_call x8, Pallas kernels: 20.8 us -> 18.9 us  [call(): pl.pallas_call(body, out_shape=shapes, in_specs=specs, out_specs=placed,...]
where the time goes in v6:
time: 102 us; the launch traced here: 101 us
  starting transfers between devices  50.2 us (49%)
  waiting for transfers between devices  29.4 us (29%)
  Pallas kernels  18.9 us (19%)
  local copies, waits for them, and re-layouts  2.09 us (2%)
    pallas_call x8, Pallas kernels, call(): pl.pallas_call(body, out_shape=shapes, in_specs=specs, out_specs=placed,...  18.9 us
    all_to_all x1, starting transfers between devices, step(): spectra = lax.all_to_all(sent, 'space', 0, 0, tiled=True)  11.1 us
    all_to_all x1, waiting for transfers between devices, step(): spectra = lax.all_to_all(sent, 'space', 0, 0, tiled=True)  10.9 us
    all_to_all x1, starting transfers between devices, step(): shares = lax.all_to_all(sent, 'coil', 0, 0, tiled=True)  8.53 us
    all_to_all x1, waiting for transfers between devices, step(): shares = lax.all_to_all(sent, 'coil', 0, 0, tiled=True)  8.42 us
    all_to_all x1, starting transfers between devices, step(): returned = lax.all_to_all(sent, 'space', 0, 0, tiled=True)  8.11 us
    all_to_all x1, starting transfers between devices, step(): estimate = lax.all_to_all(estimate, 'coil', 0, 0, tiled=True)  7.39 us
    ppermute x1, starting transfers between devices, from_previous(): lax.ppermute(tail, axis, [(i, i + 1) for i in range(lax.axis_size(axis) -...  7.23 us
  transfers between devices with their start and end apart: 8, of which 4 were waited for; matrix products, arithmetic and copies ran while one was open for 1% of the time, Pallas kernels for 13%

profile of v6, /device:TPU:1, one launch (start us, length us, event | category | flops | bytes accessed | tf_op | source)
XLA Modules:
  0.0 101.4 jit_solution(17674552517913767734)
XLA Ops:
  0.6 0.8 slice.3
  1.4 0.8 broadcast_in_dim.2
  2.2 7.4 %all-to-all-start = ((bf16[8,2,2,32,128]{4,3,2,1,0:T(8,128)(2,1)}), bf16[8,2,2,32,128]{4,3,2,1,0:T(8,128)(2,1)S(1)}, u32[]{:S(2)}, u32[]{:S(2)}) async-start(bf16[8,2,2,32,128]{4,3,2,1,0:T(8,128)(2,1)} %broadcast_in_dim.2), calls=%async_computation | async-start | bytes 524288 | tf_op jit(solution)/shard_map/all_to_all | solution.py:592
  9.6 3.5 %shard_map.113 = (bf16[448,128]{1,0:T(8,128)(2,1)S(1)}, bf16[448,128]{1,0:T(8,128)(2,1)S(1)}, bf16[32,2,32,96]{3,2,1,0:T(8,128)(2,1)S(1)}, f32[2,2,2,32,768]{4,3...) custom-call(bf16[32,2,32,96]{3,2,1,0:T(8,128)(2,1)} %state_hbm.1, ...), custom_call_target="tpu_custom_call" | custom-call | tf_op jit(solution)/shard_map/pallas_call | solution.py:30
  13.0 5.2 %all-to-all-done.est_ref = bf16[8,2,2,32,128]{4,3,2,1,0:T(8,128)(2,1)S(1)} async-done(((bf16[8,2,2,32,128]{4,3,2,1,0:T(8,128)(2,1)}), bf16[8,2,2,32,128]{4,3,2,1,0:T(8,128)(2,1)S(1)}, u32[]{:S(2)}, u32[]{:S(2)}) %all-to-all-start) | async-done | bytes 262176 | tf_op jit(solution)/shard_map/all_to_all | solution.py:592
  18.2 1.8 %shard_map.114 = bf16[768,256]{1,0:T(8,128)(2,1)} custom-call(bf16[8,2,2,32,128]{4,3,2,1,0:T(8,128)(2,1)S(1)} %all-to-all-done.est_ref, f32[2,2,2,32,768]{4,3,2,1,0:T(8,128)S(1)} %get-tuple-element.25.sens_ref, bf16[768,768]{1,0:T(8,128)(2,1)S(1)} %get-tuple-element.26.table_ref), custom_call_target="tpu_custom_call" | custom-call | tf_op jit(solution)/shard_map/pallas_call | solution.py:30
  20.0 11.1 %all-to-all-start.1 = ((bf16[32,24,256]{2,1,0:T(8,128)(2,1)}), bf16[32,24,256]{2,1,0:T(8,128)(2,1)S(1)}, u32[]{:S(2)}, u32[]{:S(2)}) async-start(bf16[32,24,256]{2,1,0:T(8,128)(2,1)} %bitcast.12), calls=%async_computation.1 | async-start | bytes 786432 | tf_op jit(solution)/shard_map/all_to_all | solution.py:634
  31.1 5.2 %collective-permute-start = (bf16[448,128]{1,0:T(8,128)(2,1)S(1)}, bf16[448,128]{1,0:T(8,128)(2,1)S(1)}, u32[]{:S(2)}, u32[]{:S(2)}) collective-permute-start(bf16[448,128]{1,0:T(8,128)(2,1)S(1)} %get-tuple-element.32), channel_id=1, source_target_pairs={{0,8},{16,24},{32,40},{48,56},{64,72},{80,88},{96,104},{112,120},{... | collective-permute-start | bytes 344072 | tf_op jit(solution)/shard_map/ppermute | solution.py:574
  36.4 0.7 collective-permute-start.1
  37.0 10.9 %all-to-all-done.1 = bf16[32,24,256]{2,1,0:T(8,128)(2,1)S(1)} async-done(((bf16[32,24,256]{2,1,0:T(8,128)(2,1)}), bf16[32,24,256]{2,1,0:T(8,128)(2,1)S(1)}, u32[]{:S(2)}, u32[]{:S(2)}) %all-to-all-start.1) | async-done | bytes 393248 | tf_op jit(solution)/shard_map/all_to_all | solution.py:634
  47.9 5.3 %shard_map.115 = bf16[768,384]{1,0:T(8,128)(2,1)} custom-call(bf16[768,256]{1,0:T(8,128)(2,1)S(1)} %bitcast.8, f32[192,1024]{1,0:T(8,128)} %get-tuple-element.29.data_hbm, f32[24,1024]{1,0:T(8,128)S(1)} %get-tuple-element.30.sampled_ref, bf16[1024,1280]{1,0:T(8,128)(2,1)} %get-tuple-element.31.table_hbm), custom_call_target="tpu_custom_call" | custom-call | tf_op jit(solution)/shard_map/pallas_call | solution.py:30
  53.1 0.0 collective-permute-done.first_ref
  53.1 0.0 collective-permute-done.1.second_ref
  53.2 8.1 %all-to-all-start.2 = ((bf16[32,24,384]{2,1,0:T(8,128)(2,1)}), bf16[32,24,384]{2,1,0:T(8,128)(2,1)S(1)}, u32[]{:S(2)}, u32[]{:S(2)}) async-start(bf16[32,24,384]{2,1,0:T(8,128)(2,1)} %bitcast.11), calls=%async_computation.2 | async-start | bytes 1179648 | tf_op jit(solution)/shard_map/all_to_all | solution.py:653
  61.3 0.4 shard_map.117
  61.7 7.2 %collective-permute-start.2 = (bf16[80,128]{1,0:T(8,128)(2,1)S(1)}, bf16[80,128]{1,0:T(8,128)(2,1)S(1)}, u32[]{:S(2)}, u32[]{:S(2)}) collective-permute-start(bf16[80,128]{1,0:T(8,128)(2,1)S(1)} %get-tuple-element.39), channel_id=1, source_target_pairs={{0,1},{1,2},{2,3},{3,4},{4,5},{5,6},{6,7},{8,9},{9,10},{10,11},{11... | collective-permute-start | bytes 61448 | tf_op jit(solution)/shard_map/ppermute | solution.py:564
  68.9 1.9 %collective-permute-start.3 = (bf16[80,128]{1,0:T(8,128)(2,1)S(1)}, bf16[80,128]{1,0:T(8,128)(2,1)S(1)}, u32[]{:S(2)}, u32[]{:S(2)}) collective-permute-start(bf16[80,128]{1,0:T(8,128)(2,1)S(1)} %get-tuple-element.40), channel_id=1, source_target_pairs={{1,0},{2,1},{3,2},{4,3},{5,4},{6,5},{7,6},{9,8},{10,9},{11,10},{12... | collective-permute-start | bytes 61448 | tf_op jit(solution)/shard_map/ppermute | solution.py:568
  70.9 4.9 %all-to-all-done.2 = bf16[32,24,384]{2,1,0:T(8,128)(2,1)S(1)} async-done(((bf16[32,24,384]{2,1,0:T(8,128)(2,1)}), bf16[32,24,384]{2,1,0:T(8,128)(2,1)S(1)}, u32[]{:S(2)}, u32[]{:S(2)}) %all-to-all-start.2) | async-done | bytes 589856 | tf_op jit(solution)/shard_map/all_to_all | solution.py:653
  75.8 0.0 copy-start.3
  75.8 3.2 %shard_map.116 = bf16[1280,128]{1,0:T(8,128)(2,1)} custom-call(bf16[768,384]{1,0:T(8,128)(2,1)S(1)} %bitcast.7, f32[2,2,2,32,768]{4,3,2,1,0:T(8,128)S(1)} %get-tuple-element.25.sens_ref, bf16[448,128]{1,0:T(8,128)(2,1)S(1)} %collective-permute-done.first_ref, bf16[448,128]{1,0:T(8,128)(2,1)S(1)} %collective-permute-done.1.second_ref, ...), custom_call_target="tpu_custom_call" | custom-call | tf_op jit(solution)/shard_map/pallas_call | solution.py:30
  79.0 0.0 copy-start
  79.0 0.0 copy-start.1
  79.0 0.0 copy-start.2
  79.0 0.0 collective-permute-done.2.left_ref
  79.0 0.0 collective-permute-done.3.right_ref
  79.0 8.5 %all-to-all-start.3 = ((bf16[8,160,128]{2,1,0:T(8,128)(2,1)}), bf16[8,160,128]{2,1,0:T(8,128)(2,1)S(1)}, u32[]{:S(2)}, u32[]{:S(2)}) async-start(bf16[8,160,128]{2,1,0:T(8,128)(2,1)} %bitcast.13), calls=%async_computation.3 | async-start | bytes 655360 | tf_op jit(solution)/shard_map/all_to_all | solution.py:674
  87.6 0.0 copy-done.3
  87.6 0.5 copy.12.kernels_ref
  88.1 0.0 copy-done
  88.1 0.0 copy-done.1
  88.1 0.0 copy-done.2
  88.1 0.4 shard_map.119
  88.5 0.6 shard_map.118.state_ref
  89.1 8.4 %all-to-all-done.3 = bf16[8,160,128]{2,1,0:T(8,128)(2,1)S(1)} async-done(((bf16[8,160,128]{2,1,0:T(8,128)(2,1)}), bf16[8,160,128]{2,1,0:T(8,128)(2,1)S(1)}, u32[]{:S(2)}, u32[]{:S(2)}) %all-to-all-start.3) | async-done | bytes 327712 | tf_op jit(solution)/shard_map/all_to_all | solution.py:674
  97.6 3.8 %shard_map.120 = (bf16[32,2,32,96]{3,2,1,0:T(8,128)(2,1)}, f32[2,2,32,96]{3,2,1,0:T(8,128)}) custom-call(bf16[1280,128]{1,0:T(8,128)(2,1)S(1)} %bitcast.9, bf16[2560,128]{1,0:T(8,128)(2,1)S(1)} %shard_map.118.state_ref, bf16[4,96,96]{2,1,0:T(8,128)(2,1)S(1)} %get-tuple-element.44.weight_ref, bf16[4,32,32]{2,1,0:T(8,128)(2,1)S(1)} %get-tuple-element.45.mixer_ref, ...), custom_call_target="tpu_custom_call" | custom-call | tf_op jit(solution)/shard_map/pallas_call | solution.py:30
  (1 shorter events, 0.0 us)
Async XLA Ops:
  2.2 16.1 %all-to-all-start = ((bf16[8,2,2,32,128]{4,3,2,1,0:T(8,128)(2,1)}), bf16[8,2,2,32,128]{4,3,2,1,0:T(8,128)(2,1)S(1)}, u32[]{:S(2)}, u32[]{:S(2)}) async-start(bf16[8,2,2,32,128]{4,3,2,1,0:T(8,128)(2,1)} %broadcast_in_dim.2), calls=%async_computation | async-start | bytes 524288 | tf_op jit(solution)/shard_map/all_to_all | solution.py:592
  20.0 27.9 %all-to-all-start.1 = ((bf16[32,24,256]{2,1,0:T(8,128)(2,1)}), bf16[32,24,256]{2,1,0:T(8,128)(2,1)S(1)}, u32[]{:S(2)}, u32[]{:S(2)}) async-start(bf16[32,24,256]{2,1,0:T(8,128)(2,1)} %bitcast.12), calls=%async_computation.1 | async-start | bytes 786432 | tf_op jit(solution)/shard_map/all_to_all | solution.py:634
  31.1 22.0 %collective-permute-start = (bf16[448,128]{1,0:T(8,128)(2,1)S(1)}, bf16[448,128]{1,0:T(8,128)(2,1)S(1)}, u32[]{:S(2)}, u32[]{:S(2)}) collective-permute-start(bf16[448,128]{1,0:T(8,128)(2,1)S(1)} %get-tuple-element.32), channel_id=1, source_target_pairs={{0,8},{16,24},{32,40},{48,56},{64,72},{80,88},{96,104},{112,120},{... | collective-permute-start | bytes 344072 | tf_op jit(solution)/shard_map/ppermute | solution.py:574
  36.4 16.8 %collective-permute-start.1 = (bf16[448,128]{1,0:T(8,128)(2,1)S(1)}, bf16[448,128]{1,0:T(8,128)(2,1)S(1)}, u32[]{:S(2)}, u32[]{:S(2)}) collective-permute-start(bf16[448,128]{1,0:T(8,128)(2,1)S(1)} %get-tuple-element.33), channel_id=1, source_target_pairs={{8,16},{24,32},{40,48},{56,64},{72,80},{88,96},{104,112},{120,128}... | collective-permute-start | bytes 344072 | tf_op jit(solution)/shard_map/ppermute | solution.py:574
  53.2 22.6 %all-to-all-start.2 = ((bf16[32,24,384]{2,1,0:T(8,128)(2,1)}), bf16[32,24,384]{2,1,0:T(8,128)(2,1)S(1)}, u32[]{:S(2)}, u32[]{:S(2)}) async-start(bf16[32,24,384]{2,1,0:T(8,128)(2,1)} %bitcast.11), calls=%async_computation.2 | async-start | bytes 1179648 | tf_op jit(solution)/shard_map/all_to_all | solution.py:653
  61.7 17.3 %collective-permute-start.2 = (bf16[80,128]{1,0:T(8,128)(2,1)S(1)}, bf16[80,128]{1,0:T(8,128)(2,1)S(1)}, u32[]{:S(2)}, u32[]{:S(2)}) collective-permute-start(bf16[80,128]{1,0:T(8,128)(2,1)S(1)} %get-tuple-element.39), channel_id=1, source_target_pairs={{0,1},{1,2},{2,3},{3,4},{4,5},{5,6},{6,7},{8,9},{9,10},{10,11},{11... | collective-permute-start | bytes 61448 | tf_op jit(solution)/shard_map/ppermute | solution.py:564
  68.9 10.1 %collective-permute-start.3 = (bf16[80,128]{1,0:T(8,128)(2,1)S(1)}, bf16[80,128]{1,0:T(8,128)(2,1)S(1)}, u32[]{:S(2)}, u32[]{:S(2)}) collective-permute-start(bf16[80,128]{1,0:T(8,128)(2,1)S(1)} %get-tuple-element.40), channel_id=1, source_target_pairs={{1,0},{2,1},{3,2},{4,3},{5,4},{6,5},{7,6},{9,8},{10,9},{11,10},{12... | collective-permute-start | bytes 61448 | tf_op jit(solution)/shard_map/ppermute | solution.py:568
  75.8 11.8 %copy-start.3 = (bf16[4,27,16,16]{1,3,2,0:T(8,128)(2,1)S(1)}, bf16[4,27,16,16]{1,3,2,0:T(8,128)(2,1)}, u32[]{:S(2)}) copy-start(bf16[4,27,16,16]{1,3,2,0:T(8,128)(2,1)} %param.15) | copy-start | bytes 165892
  79.0 9.1 %copy-start = (bf16[4,16,16]{2,1,0:T(8,128)(2,1)S(1)}, bf16[4,16,16]{2,1,0:T(8,128)(2,1)}, u32[]{:S(2)}) copy-start(bf16[4,16,16]{2,1,0:T(8,128)(2,1)} %mixers_ref.1) | copy-start | bytes 6148
  79.0 9.1 %copy-start.1 = (f32[4,16]{1,0:T(4,128)S(1)}, f32[4,16]{1,0:T(4,128)}, u32[]{:S(2)}) copy-start(f32[4,16]{1,0:T(4,128)} %biases_ref.1) | copy-start | bytes 772
  79.0 9.1 %copy-start.2 = (f32[32,2]{0,1:T(2,128)S(1)}, f32[32,2]{0,1:T(2,128)}, u32[]{:S(2)}) copy-start(f32[32,2]{0,1:T(2,128)} %param.14) | copy-start | bytes 772
  79.0 18.5 %all-to-all-start.3 = ((bf16[8,160,128]{2,1,0:T(8,128)(2,1)}), bf16[8,160,128]{2,1,0:T(8,128)(2,1)S(1)}, u32[]{:S(2)}, u32[]{:S(2)}) async-start(bf16[8,160,128]{2,1,0:T(8,128)(2,1)} %bitcast.13), calls=%async_computation.3 | async-start | bytes 655360 | tf_op jit(solution)/shard_map/all_to_all | solution.py:674

commit v7 on v6

--- a/solution.py
+++ b/solution.py
@@ -100,8 +100,8 @@
 
 def prepare(
     state_hbm, sens_hbm, par_factors_hbm, pe_factors_hbm, kdata_hbm, mask_hbm,
-    first_ref, second_ref, state_ref, sens_ref, sampled_ref, par_ref, par_hbm, pe_hbm, data_hbm,
-    par_factors, pe_factors, pe_ref, kdata_ref, mask_ref, data_ref, sems, par_sems, pe_sems,
+    first_ref, second_ref, sens_ref, sampled_ref, par_ref, data_ref, par_hbm, pe_hbm,
+    par_factors, pe_factors, pe_ref, kdata_ref, mask_ref, state_ref, sems, par_sems, pe_sems,
 ):
     pairs = (
         (par_factors_hbm, par_factors), (pe_factors_hbm, pe_factors), (state_hbm, state_ref), (sens_hbm, sens_ref),
@@ -118,10 +118,8 @@
     sent = sent + fill_table(pe_factors, pe_hbm, pe_ref, pe_sems)
     arrived(copies[2:])
     sort_lines(kdata_ref, mask_ref, data_ref, sampled_ref)
-    last = pltpu.make_async_copy(data_ref, data_hbm, sems.at[len(pairs)])
-    last.start()
     pack_rows(state_ref, sens_ref, first_ref, second_ref)
-    arrived(sent + [last])
+    arrived(sent)
 
 
 def sort_lines(kdata_ref, mask_ref, data_ref, sampled_ref):
@@ -135,9 +133,7 @@
         value = jnp.concatenate(
             [kdata_ref[part, c, p, :, here] for part in range(2) for c in range(coils) for p in range(spots)], axis=0
         )
-        high = value.astype(BF16)
-        low = (value - high.astype(F32)).astype(BF16)
-        value = nn(high, pick) + nn(low, pick)
+        value = nn(value.astype(BF16), pick).astype(BF16)
         sampled = nn(mask_ref[:, here].astype(F32).astype(BF16), pick)
         for side in range(2):
             to = pl.ds(side * npe // 2 + 128 * block, 128)
@@ -226,13 +222,10 @@
 
 
 def consistency(
-    recv_ref, data_hbm, sampled_ref, table_hbm, out_hbm,
-    x_ref, res_ref, data_ref, table_ref, out_ref, sems, data_sem, out_sems,
+    recv_ref, data_ref, sampled_ref, table_hbm, out_hbm, x_ref, res_ref, table_ref, out_ref, sems, out_sems
 ):
     step = 256
     copies = table_copies(table_hbm, table_ref, sems, step)
-    data_copy = pltpu.make_async_copy(data_hbm, data_ref, data_sem)
-    data_copy.start()
     lines, npe = sampled_ref.shape
     middle = npe // 2
     width = table_ref.shape[1] // 2
@@ -252,7 +245,6 @@
         low, high = gathered(quad), gathered(quad + quads // 2)
         x_ref[0, :, pl.ds(128 * quad, 128)] = (low + high).astype(BF16)
         x_ref[1, :, pl.ds(128 * quad, 128)] = (low - high).astype(BF16)
-    data_copy.wait()
     for odd in range(2):
         x = x_ref[odd]
         for start in range(odd * middle, (odd + 1) * middle, step):
@@ -261,8 +253,8 @@
             by_cos = nt(x, table_ref[here, 0:middle])
             by_sin = nt(x, table_ref[here, width : width + middle])
             sampled = jnp.concatenate([sampled_ref[:, here]] * 4, axis=0)
-            real = sampled * (by_cos[:half] + by_sin[half:] - data_ref[0:half, here])
-            imag = sampled * (by_cos[half:] - by_sin[:half] - data_ref[half : 2 * half, here])
+            real = sampled * (by_cos[:half] + by_sin[half:] - data_ref[0:half, here].astype(F32))
+            imag = sampled * (by_cos[half:] - by_sin[:half] - data_ref[half : 2 * half, here].astype(F32))
             res_ref[0:half, here] = real.astype(BF16)
             res_ref[half : 2 * half, here] = imag.astype(BF16)
     res = [res_ref[:, 0:middle], res_ref[:, middle:npe]]
@@ -487,8 +479,11 @@
         )
 
 
-def couple(recv_ref, state_ref, weight_ref, mixer_ref, bias_ref, inject_ref, new_ref, grad_ref, wide_ref, a_ref, b_ref):
-    channels, spots, rows, cols = new_ref.shape
+def couple(
+    recv_ref, state_ref, weight_ref, mixer_ref, bias_ref, inject_ref, new_hbm, grad_hbm,
+    wide_ref, a_ref, b_ref, new_ref, grad_ref, sems,
+):
+    channels, spots, rows, cols = new_hbm.shape
     tall = rows + 2 * REACH
     half = channels // 2
     block = spots * half
@@ -501,6 +496,23 @@
         for spot in range(spots):
             row = (part * spots + spot) * tall
             grad_ref[part, spot] = grad[row : row + rows, :cols]
+    copies = [pltpu.make_async_copy(grad_ref, grad_hbm, sems.at[0])]
+    copies[0].start()
+
+    def finish(ref, which):
+        for source in range(rows):
+            to = pl.ds(which * block * rows + source, block, stride=rows)
+            wide_ref[to, :] = ref[pl.ds((source + REACH) * block, block), :].astype(F32)
+        for channel in range(half):
+            for spot in range(spots):
+                at = (which * block + spot * half + channel) * rows
+                new_ref[which * half + channel, spot] = wide_ref[pl.ds(at, rows), :][:, :cols].astype(BF16)
+            if channel % 4 == 3:
+                here = pl.ds(which * half + channel - 3, 4)
+                copy = pltpu.make_async_copy(new_ref.at[here], new_hbm.at[here], sems.at[len(copies)])
+                copy.start()
+                copies.append(copy)
+
     space, coil = lax.axis_index("space"), lax.axis_index("coil")
     lane = lax.broadcasted_iota(jnp.int32, (1, 128), 1)
     col_id = coil * cols + jnp.where(lane < 112, lane, lane - 128)
@@ -550,14 +562,9 @@
                 here = pl.ds(i * block, block)
                 value = target_ref[here, :].astype(F32) + mixed[:, 128 * j : 128 * j + 128]
                 target_ref[here, :] = (value * keep(i)).astype(BF16)
-    for i in range(REACH, REACH + rows):
-        source = i - REACH
-        wide_ref[pl.ds(source, block, stride=rows), :] = a_ref[pl.ds(i * block, block), :].astype(F32)
-        wide_ref[pl.ds(block * rows + source, block, stride=rows), :] = b_ref[pl.ds(i * block, block), :].astype(F32)
-    for channel in range(channels):
-        for spot in range(spots):
-            at = (channel // half * block + spot * half + channel % half) * rows
-            new_ref[channel, spot] = wide_ref[pl.ds(at, rows), :][:, :cols].astype(BF16)
+        if layer >= weight_ref.shape[0] - 2:
+            finish(target_ref, 1 - layer % 2)
+    arrived(copies)
 
 
 def from_previous(tail, axis):
@@ -598,20 +605,20 @@
     pe_factors = jnp.asarray(dft_factors(npe, pe_columns))
     par_table = ((npar, npar), BF16)
     pe_table = ((npe, 2 * len(pe_columns)), BF16)
-    data_form = ((8 * lines, npe), F32)
-    first, second, state, sens, sampled, near_par, par, pe, data = call(
+    data_form = ((8 * lines, npe), BF16)
+    first, second, sens, sampled, near_par, data, par, pe = call(
         prepare,
         [((depth, 128), BF16)] * 2
-        + [(state.shape, BF16), (sens.shape, F32), (mask.shape, F32), par_table]
-        + [pltpu.HBM(*form) for form in (par_table, pe_table, data_form)],
+        + [(sens.shape, F32), (mask.shape, F32), par_table, data_form]
+        + [pltpu.HBM(*form) for form in (par_table, pe_table)],
         [
             (par_factors.shape, F32),
             (pe_factors.shape, F32),
             pe_table,
             (kdata.shape, F32),
             (mask.shape, mask.dtype),
-            data_form,
-            pltpu.SemaphoreType.DMA((7,)),
+            (state.shape, BF16),
+            pltpu.SemaphoreType.DMA((6,)),
             pltpu.SemaphoreType.DMA((npar // FINE // 4,)),
             pltpu.SemaphoreType.DMA((npe // FINE // 4,)),
         ],
@@ -640,20 +647,18 @@
         [
             ((2, 8 * lines, npe // 2), BF16),
             ((8 * lines, npe), BF16),
-            ((8 * lines, npe), F32),
             pe_table,
             ((npar, 384), BF16),
             pltpu.SemaphoreType.DMA((npe // 256,)),
-            pltpu.SemaphoreType.DMA,
             pltpu.SemaphoreType.DMA((npe // 128,)),
         ],
-        spectra, in_hbm(data), sampled, in_hbm(pe),
+        spectra, data, sampled, in_hbm(pe),
     )
     sent, first, second = lax.optimization_barrier((sent, first, second))
     returned = lax.all_to_all(sent, "space", 0, 0, tiled=True)
 
     packed = [((channels * spots * REACH // 128 * tall, 128), BF16)] * 2
-    tail, head = call(pack_cols, packed, [], state, first, second)
+    tail, head = call(pack_cols, packed, [], plain(state), first, second)
     left, right = from_previous(tail, "coil"), from_next(head, "coil")
 
     (sent,) = call(
@@ -677,7 +682,7 @@
         spread_state,
         [((tall * channels * spots, 128), BF16)],
         [((channels * spots * tall, 128), F32)],
-        state, first, second, left, right,
+        plain(state), first, second, left, right,
     )
 
     weight, mixer, bias, added = call(
@@ -693,8 +698,15 @@
     )
     new_state, gradient = call(
         couple,
-        [jax.ShapeDtypeStruct(state.shape, BF16), jax.ShapeDtypeStruct((2, spots, rows, cols), F32)],
-        [((2 * block * rows, 128), F32), ((block * tall, 128), BF16), ((block * tall, 128), BF16)],
+        [pltpu.HBM(state.shape, BF16), pltpu.HBM((2, spots, rows, cols), F32)],
+        [
+            ((2 * block * rows, 128), F32),
+            ((block * tall, 128), BF16),
+            ((block * tall, 128), BF16),
+            (state.shape, BF16),
+            ((2, spots, rows, cols), F32),
+            pltpu.SemaphoreType.DMA((1 + channels // 4,)),
+        ],
         shares, spread, weight, mixer, bias, added,
     )
     return (new_state, gradient)

time: 102 us -> 102 us (level)
  no operation moved by 1% of the time
where the time goes in v7:
time: 102 us; the launch traced here: 101 us
  starting transfers between devices  50.3 us (49%)
  waiting for transfers between devices  29.8 us (29%)
  Pallas kernels  18.3 us (18%)
  local copies, waits for them, and re-layouts  2.09 us (2%)
    pallas_call x8, Pallas kernels, call(): pl.pallas_call(body, out_shape=shapes, in_specs=specs, out_specs=placed,...  18.3 us
    all_to_all x1, starting transfers between devices, step(): spectra = lax.all_to_all(sent, 'space', 0, 0, tiled=True)  11.1 us
    all_to_all x1, waiting for transfers between devices, step(): spectra = lax.all_to_all(sent, 'space', 0, 0, tiled=True)  10.9 us
    all_to_all x1, starting transfers between devices, step(): shares = lax.all_to_all(sent, 'coil', 0, 0, tiled=True)  8.53 us
    all_to_all x1, waiting for transfers between devices, step(): shares = lax.all_to_all(sent, 'coil', 0, 0, tiled=True)  8.42 us
    all_to_all x1, starting transfers between devices, step(): returned = lax.all_to_all(sent, 'space', 0, 0, tiled=True)  8.18 us
    all_to_all x1, starting transfers between devices, step(): estimate = lax.all_to_all(estimate, 'coil', 0, 0, tiled=True)  7.39 us
    ppermute x1, starting transfers between devices, from_previous(): lax.ppermute(tail, axis, [(i, i + 1) for i in range(lax.axis_size(axis) -...  7.3 us
  transfers between devices with their start and end apart: 8, of which 4 were waited for; matrix products, arithmetic and copies ran while one was open for 1% of the time, Pallas kernels for 13%

profile of v7, /device:TPU:1, one launch (start us, length us, event | category | flops | bytes accessed | tf_op | source)
XLA Modules:
  0.0 101.3 jit_solution(15391256428993248527)
XLA Ops:
  0.6 0.8 slice.3
  1.4 0.8 broadcast_in_dim.2
  2.2 7.4 %all-to-all-start = ((bf16[8,2,2,32,128]{4,3,2,1,0:T(8,128)(2,1)}), bf16[8,2,2,32,128]{4,3,2,1,0:T(8,128)(2,1)S(1)}, u32[]{:S(2)}, u32[]{:S(2)}) async-start(bf16[8,2,2,32,128]{4,3,2,1,0:T(8,128)(2,1)} %broadcast_in_dim.2), calls=%async_computation | async-start | bytes 524288 | tf_op jit(solution)/shard_map/all_to_all | solution.py:599
  9.6 3.0 %shard_map.113 = (bf16[448,128]{1,0:T(8,128)(2,1)S(1)}, bf16[448,128]{1,0:T(8,128)(2,1)S(1)}, f32[2,2,2,32,768]{4,3,2,1,0:T(8,128)S(1)}, f32[24,1024]{1,0:T(8,12...) custom-call(bf16[32,2,32,96]{3,2,1,0:T(8,128)(2,1)} %state_ref.3, ...), custom_call_target="tpu_custom_call" | custom-call | tf_op jit(solution)/shard_map/pallas_call | solution.py:30
  12.6 5.7 %all-to-all-done.est_ref = bf16[8,2,2,32,128]{4,3,2,1,0:T(8,128)(2,1)S(1)} async-done(((bf16[8,2,2,32,128]{4,3,2,1,0:T(8,128)(2,1)}), bf16[8,2,2,32,128]{4,3,2,1,0:T(8,128)(2,1)S(1)}, u32[]{:S(2)}, u32[]{:S(2)}) %all-to-all-start) | async-done | bytes 262176 | tf_op jit(solution)/shard_map/all_to_all | solution.py:599
  18.2 1.8 %shard_map.114 = bf16[768,256]{1,0:T(8,128)(2,1)} custom-call(bf16[8,2,2,32,128]{4,3,2,1,0:T(8,128)(2,1)S(1)} %all-to-all-done.est_ref, f32[2,2,2,32,768]{4,3,2,1,0:T(8,128)S(1)} %get-tuple-element.24.sens_ref, bf16[768,768]{1,0:T(8,128)(2,1)S(1)} %get-tuple-element.25.table_ref), custom_call_target="tpu_custom_call" | custom-call | tf_op jit(solution)/shard_map/pallas_call | solution.py:30
  20.0 11.1 %all-to-all-start.1 = ((bf16[32,24,256]{2,1,0:T(8,128)(2,1)}), bf16[32,24,256]{2,1,0:T(8,128)(2,1)S(1)}, u32[]{:S(2)}, u32[]{:S(2)}) async-start(bf16[32,24,256]{2,1,0:T(8,128)(2,1)} %bitcast.12), calls=%async_computation.1 | async-start | bytes 786432 | tf_op jit(solution)/shard_map/all_to_all | solution.py:641
  31.1 5.2 %collective-permute-start = (bf16[448,128]{1,0:T(8,128)(2,1)S(1)}, bf16[448,128]{1,0:T(8,128)(2,1)S(1)}, u32[]{:S(2)}, u32[]{:S(2)}) collective-permute-start(bf16[448,128]{1,0:T(8,128)(2,1)S(1)} %get-tuple-element.31), channel_id=1, source_target_pairs={{0,8},{16,24},{32,40},{48,56},{64,72},{80,88},{96,104},{112,120},{... | collective-permute-start | bytes 344072 | tf_op jit(solution)/shard_map/ppermute | solution.py:581
  36.4 0.7 collective-permute-start.1
  37.0 10.9 %all-to-all-done.1 = bf16[32,24,256]{2,1,0:T(8,128)(2,1)S(1)} async-done(((bf16[32,24,256]{2,1,0:T(8,128)(2,1)}), bf16[32,24,256]{2,1,0:T(8,128)(2,1)S(1)}, u32[]{:S(2)}, u32[]{:S(2)}) %all-to-all-start.1) | async-done | bytes 393248 | tf_op jit(solution)/shard_map/all_to_all | solution.py:641
  47.9 5.2 %shard_map.115 = bf16[768,384]{1,0:T(8,128)(2,1)} custom-call(bf16[768,256]{1,0:T(8,128)(2,1)S(1)} %bitcast.8, bf16[192,1024]{1,0:T(8,128)(2,1)S(1)} %get-tuple-element.28.data_ref, f32[24,1024]{1,0:T(8,128)S(1)} %get-tuple-element.29.sampled_ref, bf16[1024,1280]{1,0:T(8,128)(2,1)} %get-tuple-element.30.table_hbm), custom_call_target="tpu_custom_call" | custom-call | tf_op jit(solution)/shard_map/pallas_call | solution.py:30
  53.1 0.0 copy-start
  53.1 0.0 collective-permute-done.first_ref
  53.1 0.0 collective-permute-done.1.second_ref
  53.1 8.2 %all-to-all-start.2 = ((bf16[32,24,384]{2,1,0:T(8,128)(2,1)}), bf16[32,24,384]{2,1,0:T(8,128)(2,1)S(1)}, u32[]{:S(2)}, u32[]{:S(2)}) async-start(bf16[32,24,384]{2,1,0:T(8,128)(2,1)} %bitcast.11), calls=%async_computation.2 | async-start | bytes 1179648 | tf_op jit(solution)/shard_map/all_to_all | solution.py:658
  61.3 0.0 copy-done
  61.3 0.4 shard_map.117
  61.7 7.3 %collective-permute-start.2 = (bf16[80,128]{1,0:T(8,128)(2,1)S(1)}, bf16[80,128]{1,0:T(8,128)(2,1)S(1)}, u32[]{:S(2)}, u32[]{:S(2)}) collective-permute-start(bf16[80,128]{1,0:T(8,128)(2,1)S(1)} %get-tuple-element.37), channel_id=1, source_target_pairs={{0,1},{1,2},{2,3},{3,4},{4,5},{5,6},{6,7},{8,9},{9,10},{10,11},{11... | collective-permute-start | bytes 61448 | tf_op jit(solution)/shard_map/ppermute | solution.py:571
  69.0 1.9 %collective-permute-start.3 = (bf16[80,128]{1,0:T(8,128)(2,1)S(1)}, bf16[80,128]{1,0:T(8,128)(2,1)S(1)}, u32[]{:S(2)}, u32[]{:S(2)}) collective-permute-start(bf16[80,128]{1,0:T(8,128)(2,1)S(1)} %get-tuple-element.38), channel_id=1, source_target_pairs={{1,0},{2,1},{3,2},{4,3},{5,4},{6,5},{7,6},{9,8},{10,9},{11,10},{12... | collective-permute-start | bytes 61448 | tf_op jit(solution)/shard_map/ppermute | solution.py:575
  70.9 4.9 %all-to-all-done.2 = bf16[32,24,384]{2,1,0:T(8,128)(2,1)S(1)} async-done(((bf16[32,24,384]{2,1,0:T(8,128)(2,1)}), bf16[32,24,384]{2,1,0:T(8,128)(2,1)S(1)}, u32[]{:S(2)}, u32[]{:S(2)}) %all-to-all-start.2) | async-done | bytes 589856 | tf_op jit(solution)/shard_map/all_to_all | solution.py:658
  75.8 0.0 copy-start.4
  75.8 3.2 %shard_map.116 = bf16[1280,128]{1,0:T(8,128)(2,1)} custom-call(bf16[768,384]{1,0:T(8,128)(2,1)S(1)} %bitcast.7, f32[2,2,2,32,768]{4,3,2,1,0:T(8,128)S(1)} %get-tuple-element.24.sens_ref, bf16[448,128]{1,0:T(8,128)(2,1)S(1)} %collective-permute-done.first_ref, bf16[448,128]{1,0:T(8,128)(2,1)S(1)} %collective-permute-done.1.second_ref, ...), custom_call_target="tpu_custom_call" | custom-call | tf_op jit(solution)/shard_map/pallas_call | solution.py:30
  79.0 0.0 copy-start.1
  79.0 0.0 copy-start.2
  79.0 0.0 copy-start.3
  79.0 0.0 collective-permute-done.2.left_ref
  79.0 0.0 collective-permute-done.3.right_ref
  79.0 8.5 %all-to-all-start.3 = ((bf16[8,160,128]{2,1,0:T(8,128)(2,1)}), bf16[8,160,128]{2,1,0:T(8,128)(2,1)S(1)}, u32[]{:S(2)}, u32[]{:S(2)}) async-start(bf16[8,160,128]{2,1,0:T(8,128)(2,1)} %bitcast.13), calls=%async_computation.3 | async-start | bytes 655360 | tf_op jit(solution)/shard_map/all_to_all | solution.py:679
  87.6 0.0 copy-done.4
  87.6 0.5 copy.12.kernels_ref
  88.1 0.0 copy-done.1
  88.1 0.0 copy-done.2
  88.1 0.0 copy-done.3
  88.1 0.4 shard_map.119
  88.5 0.6 shard_map.118.state_ref
  89.1 8.4 %all-to-all-done.3 = bf16[8,160,128]{2,1,0:T(8,128)(2,1)S(1)} async-done(((bf16[8,160,128]{2,1,0:T(8,128)(2,1)}), bf16[8,160,128]{2,1,0:T(8,128)(2,1)S(1)}, u32[]{:S(2)}, u32[]{:S(2)}) %all-to-all-start.3) | async-done | bytes 327712 | tf_op jit(solution)/shard_map/all_to_all | solution.py:679
  97.6 3.8 %shard_map.120 = (bf16[32,2,32,96]{3,2,1,0:T(8,128)(2,1)}, f32[2,2,32,96]{3,2,1,0:T(8,128)}) custom-call(bf16[1280,128]{1,0:T(8,128)(2,1)S(1)} %bitcast.9, bf16[2560,128]{1,0:T(8,128)(2,1)S(1)} %shard_map.118.state_ref, bf16[4,96,96]{2,1,0:T(8,128)(2,1)S(1)} %get-tuple-element.42.weight_ref, bf16[4,32,32]{2,1,0:T(8,128)(2,1)S(1)} %get-tuple-element.43.mixer_ref, ...), custom_call_target="tpu_custom_call" | custom-call | tf_op jit(solution)/shard_map/pallas_call | solution.py:30
  (1 shorter events, 0.0 us)
Async XLA Ops:
  2.2 16.1 %all-to-all-start = ((bf16[8,2,2,32,128]{4,3,2,1,0:T(8,128)(2,1)}), bf16[8,2,2,32,128]{4,3,2,1,0:T(8,128)(2,1)S(1)}, u32[]{:S(2)}, u32[]{:S(2)}) async-start(bf16[8,2,2,32,128]{4,3,2,1,0:T(8,128)(2,1)} %broadcast_in_dim.2), calls=%async_computation | async-start | bytes 524288 | tf_op jit(solution)/shard_map/all_to_all | solution.py:599
  20.0 27.9 %all-to-all-start.1 = ((bf16[32,24,256]{2,1,0:T(8,128)(2,1)}), bf16[32,24,256]{2,1,0:T(8,128)(2,1)S(1)}, u32[]{:S(2)}, u32[]{:S(2)}) async-start(bf16[32,24,256]{2,1,0:T(8,128)(2,1)} %bitcast.12), calls=%async_computation.1 | async-start | bytes 786432 | tf_op jit(solution)/shard_map/all_to_all | solution.py:641
  31.1 21.9 %collective-permute-start = (bf16[448,128]{1,0:T(8,128)(2,1)S(1)}, bf16[448,128]{1,0:T(8,128)(2,1)S(1)}, u32[]{:S(2)}, u32[]{:S(2)}) collective-permute-start(bf16[448,128]{1,0:T(8,128)(2,1)S(1)} %get-tuple-element.31), channel_id=1, source_target_pairs={{0,8},{16,24},{32,40},{48,56},{64,72},{80,88},{96,104},{112,120},{... | collective-permute-start | bytes 344072 | tf_op jit(solution)/shard_map/ppermute | solution.py:581
  36.4 16.7 %collective-permute-start.1 = (bf16[448,128]{1,0:T(8,128)(2,1)S(1)}, bf16[448,128]{1,0:T(8,128)(2,1)S(1)}, u32[]{:S(2)}, u32[]{:S(2)}) collective-permute-start(bf16[448,128]{1,0:T(8,128)(2,1)S(1)} %get-tuple-element.32), channel_id=1, source_target_pairs={{8,16},{24,32},{40,48},{56,64},{72,80},{88,96},{104,112},{120,128}... | collective-permute-start | bytes 344072 | tf_op jit(solution)/shard_map/ppermute | solution.py:581
  53.1 8.2 %copy-start = (bf16[32,2,32,96]{3,2,1,0:T(8,128)(2,1)S(1)}, bf16[32,2,32,96]{3,2,1,0:T(8,128)(2,1)}, u32[]{:S(2)}) copy-start(bf16[32,2,32,96]{3,2,1,0:T(8,128)(2,1)} %state_ref.3) | copy-start | bytes 1179652
  53.1 22.7 %all-to-all-start.2 = ((bf16[32,24,384]{2,1,0:T(8,128)(2,1)}), bf16[32,24,384]{2,1,0:T(8,128)(2,1)S(1)}, u32[]{:S(2)}, u32[]{:S(2)}) async-start(bf16[32,24,384]{2,1,0:T(8,128)(2,1)} %bitcast.11), calls=%async_computation.2 | async-start | bytes 1179648 | tf_op jit(solution)/shard_map/all_to_all | solution.py:658
  61.7 17.3 %collective-permute-start.2 = (bf16[80,128]{1,0:T(8,128)(2,1)S(1)}, bf16[80,128]{1,0:T(8,128)(2,1)S(1)}, u32[]{:S(2)}, u32[]{:S(2)}) collective-permute-start(bf16[80,128]{1,0:T(8,128)(2,1)S(1)} %get-tuple-element.37), channel_id=1, source_target_pairs={{0,1},{1,2},{2,3},{3,4},{4,5},{5,6},{6,7},{8,9},{9,10},{10,11},{11... | collective-permute-start | bytes 61448 | tf_op jit(solution)/shard_map/ppermute | solution.py:571
  69.0 10.0 %collective-permute-start.3 = (bf16[80,128]{1,0:T(8,128)(2,1)S(1)}, bf16[80,128]{1,0:T(8,128)(2,1)S(1)}, u32[]{:S(2)}, u32[]{:S(2)}) collective-permute-start(bf16[80,128]{1,0:T(8,128)(2,1)S(1)} %get-tuple-element.38), channel_id=1, source_target_pairs={{1,0},{2,1},{3,2},{4,3},{5,4},{6,5},{7,6},{9,8},{10,9},{11,10},{12... | collective-permute-start | bytes 61448 | tf_op jit(solution)/shard_map/ppermute | solution.py:575
  75.8 11.8 %copy-start.4 = (bf16[4,27,16,16]{1,3,2,0:T(8,128)(2,1)S(1)}, bf16[4,27,16,16]{1,3,2,0:T(8,128)(2,1)}, u32[]{:S(2)}) copy-start(bf16[4,27,16,16]{1,3,2,0:T(8,128)(2,1)} %param.15) | copy-start | bytes 165892
  79.0 9.1 %copy-start.1 = (bf16[4,16,16]{2,1,0:T(8,128)(2,1)S(1)}, bf16[4,16,16]{2,1,0:T(8,128)(2,1)}, u32[]{:S(2)}) copy-start(bf16[4,16,16]{2,1,0:T(8,128)(2,1)} %mixers_ref.1) | copy-start | bytes 6148
  79.0 9.1 %copy-start.2 = (f32[4,16]{1,0:T(4,128)S(1)}, f32[4,16]{1,0:T(4,128)}, u32[]{:S(2)}) copy-start(f32[4,16]{1,0:T(4,128)} %biases_ref.1) | copy-start | bytes 772
  79.0 9.1 %copy-start.3 = (f32[32,2]{0,1:T(2,128)S(1)}, f32[32,2]{0,1:T(2,128)}, u32[]{:S(2)}) copy-start(f32[32,2]{0,1:T(2,128)} %param.14) | copy-start | bytes 772
  79.0 18.5 %all-to-all-start.3 = ((bf16[8,160,128]{2,1,0:T(8,128)(2,1)}), bf16[8,160,128]{2,1,0:T(8,128)(2,1)S(1)}, u32[]{:S(2)}, u32[]{:S(2)}) async-start(bf16[8,160,128]{2,1,0:T(8,128)(2,1)} %bitcast.13), calls=%async_computation.3 | async-start | bytes 655360 | tf_op jit(solution)/shard_map/all_to_all | solution.py:679

commit v8 on v7

--- a/solution.py
+++ b/solution.py
@@ -6,7 +6,6 @@
 from jax.experimental import pallas as pl
 from jax.experimental.pallas import tpu as pltpu
 from jax.sharding import PartitionSpec as P
-
 
 F32 = jnp.float32
 BF16 = jnp.bfloat16
@@ -17,7 +16,7 @@
 HBM = pl.BlockSpec(memory_space=pltpu.HBM)
 
 
-def call(body, outs, scratch, *args):
+def call(body, outs, scratch, name, *args):
     specs, values = [], []
     for arg in args:
         where, value = arg if isinstance(arg, tuple) else ("vmem", arg)
@@ -34,6 +33,7 @@
         out_specs=placed,
         scratch_shapes=[each if not isinstance(each, tuple) else pltpu.VMEM(*each) for each in scratch],
         compiler_params=pltpu.CompilerParams(vmem_limit_bytes=20 * 2**20),
+        name=name,
     )(*values)
 
 
@@ -127,7 +127,7 @@
     row = lax.broadcasted_iota(jnp.int32, (step, step), 0)
     lane = lax.broadcasted_iota(jnp.int32, (step, step), 1)
     pick = jnp.where(row == 2 * (lane % 128) + lane // 128, 1.0, 0.0).astype(BF16)
-    coils, spots, _, npe = kdata_ref.shape[1:]
+    coils, spots, lines, npe = kdata_ref.shape[1:]
     for block in range(npe // step):
         here = pl.ds(step * block, step)
         value = jnp.concatenate(
@@ -359,7 +359,7 @@
 
 
 def pack_rows(state_ref, sens_ref, first_ref, second_ref):
-    channels, _, rows, cols = state_ref.shape
+    channels, spots, rows, cols = state_ref.shape
     coils, npar = sens_ref.shape[1], sens_ref.shape[4]
     even = lax.axis_index("space") % 2 == 0
     at = 0
@@ -581,7 +581,7 @@
     return lax.ppermute(array, axis, pairs + [(j, i) for i, j in pairs])
 
 
-def step(state, sens, kdata, mask, inject, kernels, biases, mixers):
+def per_device(state, sens, kdata, mask, inject, kernels, biases, mixers):
     channels, spots, rows, cols = state.shape
     coils = sens.shape[1]
     npar = sens.shape[4]
@@ -622,6 +622,7 @@
             pltpu.SemaphoreType.DMA((npar // FINE // 4,)),
             pltpu.SemaphoreType.DMA((npe // FINE // 4,)),
         ],
+        "prepare",
         *[in_hbm(each) for each in (state, sens, par_factors, pe_factors, kdata, mask)],
     )
 
@@ -634,12 +635,12 @@
             ((npar, 2 * cells), BF16),
             pltpu.SemaphoreType.DMA((npar // 256,)),
         ],
+        "forward_columns",
         estimate, sens, near_par,
     )
-    first = swapped(first, "space", 0)
-    sent, second = lax.optimization_barrier((sent, second))
+    sent, first, second = lax.optimization_barrier((sent, first, second))
     spectra = lax.all_to_all(sent, "space", 0, 0, tiled=True)
-    second = swapped(second, "space", 1)
+    first, second = swapped(first, "space", 0), swapped(second, "space", 1)
 
     (sent,) = call(
         consistency,
@@ -652,13 +653,14 @@
             pltpu.SemaphoreType.DMA((npe // 256,)),
             pltpu.SemaphoreType.DMA((npe // 128,)),
         ],
+        "consistency",
         spectra, data, sampled, in_hbm(pe),
     )
     sent, first, second = lax.optimization_barrier((sent, first, second))
     returned = lax.all_to_all(sent, "space", 0, 0, tiled=True)
 
     packed = [((channels * spots * REACH // 128 * tall, 128), BF16)] * 2
-    tail, head = call(pack_cols, packed, [], plain(state), first, second)
+    tail, head = call(pack_cols, packed, [], "pack_cols", plain(state), first, second)
     left, right = from_previous(tail, "coil"), from_next(head, "coil")
 
     (sent,) = call(
@@ -673,6 +675,7 @@
             pltpu.SemaphoreType.DMA((2,)),
             pltpu.SemaphoreType.DMA((owners,)),
         ],
+        "backward_columns",
         returned, sens, first, second, in_hbm(par),
     )
     sent, left, right = lax.optimization_barrier((sent, left, right))
@@ -682,6 +685,7 @@
         spread_state,
         [((tall * channels * spots, 128), BF16)],
         [((channels * spots * tall, 128), F32)],
+        "spread_state",
         plain(state), first, second, left, right,
     )
 
@@ -694,6 +698,7 @@
             ((2, 2 * block, 128), F32),
         ],
         [],
+        "coupling_weights",
         plain(kernels), plain(biases), plain(mixers), plain(inject.T),
     )
     new_state, gradient = call(
@@ -707,6 +712,7 @@
             ((2, spots, rows, cols), F32),
             pltpu.SemaphoreType.DMA((1 + channels // 4,)),
         ],
+        "couple",
         shares, spread, weight, mixer, bias, added,
     )
     return (new_state, gradient)
@@ -714,7 +720,7 @@
 
 def solution(mesh):
     return jax.shard_map(
-        step,
+        per_device,
         mesh=mesh,
         in_specs=(
             P(None, None, "space", "coil"),

time: 102 us -> 102 us (level)
  no operation moved by 1% of the time
where the time goes in v8:
time: 102 us; the launch traced here: 101 us
  starting transfers between devices  50.3 us (49%)
  waiting for transfers between devices  29.8 us (29%)
  Pallas kernels  18.3 us (18%)
  local copies, waits for them, and re-layouts  2.09 us (2%)
    pallas_call x8, Pallas kernels, call(): pl.pallas_call(body, out_shape=shapes, in_specs=specs, out_specs=placed,...  18.3 us
    all_to_all x1, starting transfers between devices, per_device(): spectra = lax.all_to_all(sent, 'space', 0, 0, tiled=True)  11.1 us
    all_to_all x1, waiting for transfers between devices, per_device(): spectra = lax.all_to_all(sent, 'space', 0, 0, tiled=True)  10.9 us
    all_to_all x1, starting transfers between devices, per_device(): shares = lax.all_to_all(sent, 'coil', 0, 0, tiled=True)  8.53 us
    all_to_all x1, waiting for transfers between devices, per_device(): shares = lax.all_to_all(sent, 'coil', 0, 0, tiled=True)  8.42 us
    all_to_all x1, starting transfers between devices, per_device(): returned = lax.all_to_all(sent, 'space', 0, 0, tiled=True)  8.18 us
    all_to_all x1, starting transfers between devices, per_device(): estimate = lax.all_to_all(estimate, 'coil', 0, 0, tiled=True)  7.39 us
    ppermute x1, starting transfers between devices, from_previous(): lax.ppermute(tail, axis, [(i, i + 1) for i in range(lax.axis_size(axis) -...  7.3 us
  transfers between devices with their start and end apart: 8, of which 4 were waited for; matrix products, arithmetic and copies ran while one was open for 1% of the time, Pallas kernels for 13%

profile of v8, /device:TPU:1, one launch (start us, length us, event | category | flops | bytes accessed | tf_op | source)
XLA Modules:
  0.0 101.4 jit_solution(5911656557768604447)
XLA Ops:
  0.6 0.8 slice.3
  1.4 0.8 broadcast_in_dim.2
  2.2 7.4 %all-to-all-start = ((bf16[8,2,2,32,128]{4,3,2,1,0:T(8,128)(2,1)}), bf16[8,2,2,32,128]{4,3,2,1,0:T(8,128)(2,1)S(1)}, u32[]{:S(2)}, u32[]{:S(2)}) async-start(bf16[8,2,2,32,128]{4,3,2,1,0:T(8,128)(2,1)} %broadcast_in_dim.2), calls=%async_computation | async-start | bytes 524288 | tf_op jit(solution)/shard_map/all_to_all | solution.py:599
  9.6 3.0 %prepare.1 = (bf16[448,128]{1,0:T(8,128)(2,1)S(1)}, bf16[448,128]{1,0:T(8,128)(2,1)S(1)}, f32[2,2,2,32,768]{4,3,2,1,0:T(8,128)S(1)}, f32[24,1024]{1,0:T(8,128)S(...) custom-call(bf16[32,2,32,96]{3,2,1,0:T(8,128)(2,1)} %state_ref.3, ...), custom_call_target="tpu_custom_call" | custom-call | tf_op jit(solution)/shard_map/prepare/pallas_call | solution.py:29
  12.6 5.7 %all-to-all-done.est_ref = bf16[8,2,2,32,128]{4,3,2,1,0:T(8,128)(2,1)S(1)} async-done(((bf16[8,2,2,32,128]{4,3,2,1,0:T(8,128)(2,1)}), bf16[8,2,2,32,128]{4,3,2,1,0:T(8,128)(2,1)S(1)}, u32[]{:S(2)}, u32[]{:S(2)}) %all-to-all-start) | async-done | bytes 262176 | tf_op jit(solution)/shard_map/all_to_all | solution.py:599
  18.2 1.8 %forward_columns.1 = bf16[768,256]{1,0:T(8,128)(2,1)} custom-call(bf16[8,2,2,32,128]{4,3,2,1,0:T(8,128)(2,1)S(1)} %all-to-all-done.est_ref, f32[2,2,2,32,768]{4,3,2,1,0:T(8,128)S(1)} %get-tuple-element.25.sens_ref, bf16[768,768]{1,0:T(8,128)(2,1)S(1)} %get-tuple-element.26.table_ref), custom_call_target="tpu_custom_call" | custom-call | tf_op jit(solution)/shard_map/forward_columns/pallas_call | solution.py:29
  20.0 11.1 %all-to-all-start.1 = ((bf16[32,24,256]{2,1,0:T(8,128)(2,1)}), bf16[32,24,256]{2,1,0:T(8,128)(2,1)S(1)}, u32[]{:S(2)}, u32[]{:S(2)}) async-start(bf16[32,24,256]{2,1,0:T(8,128)(2,1)} %bitcast.12), calls=%async_computation.1 | async-start | bytes 786432 | tf_op jit(solution)/shard_map/all_to_all | solution.py:642
  31.1 5.2 %collective-permute-start = (bf16[448,128]{1,0:T(8,128)(2,1)S(1)}, bf16[448,128]{1,0:T(8,128)(2,1)S(1)}, u32[]{:S(2)}, u32[]{:S(2)}) collective-permute-start(bf16[448,128]{1,0:T(8,128)(2,1)S(1)} %get-tuple-element.33), channel_id=1, source_target_pairs={{0,8},{16,24},{32,40},{48,56},{64,72},{80,88},{96,104},{112,120},{... | collective-permute-start | bytes 344072 | tf_op jit(solution)/shard_map/ppermute | solution.py:581
  36.4 0.7 collective-permute-start.1
  37.0 10.9 %all-to-all-done.1 = bf16[32,24,256]{2,1,0:T(8,128)(2,1)S(1)} async-done(((bf16[32,24,256]{2,1,0:T(8,128)(2,1)}), bf16[32,24,256]{2,1,0:T(8,128)(2,1)S(1)}, u32[]{:S(2)}, u32[]{:S(2)}) %all-to-all-start.1) | async-done | bytes 393248 | tf_op jit(solution)/shard_map/all_to_all | solution.py:642
  47.9 5.2 %consistency.1 = bf16[768,384]{1,0:T(8,128)(2,1)} custom-call(bf16[768,256]{1,0:T(8,128)(2,1)S(1)} %bitcast.8, bf16[192,1024]{1,0:T(8,128)(2,1)S(1)} %get-tuple-element.30.data_ref, f32[24,1024]{1,0:T(8,128)S(1)} %get-tuple-element.31.sampled_ref, bf16[1024,1280]{1,0:T(8,128)(2,1)} %get-tuple-element.32.table_hbm), custom_call_target="tpu_custom_call" | custom-call | tf_op jit(solution)/shard_map/consistency/pallas_call | solution.py:29
  53.1 0.0 copy-start
  53.1 0.0 collective-permute-done.first_ref
  53.1 0.0 collective-permute-done.1.second_ref
  53.1 8.2 %all-to-all-start.2 = ((bf16[32,24,384]{2,1,0:T(8,128)(2,1)}), bf16[32,24,384]{2,1,0:T(8,128)(2,1)S(1)}, u32[]{:S(2)}, u32[]{:S(2)}) async-start(bf16[32,24,384]{2,1,0:T(8,128)(2,1)} %bitcast.11), calls=%async_computation.2 | async-start | bytes 1179648 | tf_op jit(solution)/shard_map/all_to_all | solution.py:660
  61.3 0.0 copy-done
  61.3 0.4 pack_cols.1
  61.7 7.3 %collective-permute-start.2 = (bf16[80,128]{1,0:T(8,128)(2,1)S(1)}, bf16[80,128]{1,0:T(8,128)(2,1)S(1)}, u32[]{:S(2)}, u32[]{:S(2)}) collective-permute-start(bf16[80,128]{1,0:T(8,128)(2,1)S(1)} %get-tuple-element.39), channel_id=1, source_target_pairs={{0,1},{1,2},{2,3},{3,4},{4,5},{5,6},{6,7},{8,9},{9,10},{10,11},{11... | collective-permute-start | bytes 61448 | tf_op jit(solution)/shard_map/ppermute | solution.py:571
  69.0 1.9 %collective-permute-start.3 = (bf16[80,128]{1,0:T(8,128)(2,1)S(1)}, bf16[80,128]{1,0:T(8,128)(2,1)S(1)}, u32[]{:S(2)}, u32[]{:S(2)}) collective-permute-start(bf16[80,128]{1,0:T(8,128)(2,1)S(1)} %get-tuple-element.40), channel_id=1, source_target_pairs={{1,0},{2,1},{3,2},{4,3},{5,4},{6,5},{7,6},{9,8},{10,9},{11,10},{12... | collective-permute-start | bytes 61448 | tf_op jit(solution)/shard_map/ppermute | solution.py:575
  70.9 4.9 %all-to-all-done.2 = bf16[32,24,384]{2,1,0:T(8,128)(2,1)S(1)} async-done(((bf16[32,24,384]{2,1,0:T(8,128)(2,1)}), bf16[32,24,384]{2,1,0:T(8,128)(2,1)S(1)}, u32[]{:S(2)}, u32[]{:S(2)}) %all-to-all-start.2) | async-done | bytes 589856 | tf_op jit(solution)/shard_map/all_to_all | solution.py:660
  75.8 0.0 copy-start.4
  75.8 3.2 %backward_columns.1 = bf16[1280,128]{1,0:T(8,128)(2,1)} custom-call(bf16[768,384]{1,0:T(8,128)(2,1)S(1)} %bitcast.7, f32[2,2,2,32,768]{4,3,2,1,0:T(8,128)S(1)} %get-tuple-element.25.sens_ref, bf16[448,128]{1,0:T(8,128)(2,1)S(1)} %collective-permute-done.first_ref, bf16[448,128]{1,0:T(8,128)(2,1)S(1)} %collective-permute-done.1.second_ref, ...), custom_call_target="tpu_custom_call" | custom-call | tf_op jit(solution)/shard_map/backward_columns/pallas_call | solution.py:29
  79.0 0.0 copy-start.1
  79.0 0.0 copy-start.2
  79.0 0.0 copy-start.3
  79.0 0.0 collective-permute-done.2.left_ref
  79.0 0.0 collective-permute-done.3.right_ref
  79.0 8.5 %all-to-all-start.3 = ((bf16[8,160,128]{2,1,0:T(8,128)(2,1)}), bf16[8,160,128]{2,1,0:T(8,128)(2,1)S(1)}, u32[]{:S(2)}, u32[]{:S(2)}) async-start(bf16[8,160,128]{2,1,0:T(8,128)(2,1)} %bitcast.13), calls=%async_computation.3 | async-start | bytes 655360 | tf_op jit(solution)/shard_map/all_to_all | solution.py:682
  87.6 0.0 copy-done.4
  87.6 0.5 copy.12.kernels_ref
  88.1 0.0 copy-done.1
  88.1 0.0 copy-done.2
  88.1 0.0 copy-done.3
  88.1 0.4 coupling_weights.1
  88.5 0.6 spread_state.1.state_ref
  89.1 8.4 %all-to-all-done.3 = bf16[8,160,128]{2,1,0:T(8,128)(2,1)S(1)} async-done(((bf16[8,160,128]{2,1,0:T(8,128)(2,1)}), bf16[8,160,128]{2,1,0:T(8,128)(2,1)S(1)}, u32[]{:S(2)}, u32[]{:S(2)}) %all-to-all-start.3) | async-done | bytes 327712 | tf_op jit(solution)/shard_map/all_to_all | solution.py:682
  97.6 3.8 %couple.1 = (bf16[32,2,32,96]{3,2,1,0:T(8,128)(2,1)}, f32[2,2,32,96]{3,2,1,0:T(8,128)}) custom-call(bf16[1280,128]{1,0:T(8,128)(2,1)S(1)} %bitcast.9, bf16[2560,128]{1,0:T(8,128)(2,1)S(1)} %spread_state.1.state_ref, bf16[4,96,96]{2,1,0:T(8,128)(2,1)S(1)} %get-tuple-element.44.weight_ref, bf16[4,32,32]{2,1,0:T(8,128)(2,1)S(1)} %get-tuple-element.45.mixer_ref, ...), custom_call_target="tpu_custom_call" | custom-call | tf_op jit(solution)/shard_map/couple/pallas_call | solution.py:29
  (1 shorter events, 0.0 us)
Async XLA Ops:
  2.2 16.1 %all-to-all-start = ((bf16[8,2,2,32,128]{4,3,2,1,0:T(8,128)(2,1)}), bf16[8,2,2,32,128]{4,3,2,1,0:T(8,128)(2,1)S(1)}, u32[]{:S(2)}, u32[]{:S(2)}) async-start(bf16[8,2,2,32,128]{4,3,2,1,0:T(8,128)(2,1)} %broadcast_in_dim.2), calls=%async_computation | async-start | bytes 524288 | tf_op jit(solution)/shard_map/all_to_all | solution.py:599
  20.0 27.9 %all-to-all-start.1 = ((bf16[32,24,256]{2,1,0:T(8,128)(2,1)}), bf16[32,24,256]{2,1,0:T(8,128)(2,1)S(1)}, u32[]{:S(2)}, u32[]{:S(2)}) async-start(bf16[32,24,256]{2,1,0:T(8,128)(2,1)} %bitcast.12), calls=%async_computation.1 | async-start | bytes 786432 | tf_op jit(solution)/shard_map/all_to_all | solution.py:642
  31.1 21.9 %collective-permute-start = (bf16[448,128]{1,0:T(8,128)(2,1)S(1)}, bf16[448,128]{1,0:T(8,128)(2,1)S(1)}, u32[]{:S(2)}, u32[]{:S(2)}) collective-permute-start(bf16[448,128]{1,0:T(8,128)(2,1)S(1)} %get-tuple-element.33), channel_id=1, source_target_pairs={{0,8},{16,24},{32,40},{48,56},{64,72},{80,88},{96,104},{112,120},{... | collective-permute-start | bytes 344072 | tf_op jit(solution)/shard_map/ppermute | solution.py:581
  36.4 16.7 %collective-permute-start.1 = (bf16[448,128]{1,0:T(8,128)(2,1)S(1)}, bf16[448,128]{1,0:T(8,128)(2,1)S(1)}, u32[]{:S(2)}, u32[]{:S(2)}) collective-permute-start(bf16[448,128]{1,0:T(8,128)(2,1)S(1)} %get-tuple-element.34), channel_id=1, source_target_pairs={{8,16},{24,32},{40,48},{56,64},{72,80},{88,96},{104,112},{120,128}... | collective-permute-start | bytes 344072 | tf_op jit(solution)/shard_map/ppermute | solution.py:581
  53.1 8.2 %copy-start = (bf16[32,2,32,96]{3,2,1,0:T(8,128)(2,1)S(1)}, bf16[32,2,32,96]{3,2,1,0:T(8,128)(2,1)}, u32[]{:S(2)}) copy-start(bf16[32,2,32,96]{3,2,1,0:T(8,128)(2,1)} %state_ref.3) | copy-start | bytes 1179652
  53.1 22.7 %all-to-all-start.2 = ((bf16[32,24,384]{2,1,0:T(8,128)(2,1)}), bf16[32,24,384]{2,1,0:T(8,128)(2,1)S(1)}, u32[]{:S(2)}, u32[]{:S(2)}) async-start(bf16[32,24,384]{2,1,0:T(8,128)(2,1)} %bitcast.11), calls=%async_computation.2 | async-start | bytes 1179648 | tf_op jit(solution)/shard_map/all_to_all | solution.py:660
  61.7 17.3 %collective-permute-start.2 = (bf16[80,128]{1,0:T(8,128)(2,1)S(1)}, bf16[80,128]{1,0:T(8,128)(2,1)S(1)}, u32[]{:S(2)}, u32[]{:S(2)}) collective-permute-start(bf16[80,128]{1,0:T(8,128)(2,1)S(1)} %get-tuple-element.39), channel_id=1, source_target_pairs={{0,1},{1,2},{2,3},{3,4},{4,5},{5,6},{6,7},{8,9},{9,10},{10,11},{11... | collective-permute-start | bytes 61448 | tf_op jit(solution)/shard_map/ppermute | solution.py:571
  69.0 10.0 %collective-permute-start.3 = (bf16[80,128]{1,0:T(8,128)(2,1)S(1)}, bf16[80,128]{1,0:T(8,128)(2,1)S(1)}, u32[]{:S(2)}, u32[]{:S(2)}) collective-permute-start(bf16[80,128]{1,0:T(8,128)(2,1)S(1)} %get-tuple-element.40), channel_id=1, source_target_pairs={{1,0},{2,1},{3,2},{4,3},{5,4},{6,5},{7,6},{9,8},{10,9},{11,10},{12... | collective-permute-start | bytes 61448 | tf_op jit(solution)/shard_map/ppermute | solution.py:575
  75.8 11.8 %copy-start.4 = (bf16[4,27,16,16]{1,3,2,0:T(8,128)(2,1)S(1)}, bf16[4,27,16,16]{1,3,2,0:T(8,128)(2,1)}, u32[]{:S(2)}) copy-start(bf16[4,27,16,16]{1,3,2,0:T(8,128)(2,1)} %param.15) | copy-start | bytes 165892
  79.0 9.1 %copy-start.1 = (bf16[4,16,16]{2,1,0:T(8,128)(2,1)S(1)}, bf16[4,16,16]{2,1,0:T(8,128)(2,1)}, u32[]{:S(2)}) copy-start(bf16[4,16,16]{2,1,0:T(8,128)(2,1)} %mixers_ref.1) | copy-start | bytes 6148
  79.0 9.1 %copy-start.2 = (f32[4,16]{1,0:T(4,128)S(1)}, f32[4,16]{1,0:T(4,128)}, u32[]{:S(2)}) copy-start(f32[4,16]{1,0:T(4,128)} %biases_ref.1) | copy-start | bytes 772
  79.0 9.1 %copy-start.3 = (f32[32,2]{0,1:T(2,128)S(1)}, f32[32,2]{0,1:T(2,128)}, u32[]{:S(2)}) copy-start(f32[32,2]{0,1:T(2,128)} %param.14) | copy-start | bytes 772
  79.0 18.5 %all-to-all-start.3 = ((bf16[8,160,128]{2,1,0:T(8,128)(2,1)}), bf16[8,160,128]{2,1,0:T(8,128)(2,1)S(1)}, u32[]{:S(2)}, u32[]{:S(2)}) async-start(bf16[8,160,128]{2,1,0:T(8,128)(2,1)} %bitcast.13), calls=%async_computation.3 | async-start | bytes 655360 | tf_op jit(solution)/shard_map/all_to_all | solution.py:682
